TPU v7x, 32 devices: a whole 2x2x4 slice. The times are simulated.
32 devices in a mesh: tok: 8 (over z, y), head: 4 (over x, core).
Axes of the slice: x: 2, y: 2, z: 4, core: 2. Of those that a mesh axis runs over, the one named last changes fastest.
Arguments:
- tokens: bfloat16 [37632, 1024], P(('tok', 'head')), may hold values from -6 to 6
- target_prenorm: bfloat16 [1024], P('tok'), may hold values from 0.25 to 1.75
- target_project: bfloat16 [1024, 3072], P('tok'), may hold values from -0.1875 to 0.1875
- target_outward: bfloat16 [1024, 1024], P('tok'), may hold values from -1.5 to 1.5
- target_midnorm: bfloat16 [1024], P('tok'), may hold values from 0.25 to 1.75
- target_expand: bfloat16 [1024, 4096], P('tok'), may hold values from -0.1875 to 0.1875
- target_shrink: bfloat16 [4096, 1024], P('tok'), may hold values from -0.09375 to 0.09375
- context_prenorm: bfloat16 [1024], P('tok'), may hold values from 0.25 to 1.75
- context_project: bfloat16 [1024, 3072], P('tok'), may hold values from -0.1875 to 0.1875
- context_outward: bfloat16 [1024, 1024], P('tok'), may hold values from -1.5 to 1.5
- context_midnorm: bfloat16 [1024], P('tok'), may hold values from 0.25 to 1.75
- context_expand: bfloat16 [1024, 4096], P('tok'), may hold values from -0.1875 to 0.1875
- context_shrink: bfloat16 [4096, 1024], P('tok'), may hold values from -0.09375 to 0.09375
- predict_entry: bfloat16 [1024, 384], replicated, may hold values from -0.1875 to 0.1875
- mask_token: bfloat16 [384], replicated, may hold values from -6 to 6
- predict_prenorm: bfloat16 [384], replicated, may hold values from 0.25 to 1.75
- predict_project: bfloat16 [384, 1152], replicated, may hold values from -0.3125 to 0.3125
- predict_outward: bfloat16 [384, 384], replicated, may hold values from -1.75 to 1.75
- predict_midnorm: bfloat16 [384], replicated, may hold values from 0.25 to 1.75
- predict_expand: bfloat16 [384, 1536], replicated, may hold values from -0.3125 to 0.3125
- predict_shrink: bfloat16 [1536, 384], replicated, may hold values from -0.15625 to 0.15625
- predict_endnorm: bfloat16 [384], replicated, may hold values from 0.25 to 1.75
- predict_exit: bfloat16 [384, 1024], replicated, may hold values from -0.3125 to 0.3125
- clip_order: int32 [32, 1176], P(('tok', 'head')), may hold values from 0 to 1175, as said below
- visible_count: int32 [32], replicated, may hold values from 128 to 464, as said below
Outputs:
- clip_loss: float32 [32], P(('tok', 'head'))
- tokens_grad: float32 [37632, 1024], P(('tok', 'head'))
- context_prenorm_grad: float32 [1024], P('tok')
- context_project_grad: float32 [1024, 3072], P('tok')
- context_outward_grad: float32 [1024, 1024], P('tok')
- context_midnorm_grad: float32 [1024], P('tok')
- context_expand_grad: float32 [1024, 4096], P('tok')
- context_shrink_grad: float32 [4096, 1024], P('tok')
- predict_entry_grad: float32 [1024, 384], replicated
- mask_token_grad: float32 [384], replicated
- predict_prenorm_grad: float32 [384], replicated
- predict_project_grad: float32 [384, 1152], replicated
- predict_outward_grad: float32 [384, 384], replicated
- predict_midnorm_grad: float32 [384], replicated
- predict_expand_grad: float32 [384, 1536], replicated
- predict_shrink_grad: float32 [1536, 384], replicated
- predict_endnorm_grad: float32 [384], replicated
- predict_exit_grad: float32 [384, 1024], replicated
Inputs may be any that keep to these rules, and one draw needn't show every extreme that they name: visible_count[c] is the number of visible tokens of clip c. For every h, the clips c with (c) % 4 == h hold 2368 visible tokens together, and one of them holds exactly 464. `clip_order`: each row is a permutation of the clip's positions: its first visible_count[c] entries are the visible positions in ascending order, the others the hidden positions in ascending order.
All inputs are finite; a program needn't handle non-finite values.
Results may differ from a plain program's by a relative error of at most 0.014.
Values may be sent and summed in bfloat16 or wider, within the bound.
A program may use at most 256 MiB of HBM per device.

v0:
```python
import jax
import jax.numpy as jnp
from jax import lax
from jax.sharding import PartitionSpec as P

H = 16
PD = 384
PH = 12
VMOST = 464


EPSILON = 1e-06
HUBER = 0.25


def layer_norm(values, gains):
    center = values - jnp.mean(values, axis=-1, keepdims=True)
    spread = jnp.mean(center * center, axis=-1, keepdims=True)
    return center * lax.rsqrt(spread + EPSILON) * gains


def plain_norm(values):
    center = values - jnp.mean(values, axis=-1, keepdims=True)
    spread = jnp.mean(center * center, axis=-1, keepdims=True)
    return center * lax.rsqrt(spread + EPSILON)


def smooth_error(differ):
    magnitude = jnp.abs(differ)
    return jnp.where(magnitude < HUBER, 0.5 * differ * differ / HUBER, magnitude - 0.5 * HUBER)


def positions(length, breadth):
    half_width = breadth // 2
    places = jnp.arange(length, dtype=jnp.float32)[:, None]
    freqs = jnp.exp(-jnp.log(10000.0) * jnp.arange(half_width, dtype=jnp.float32) / half_width)
    angles = places * freqs[None, :]
    return jnp.concatenate([jnp.sin(angles), jnp.cos(angles)], axis=1)


def product(former, latter):
    return jnp.dot(former, latter, preferred_element_type=jnp.float32)


def inner_rows(former, latter):
    return lax.dot_general(
        former, latter, (((0,), (0,)), ((), ())), preferred_element_type=jnp.float32
    )


def inner_cols(former, latter):
    return lax.dot_general(
        former, latter, (((1,), (1,)), ((), ())), preferred_element_type=jnp.float32
    )


def split_heads(values, head_count, groups):
    total_rows, full_width = values.shape
    length = total_rows // groups
    head_size = full_width // head_count
    shaped = values.reshape(groups, length, head_count, head_size).transpose(0, 2, 1, 3)
    return shaped.reshape(groups * head_count, length, head_size)


def merge_heads(values, head_count, groups):
    member_count, length, head_size = values.shape
    shaped = values.reshape(groups, head_count, length, head_size).transpose(0, 2, 1, 3)
    return shaped.reshape(groups * length, head_count * head_size)


def attend(queries, key_rows, value_rows, usable, factor):

    def single(member):
        query_head, key_head, value_head, usable_head = member
        scores = inner_cols(query_head, key_head) * factor
        scores = jnp.where(usable_head[None, :], scores, -1e30)
        maxima = jnp.max(scores, axis=1, keepdims=True)
        raised = jnp.exp(scores - maxima)
        totals = jnp.sum(raised, axis=1, keepdims=True)
        shares = (raised / totals).astype(jnp.bfloat16)
        result = product(shares, value_head)
        return (result, (maxima + jnp.log(totals))[:, 0])

    return lax.map(single, (queries, key_rows, value_rows, usable))


def attend_back(queries, key_rows, value_rows, usable, logsum, grad_heads, factor):

    def single(member):
        query_head, key_head, value_head, usable_head, logsum_head, grad_head = member
        scores = inner_cols(query_head, key_head) * factor
        scores = jnp.where(usable_head[None, :], scores, -1e30)
        shares = jnp.exp(scores - logsum_head[:, None])
        grad_shares = inner_cols(grad_head, value_head)
        grad_value = inner_rows(shares.astype(jnp.bfloat16), grad_head)
        center = jnp.sum(grad_shares * shares, axis=1, keepdims=True)
        grad_scores = (shares * (grad_shares - center)).astype(jnp.bfloat16)
        grad_query = product(grad_scores, key_head) * factor
        grad_key = inner_rows(grad_scores, query_head) * factor
        return (grad_query, grad_key, grad_value)

    return lax.map(single, (queries, key_rows, value_rows, usable, logsum, grad_heads))


def attention_block(mixed, head_count, groups, usable):
    column_span = mixed.shape[1] // 3
    queries = split_heads(mixed[:, :column_span], head_count, groups)
    key_rows = split_heads(mixed[:, column_span : 2 * column_span], head_count, groups)
    value_rows = split_heads(mixed[:, 2 * column_span :], head_count, groups)
    factor = queries.shape[2] ** (-0.5)
    result, logsum = attend(queries, key_rows, value_rows, usable, factor)
    return (
        merge_heads(result.astype(jnp.bfloat16), head_count, groups),
        (queries, key_rows, value_rows, logsum),
    )


def attention_block_back(saved, grad_merged, head_count, groups, usable, block_in, project):
    queries, key_rows, value_rows, logsum = saved
    factor = queries.shape[2] ** (-0.5)
    grad_heads = split_heads(grad_merged, head_count, groups)
    grad_query, grad_key, grad_value = attend_back(
        queries, key_rows, value_rows, usable, logsum, grad_heads, factor
    )
    grad_mixed = jnp.concatenate(
        [
            merge_heads(portion.astype(jnp.bfloat16), head_count, groups)
            for portion in (grad_query, grad_key, grad_value)
        ],
        axis=1,
    )
    return (inner_rows(block_in, grad_mixed), inner_cols(grad_mixed, project))


def feed_forward(mid_rows, midnorm, expand, shrink):
    mid_wide = mid_rows.astype(jnp.float32)
    normed = layer_norm(mid_wide, midnorm).astype(jnp.bfloat16)
    raised = product(normed, expand)
    active = jax.nn.gelu(raised).astype(jnp.bfloat16)
    output = (mid_wide + product(active, shrink)).astype(jnp.bfloat16)
    return (output, (mid_wide, normed, raised, active))


def feed_forward_back(grad_rows, saved, midnorm, expand, shrink):
    mid_wide, normed, raised, active = saved
    grad_shrink = inner_rows(active, grad_rows)
    grad_active = inner_cols(grad_rows, shrink)
    unused, gelu_pullback = jax.vjp(jax.nn.gelu, raised)
    grad_raised = gelu_pullback(grad_active)[0].astype(jnp.bfloat16)
    grad_expand = inner_rows(normed, grad_raised)
    grad_normed = inner_cols(grad_raised, expand)
    unused, norm_pullback = jax.vjp(layer_norm, mid_wide, midnorm)
    grad_mid, grad_midnorm = norm_pullback(grad_normed)
    grad_total = (grad_rows.astype(jnp.float32) + grad_mid).astype(jnp.bfloat16)
    return (grad_total, (grad_midnorm, grad_expand, grad_shrink))


def shards(
    tokens,
    target_prenorm,
    target_project,
    target_outward,
    target_midnorm,
    target_expand,
    target_shrink,
    context_prenorm,
    context_project,
    context_outward,
    context_midnorm,
    context_expand,
    context_shrink,
    predict_entry,
    mask_token,
    predict_prenorm,
    predict_project,
    predict_outward,
    predict_midnorm,
    predict_expand,
    predict_shrink,
    predict_endnorm,
    predict_exit,
    clip_order,
    visible_count,
):
    clips_here = clip_order.shape[0]
    clip_len = clip_order.shape[1]
    model_width = tokens.shape[1]
    head_devices = lax.axis_size("head")
    lane_index = lax.axis_index("tok")
    head_index = lax.axis_index("head")
    device_index = lane_index * head_devices + head_index
    counts_here = lax.dynamic_slice_in_dim(visible_count, device_index * clips_here, clips_here)
    gathered = (
        lax.all_gather(target_prenorm, "tok", axis=0, tiled=True),
        lax.all_gather(target_project, "tok", axis=0, tiled=True),
        lax.all_gather(target_outward, "tok", axis=0, tiled=True),
        lax.all_gather(target_midnorm, "tok", axis=0, tiled=True),
        lax.all_gather(target_expand, "tok", axis=0, tiled=True),
        lax.all_gather(target_shrink, "tok", axis=0, tiled=True),
        lax.all_gather(context_prenorm, "tok", axis=0, tiled=True),
        lax.all_gather(context_project, "tok", axis=0, tiled=True),
        lax.all_gather(context_outward, "tok", axis=0, tiled=True),
        lax.all_gather(context_midnorm, "tok", axis=0, tiled=True),
        lax.all_gather(context_expand, "tok", axis=0, tiled=True),
        lax.all_gather(context_shrink, "tok", axis=0, tiled=True),
    )
    (
        tgt_prenorm_full,
        tgt_project_full,
        tgt_outward_full,
        tgt_midnorm_full,
        tgt_expand_full,
        tgt_shrink_full,
    ) = gathered[:6]
    (
        ctx_prenorm_full,
        ctx_project_full,
        ctx_outward_full,
        ctx_midnorm_full,
        ctx_expand_full,
        ctx_shrink_full,
    ) = gathered[6:]
    tokens_wide = tokens.astype(jnp.float32)
    every_target = jnp.ones((clips_here * H, clip_len), dtype=jnp.bool_)
    target_in = layer_norm(tokens_wide, tgt_prenorm_full.astype(jnp.float32)).astype(jnp.bfloat16)
    target_mixed = product(target_in, tgt_project_full).astype(jnp.bfloat16)
    target_attn, unused_saved = attention_block(target_mixed, H, clips_here, every_target)
    target_mid = tokens_wide + product(target_attn, tgt_outward_full)
    target_normed = layer_norm(target_mid, tgt_midnorm_full.astype(jnp.float32)).astype(
        jnp.bfloat16
    )
    target_active = jax.nn.gelu(product(target_normed, tgt_expand_full)).astype(jnp.bfloat16)
    target_out = plain_norm(target_mid + product(target_active, tgt_shrink_full))
    order_rank = jnp.argsort(clip_order, axis=1)
    visible = order_rank < counts_here[:, None]
    visible_pos = clip_order[:, :VMOST]
    slot_live = jnp.arange(VMOST, dtype=jnp.int32)[None, :] < counts_here[:, None]
    token_grid = tokens.reshape(clips_here, clip_len, model_width)
    seen_rows = jnp.take_along_axis(token_grid, visible_pos[:, :, None], axis=1)
    seen_rows = seen_rows.reshape(clips_here * VMOST, model_width).astype(jnp.float32)
    key_usable = jnp.repeat(slot_live, H, axis=0)
    ctx_prenorm_wide = ctx_prenorm_full.astype(jnp.float32)
    ctx_midnorm_wide = ctx_midnorm_full.astype(jnp.float32)
    context_in = layer_norm(seen_rows, ctx_prenorm_wide).astype(jnp.bfloat16)
    context_mixed = product(context_in, ctx_project_full).astype(jnp.bfloat16)
    context_attn, context_saved = attention_block(context_mixed, H, clips_here, key_usable)
    context_mid = (seen_rows + product(context_attn, ctx_outward_full)).astype(jnp.bfloat16)
    context_out, ffn_saved = feed_forward(
        context_mid, ctx_midnorm_wide, ctx_expand_full, ctx_shrink_full
    )
    entry_rows = product(context_out, predict_entry).reshape(clips_here, VMOST, -1)
    placed = jnp.take_along_axis(entry_rows, jnp.minimum(order_rank, VMOST - 1)[:, :, None], axis=1)
    start_rows = jnp.where(
        visible[:, :, None], placed, mask_token.astype(jnp.float32)[None, None, :]
    )
    start_rows = (start_rows + positions(clip_len, PD)[None]).reshape(clips_here * clip_len, PD)
    pred_prenorm_wide = predict_prenorm.astype(jnp.float32)
    pred_midnorm_wide = predict_midnorm.astype(jnp.float32)
    pred_endnorm_wide = predict_endnorm.astype(jnp.float32)
    every_predict = jnp.ones((clips_here * PH, clip_len), dtype=jnp.bool_)
    predict_in = layer_norm(start_rows, pred_prenorm_wide).astype(jnp.bfloat16)
    predict_mixed = product(predict_in, predict_project).astype(jnp.bfloat16)
    predict_attn, predict_saved = attention_block(predict_mixed, PH, clips_here, every_predict)
    branch_rows = start_rows + product(predict_attn, predict_outward)
    predict_normed = layer_norm(branch_rows, pred_midnorm_wide).astype(jnp.bfloat16)
    predict_raised = product(predict_normed, predict_expand)
    predict_active = jax.nn.gelu(predict_raised).astype(jnp.bfloat16)
    final_rows = branch_rows + product(predict_active, predict_shrink)
    final_in = layer_norm(final_rows, pred_endnorm_wide).astype(jnp.bfloat16)
    predicted = product(final_in, predict_exit)
    differ = predicted - target_out
    hidden_rows = jnp.logical_not(visible).reshape(-1)
    row_error = jnp.mean(smooth_error(differ), axis=1)
    clip_sums = jnp.sum(
        jnp.where(hidden_rows, row_error, 0.0).reshape(clips_here, clip_len), axis=1
    )
    clip_loss = clip_sums / (clip_len - counts_here).astype(jnp.float32)
    slope = jnp.clip(differ / HUBER, -1.0, 1.0)
    grad_predicted = (jnp.where(hidden_rows[:, None], slope, 0.0) / model_width).astype(
        jnp.bfloat16
    )
    grad_exit = inner_rows(final_in, grad_predicted)
    grad_final_in = inner_cols(grad_predicted, predict_exit)
    unused, norm_pullback = jax.vjp(layer_norm, final_rows, pred_endnorm_wide)
    grad_final, grad_endnorm = norm_pullback(grad_final_in)
    grad_second = grad_final.astype(jnp.bfloat16)
    grad_pred_shrink = inner_rows(predict_active, grad_second)
    grad_pred_active = inner_cols(grad_second, predict_shrink)
    unused, gelu_pullback = jax.vjp(jax.nn.gelu, predict_raised)
    grad_pred_raised = gelu_pullback(grad_pred_active)[0].astype(jnp.bfloat16)
    grad_pred_expand = inner_rows(predict_normed, grad_pred_raised)
    grad_pred_normed = inner_cols(grad_pred_raised, predict_expand)
    unused, norm_pullback = jax.vjp(layer_norm, branch_rows, pred_midnorm_wide)
    grad_branch_norm, grad_pred_midnorm = norm_pullback(grad_pred_normed)
    grad_branch = grad_final + grad_branch_norm
    grad_first = grad_branch.astype(jnp.bfloat16)
    grad_pred_outward = inner_rows(predict_attn, grad_first)
    grad_pred_attn = inner_cols(grad_first, predict_outward).astype(jnp.bfloat16)
    grad_pred_project, grad_pred_in = attention_block_back(
        predict_saved, grad_pred_attn, PH, clips_here, every_predict, predict_in, predict_project
    )
    unused, norm_pullback = jax.vjp(layer_norm, start_rows, pred_prenorm_wide)
    grad_start_norm, grad_pred_prenorm = norm_pullback(grad_pred_in)
    grad_start = (grad_branch + grad_start_norm).reshape(clips_here, clip_len, PD)
    grad_mask = jnp.sum(jnp.where(visible[:, :, None], 0.0, grad_start), axis=(0, 1))
    grad_entry_rows = jnp.take_along_axis(grad_start, visible_pos[:, :, None], axis=1)
    grad_entry_rows = jnp.where(slot_live[:, :, None], grad_entry_rows, 0.0)
    grad_entry_rows = grad_entry_rows.reshape(clips_here * VMOST, PD).astype(jnp.bfloat16)
    grad_entry = inner_rows(context_out, grad_entry_rows)
    grad_context_out = inner_cols(grad_entry_rows, predict_entry).astype(jnp.bfloat16)
    refetched = (
        lax.all_gather(context_prenorm, "tok", axis=0, tiled=True),
        lax.all_gather(context_project, "tok", axis=0, tiled=True),
        lax.all_gather(context_outward, "tok", axis=0, tiled=True),
        lax.all_gather(context_midnorm, "tok", axis=0, tiled=True),
        lax.all_gather(context_expand, "tok", axis=0, tiled=True),
        lax.all_gather(context_shrink, "tok", axis=0, tiled=True),
    )
    back_prenorm, back_project, back_outward, back_midnorm, back_expand, back_shrink = refetched
    back_prenorm_wide = back_prenorm.astype(jnp.float32)
    back_midnorm_wide = back_midnorm.astype(jnp.float32)
    grad_mid, ffn_grads = feed_forward_back(
        grad_context_out, ffn_saved, back_midnorm_wide, back_expand, back_shrink
    )
    grad_ctx_outward = inner_rows(context_attn, grad_mid)
    grad_ctx_attn = inner_cols(grad_mid, back_outward).astype(jnp.bfloat16)
    grad_ctx_project, grad_ctx_in = attention_block_back(
        context_saved, grad_ctx_attn, H, clips_here, key_usable, context_in, back_project
    )
    unused, norm_pullback = jax.vjp(layer_norm, seen_rows, back_prenorm_wide)
    grad_seen_norm, grad_ctx_prenorm = norm_pullback(grad_ctx_in)
    grad_seen = (grad_mid.astype(jnp.float32) + grad_seen_norm).reshape(
        clips_here, VMOST, model_width
    )
    grad_grid = jnp.take_along_axis(
        grad_seen, jnp.minimum(order_rank, VMOST - 1)[:, :, None], axis=1
    )
    tokens_grad = jnp.where(visible[:, :, None], grad_grid, 0.0).reshape(
        clips_here * clip_len, model_width
    )
    lane_parts = (
        lax.psum_scatter(grad_ctx_prenorm, "tok", scatter_dimension=0, tiled=True),
        lax.psum_scatter(grad_ctx_project, "tok", scatter_dimension=0, tiled=True),
        lax.psum_scatter(grad_ctx_outward, "tok", scatter_dimension=0, tiled=True),
        lax.psum_scatter(ffn_grads[0], "tok", scatter_dimension=0, tiled=True),
        lax.psum_scatter(ffn_grads[1], "tok", scatter_dimension=0, tiled=True),
        lax.psum_scatter(ffn_grads[2], "tok", scatter_dimension=0, tiled=True),
    )
    context_sums = (
        lax.psum(lane_parts[0].astype(jnp.bfloat16), "head").astype(jnp.float32),
        lax.psum(lane_parts[1].astype(jnp.bfloat16), "head").astype(jnp.float32),
        lax.psum(lane_parts[2].astype(jnp.bfloat16), "head").astype(jnp.float32),
        lax.psum(lane_parts[3].astype(jnp.bfloat16), "head").astype(jnp.float32),
        lax.psum(lane_parts[4].astype(jnp.bfloat16), "head").astype(jnp.float32),
        lax.psum(lane_parts[5].astype(jnp.bfloat16), "head").astype(jnp.float32),
    )
    predict_sums = lax.psum(
        (
            grad_entry,
            grad_mask,
            grad_pred_prenorm,
            grad_pred_project,
            grad_pred_outward,
            grad_pred_midnorm,
            grad_pred_expand,
            grad_pred_shrink,
            grad_endnorm,
            grad_exit,
        ),
        ("tok", "head"),
    )
    return (
        clip_loss,
        tokens_grad,
        context_sums[0],
        context_sums[1],
        context_sums[2],
        context_sums[3],
        context_sums[4],
        context_sums[5],
        predict_sums[0],
        predict_sums[1],
        predict_sums[2],
        predict_sums[3],
        predict_sums[4],
        predict_sums[5],
        predict_sums[6],
        predict_sums[7],
        predict_sums[8],
        predict_sums[9],
    )


def solution(mesh):
    return jax.shard_map(
        shards,
        mesh=mesh,
        in_specs=(
            P(("tok", "head"), None),
            P("tok"),
            P("tok", None),
            P("tok", None),
            P("tok"),
            P("tok", None),
            P("tok", None),
            P("tok"),
            P("tok", None),
            P("tok", None),
            P("tok"),
            P("tok", None),
            P("tok", None),
            P(),
            P(),
            P(),
            P(),
            P(),
            P(),
            P(),
            P(),
            P(),
            P(),
            P(("tok", "head"), None),
            P(),
        ),
        out_specs=(
            P(("tok", "head")),
            P(("tok", "head"), None),
            P("tok"),
            P("tok", None),
            P("tok", None),
            P("tok"),
            P("tok", None),
            P("tok", None),
            P(),
            P(),
            P(),
            P(),
            P(),
            P(),
            P(),
            P(),
            P(),
            P(),
        ),
        check_vma=False,
    )
```

profile of v0, /device:TPU:0, one launch (start us, length us, event | category | flops | bytes accessed | tf_op | source)
XLA Modules:
  0.0 2413.1 jit_solution(4325232939798065937)
XLA Ops:
  23.9 23.0 all-gather.2
  47.0 16.5 all-gather.3
  63.5 19.1 all-gather
  82.6 16.9 all-gather.1
  116.1 11.3 convolution_convert_fusion
  143.8 89.0 %while.64 = (s32[]{:T(128)}, bf16[16,1176,64]{1,2,0:T(8,128)(2,1)}, bf16[16,1176,64]{1,2,0:T(8,128)(2,1)}, bf16[16,1176,64]{1,2,0:T(8,128)(2,1)}, bf16[16,1176,64]{1,2,0:T(8,128)(2,1)}, /*index=5*/s32[]{:T(128)}) while((s32[]{:T(128)}, bf16[16,1176,64]{1,2,0:T(8,128)(2,1)}, bf16[16,1176,64]{1,2,0:T(8,128)(2,1)}, ...), condition=%wide.region_24.25_spmd, body=%wide.region_21.24_spmd.sunk | while | flops 363720320 | bytes 17440556 | solution.py:84
  252.1 75.3 %while.62 = (s32[]{:T(128)}, bf16[16,464,64]{1,2,0:T(8,128)(2,1)}, f32[16,464]{1,0:T(8,128)}, pred[16,464]{1,0:T(8,128)(4,1)S(1)}, bf16[16,464,64]{2,1,0:T(8,128...) while((s32[]{:T(128)}, bf16[16,464,64]{1,2,0:T(8,128)(2,1)}, ...), condition=%wide.region_6.7_spmd, body=%wide.region_3.0_spmd.sunk | while | flops 56837680 | bytes 3093085 | solution.py:84
  340.7 94.6 %all-gather.25.cloned.1.call-done = bf16[1024,4096]{1,0:T(8,128)(2,1)} async-done(((bf16[128,4096]{1,0:T(8,128)(2,1)}), bf16[1024,4096]{1,0:T(8,128)(2,1)}) %all-gather.25.cloned.1.call-update) | async-done | bytes 8388624 | tf_op jit(solution)/shard_map/all_gather | solution.py:198
  435.2 124.7 %all-gather.27.cloned.1.call-done = bf16[4096,1024]{1,0:T(8,128)(2,1)} async-done(((bf16[512,1024]{1,0:T(8,128)(2,1)}), bf16[4096,1024]{1,0:T(8,128)(2,1)}) %all-gather.27.cloned.1.call-update) | async-done | bytes 8388624 | tf_op jit(solution)/shard_map/all_gather | solution.py:199
  559.9 31.7 %fusion.217 = (f32[1176]{0:T(1024)S(1)}, f32[1176,1024]{1,0:T(8,128)}) fusion(f32[1176,1024]{1,0:T(8,128)} %copy-done.19, bf16[4096,1024]{1,0:T(8,128)(2,1)} %all-gather.27.cloned.1.call-done, bf16[1024,4096]{1,0:T(8,128)(2,1)} %all-gather.25.cloned.1.call-done, f32[1024]{0:T(1024)S(1)} %bitcast.409, f32[1176]{0:T(1024)S(1)} %add_rsqrt_fusion.1, ...), kind=kOutput, calls=%fused_computation.336 | convolution fusion | flops 19780581376 | bytes 26429216 | tf_op jit(solution)/shard_map/dot_general | solution.py:42
  591.6 93.1 %all-gather.17.cloned.1.call-done = bf16[1024,4096]{1,0:T(8,128)(2,1)} async-done(((bf16[128,4096]{1,0:T(8,128)(2,1)}), bf16[1024,4096]{1,0:T(8,128)(2,1)}) %all-gather.17.cloned.1.call-update) | async-done | bytes 8388624 | tf_op jit(solution)/shard_map/all_gather | solution.py:204
  694.8 114.8 %all-gather.19.cloned.1.call-done = bf16[4096,1024]{1,0:T(8,128)(2,1)} async-done(((bf16[512,1024]{1,0:T(8,128)(2,1)}), bf16[4096,1024]{1,0:T(8,128)(2,1)}) %all-gather.19.cloned.1.call-update) | async-done | bytes 8388624 | tf_op jit(solution)/shard_map/all_gather | solution.py:205
  853.2 85.7 %while.63 = (s32[]{:T(128)}, bf16[12,1176,32]{1,2,0:T(8,128)(2,1)}, f32[12,1176]{1,0:T(8,128)}, bf16[12,1176,32]{2,1,0:T(8,128)(2,1)}, bf16[12,1176,32]{2,1,0:T(...) while((s32[]{:T(128)}, bf16[12,1176,32]{1,2,0:T(8,128)(2,1)}, ...), condition=%wide.region_14.15_spmd, body=%wide.region_11.14_spmd.sunk | while | flops 186700576 | bytes 17721312 | solution.py:84
  975.9 158.9 %while.65 = (s32[]{:T(128)}, bf16[12,1176,32]{1,2,0:T(8,128)(2,1)}, bf16[12,1176,32]{1,2,0:T(8,128)(2,1)}, bf16[12,1176,32]{1,2,0:T(8,128)(2,1)S(1)}, bf16[12,11...) while((s32[]{:T(128)}, bf16[12,1176,32]{1,2,0:T(8,128)(2,1)}, ...), condition=%wide.region_37.38_spmd, body=%wide.region_35.37_spmd.sunk | while | flops 453690208 | bytes 44167888 | solution.py:102
  1145.7 12.1 fusion.116
  1179.9 151.6 %while.66 = (s32[]{:T(128)}, bf16[16,464,64]{1,2,0:T(8,128)(2,1)}, bf16[16,464,64]{1,2,0:T(8,128)(2,1)}, bf16[16,464,64]{1,2,0:T(8,128)(2,1)}, pred[16,464]{1,0:...) while((s32[]{:T(128)}, bf16[16,464,64]{1,2,0:T(8,128)(2,1)}, ...), condition=%wide.region_44.45_spmd, body=%wide.region_42.44_spmd.sunk | while | flops 139786032 | bytes 7593005 | solution.py:102
  1331.4 10.5 fusion.168
  1343.1 14.1 fusion.205
  1382.5 165.3 %reduce-scatter.5.cloned.1.call-done = f32[128,3072]{1,0:T(8,128)} async-done(((f32[1024,3072]{1,0:T(8,128)}), f32[128,3072]{1,0:T(8,128)}) %reduce-scatter.5.cloned.1.call-update) | async-done | bytes 1572880 | tf_op jit(solution)/shard_map/reduce_scatter | solution.py:343
  1550.2 280.6 %reduce-scatter.11.cloned.1.call-done = f32[512,1024]{1,0:T(8,128)} async-done(((f32[4096,1024]{1,0:T(8,128)}), f32[512,1024]{1,0:T(8,128)}) %reduce-scatter.11.cloned.1.call-update) | async-done | bytes 2097168 | tf_op jit(solution)/shard_map/reduce_scatter | solution.py:347
  1833.5 280.2 %reduce-scatter.9.cloned.1.call-done = f32[128,4096]{1,0:T(8,128)} async-done(((f32[1024,4096]{1,0:T(8,128)}), f32[128,4096]{1,0:T(8,128)}) %reduce-scatter.9.cloned.1.call-update) | async-done | bytes 2097168 | tf_op jit(solution)/shard_map/reduce_scatter | solution.py:346
  2143.0 19.7 all-reduce.4
  2180.0 38.1 %all-reduce.2 = (f32[384]{0:T(512)}, f32[384]{0:T(512)}, f32[384]{0:T(512)}, f32[384]{0:T(512)}) all-reduce(f32[384]{0:T(512)S(1)} %get-tuple-element.410, f32[384]{0:T(512)S(1)} %get-tuple-element.310, f32[384]{0:T(512)S(1)} %copy-done.98, f32[384]{0:T(512)S(1)} %copy-done.97), channel_id=1, replica_groups=mesh['tok'=8,'head'=4] {'tok','head'}, use_global_device_ids=true, to_apply=%region_63.64 | all-reduce | flops 1536 | bytes 12288 | tf_op jit(solution)/shard_map/psum | solution.py:357
  2230.3 163.5 %all-reduce.10.cloned.1.call-done = (f32[1024,384]{1,0:T(8,128)}, f32[384,1152]{1,0:T(8,128)}, f32[384,384]{1,0:T(8,128)}, f32[384,1536]{1,0:T(8,128)}, f32[1536,384]{1,0:T(8,128)}, /*index=5*/f32[384,1024]{1,0:T(8,128)}) async-done(((f32[1024,384]{1,0:T(8,128)}, f32[384,1152]{1,0:T(8,128)}, f32[384,384]{1,0:T(8,128)}, f32[384,1536]{1,0:T(8,128)}, f32[1536,384]{1,0:T(8,128)}, ...) | async-done | bytes 10223632 | tf_op jit(solution)/shard_map/psum | solution.py:357
  (855 shorter events, 862.4 us)
Async XLA Ops:
  7.2 937.5 %copy-start = (bf16[384,1536]{1,0:T(8,128)(2,1)S(1)}, bf16[384,1536]{1,0:T(8,128)(2,1)}, u32[]{:S(2)}) copy-start(bf16[384,1536]{1,0:T(8,128)(2,1)} %param.54) | copy-start | bytes 3538948
  7.2 108.9 %all-gather.21.cloned.1.call-start = ((), (), s32[]{:S(2)}) async-start(), calls=%async_computation.8 | async-start | bytes 7077888 | tf_op jit(solution)/shard_map/all_gather | solution.py:195
  8.0 224.8 %all-gather.13.cloned.1.call-start = ((), (), s32[]{:S(2)}) async-start(), calls=%async_computation.4 | async-start | bytes 7077888 | tf_op jit(solution)/shard_map/all_gather | solution.py:201
  8.8 318.6 %all-gather.15.cloned.1.call-start = ((), (), s32[]{:S(2)}) async-start(), calls=%async_computation.5 | async-start | bytes 2359296 | tf_op jit(solution)/shard_map/all_gather | solution.py:202
  9.5 322.1 %all-gather.23.cloned.1.call-start = ((), (), s32[]{:S(2)}) async-start(), calls=%async_computation.9 | async-start | bytes 2359296 | tf_op jit(solution)/shard_map/all_gather | solution.py:196
  10.1 425.1 %all-gather.25.cloned.1.call-start = ((), (), s32[]{:S(2)}) async-start(), calls=%async_computation.10 | async-start | bytes 9437184 | tf_op jit(solution)/shard_map/all_gather | solution.py:198
  10.7 549.2 %all-gather.27.cloned.1.call-start = ((), (), s32[]{:S(2)}) async-start(), calls=%async_computation.11 | async-start | bytes 9437184 | tf_op jit(solution)/shard_map/all_gather | solution.py:199
  11.3 673.4 %all-gather.17.cloned.1.call-start = ((), (), s32[]{:S(2)}) async-start(), calls=%async_computation.6 | async-start | bytes 9437184 | tf_op jit(solution)/shard_map/all_gather | solution.py:204
  12.0 797.5 %all-gather.19.cloned.1.call-start = ((), (), s32[]{:S(2)}) async-start(), calls=%async_computation.7 | async-start | bytes 9437184 | tf_op jit(solution)/shard_map/all_gather | solution.py:205
  12.8 1367.9 %reduce-scatter.7.cloned.1.call-start = ((), (), s32[]{:S(2)}) async-start(), calls=%async_computation.13 | async-start | bytes 4718592 | tf_op jit(solution)/shard_map/reduce_scatter | solution.py:344
  14.1 236.9 %copy-start.107 = (pred[464]{0:T(512)(128)(4,1)}, pred[464]{0:T(512)(128)(4,1)S(1)}, u32[]{:S(2)}) copy-start(pred[464]{0:T(512)(128)(4,1)S(1)} %iota_compare_fusion) | copy-start | bytes 1396
  23.9 303.5 %copy-start.90 = (pred[464]{0:T(512)(128)(4,1)}, pred[464]{0:T(512)(128)(4,1)S(1)}, u32[]{:S(2)}) copy-start(pred[464]{0:T(512)(128)(4,1)S(1)} %compare_and_fusion.1) | copy-start | bytes 1396
  109.2 218.2 %copy-start.7 = (bf16[464,1024]{1,0:T(8,128)(2,1)}, bf16[464,1024]{1,0:T(8,128)(2,1)S(1)}, u32[]{:S(2)}) copy-start(bf16[464,1024]{1,0:T(8,128)(2,1)S(1)} %gather_fusion) | copy-start | bytes 2850820
  330.6 478.9 %copy-start.13 = (bf16[464,1024]{1,0:T(8,128)(2,1)}, bf16[464,1024]{1,0:T(8,128)(2,1)S(1)}, u32[]{:S(2)}) copy-start(bf16[464,1024]{1,0:T(8,128)(2,1)S(1)} %get-tuple-element.448) | copy-start | bytes 2850820
  330.6 354.1 %copy-start.75 = (f32[464]{0:T(512)}, f32[464]{0:T(512)S(1)}, u32[]{:S(2)}) copy-start(f32[464]{0:T(512)S(1)} %broadcast_multiply_fusion.7) | copy-start | bytes 5572
  331.6 353.1 %copy-start.85 = (f32[464]{0:T(512)}, f32[464]{0:T(512)S(1)}, u32[]{:S(2)}) copy-start(f32[464]{0:T(512)S(1)} %fusion.182) | copy-start | bytes 5572
  975.9 158.9 %copy-start.72 = (f32[1176]{0:T(1024)S(1)}, f32[1176]{0:T(1024)}, u32[]{:S(2)}) copy-start(f32[1176]{0:T(1024)} %copy-done.71) | copy-start | bytes 14116
  975.9 158.9 %copy-start.93 = (f32[384]{0:T(512)S(1)}, f32[384]{0:T(512)}, u32[]{:S(2)}) copy-start(f32[384]{0:T(512)} %convert_element_type.215) | copy-start | bytes 4612
  1176.5 371.3 %reduce-scatter.5.cloned.1.call-start = ((), (), s32[]{:S(2)}) async-start(), calls=%async_computation.12 | async-start | bytes 14155776 | tf_op jit(solution)/shard_map/reduce_scatter | solution.py:343
  1342.0 488.8 %reduce-scatter.11.cloned.1.call-start = ((), (), s32[]{:S(2)}) async-start(), calls=%async_computation.15 | async-start | bytes 18874368 | tf_op jit(solution)/shard_map/reduce_scatter | solution.py:347
  1357.2 756.5 %reduce-scatter.9.cloned.1.call-start = ((), (), s32[]{:S(2)}) async-start(), calls=%async_computation.14 | async-start | bytes 18874368 | tf_op jit(solution)/shard_map/reduce_scatter | solution.py:346
  1368.8 854.0 %all-reduce.12.cloned.1.call-start = ((), (), s32[]{:S(2)}) async-start(), calls=%async_computation.17 | async-start | bytes 6291456 | tf_op jit(solution)/shard_map/psum | solution.py:351
  1833.5 283.2 %copy-start.37 = (bf16[464,1024]{1,0:T(8,128)(2,1)S(1)}, bf16[464,1024]{1,0:T(8,128)(2,1)}, u32[]{:S(2)}) copy-start(bf16[464,1024]{1,0:T(8,128)(2,1)} %copy-done.36) | copy-start | bytes 2850820
  2116.4 277.3 %all-reduce.10.cloned.1.call-start = ((), (), s32[]{:S(2)}) async-start(), calls=%async_computation.16 | async-start | bytes 20447232 | tf_op jit(solution)/shard_map/psum | solution.py:357
  (109 other events, 2351.1 us)
Sparse Core Ops, SparseCore 0:
  10.2 101.6 all-gather.20
  114.0 96.8 all-gather.12
  213.1 47.3 all-gather.14
  262.5 47.6 all-gather.22
  312.1 123.1 all-gather.24
  437.2 122.6 all-gather.26
  562.0 122.6 all-gather.16
  686.8 122.6 all-gather.18
  1176.6 86.4 reduce-scatter.6
  1342.1 205.6 reduce-scatter.4
  1551.5 279.2 reduce-scatter.10
  1834.4 279.2 reduce-scatter.8
  2116.9 67.8 all-reduce.11
  2192.2 201.5 all-reduce.9
where the time goes:
time: 2430 us; the launch traced here: 2410 us
  waiting for transfers between devices  1320 us (54%)
  matrix products  647 us (27%)
  local copies, waits for them, and re-layouts  172 us (7%)
  blocking collectives  140 us (6%)
  other arithmetic  111 us (5%)
    reduce_scatter x1, waiting for transfers between devices, shards(): lax.psum_scatter(ffn_grads[2], 'tok', scatter_dimension=0, tiled=True)  281 us
    reduce_scatter x1, waiting for transfers between devices, shards(): lax.psum_scatter(ffn_grads[1], 'tok', scatter_dimension=0, tiled=True)  280 us
    dot_general x85, matrix products, product(): return jnp.dot(former, latter, preferred_element_type=jnp.float32)  256 us
    dot_general x110, matrix products, inner_cols(): lax.dot_general(former, latter, (((1,), (1,)), ((), ())), preferred_eleme...  217 us
    dot_general x66, matrix products, inner_rows(): lax.dot_general(former, latter, (((0,), (0,)), ((), ())), preferred_eleme...  175 us
    reduce_scatter x1, waiting for transfers between devices, shards(): lax.psum_scatter(grad_ctx_project, 'tok', scatter_dimension=0, tiled=True)  165 us
    psum x1, waiting for transfers between devices, shards(): lax.psum((grad_entry, grad_mask, grad_pred_prenorm, grad_pred_project, gr...  163 us
    all_gather x1, waiting for transfers between devices, shards(): lax.all_gather(target_shrink, 'tok', axis=0, tiled=True)  125 us
  transfers between devices with their start and end apart: 14, of which 8 were waited for; matrix products, arithmetic and copies ran while one was open for 22% of the time, Pallas kernels for 0%

commit v1 on v0

--- a/solution.py
+++ b/solution.py
@@ -1,6 +1,10 @@
+import functools
+
 import jax
 import jax.numpy as jnp
 from jax import lax
+from jax.experimental import pallas as pl
+from jax.experimental.pallas import tpu as pltpu
 from jax.sharding import PartitionSpec as P
 
 H = 16
@@ -54,82 +58,101 @@
     )
 
 
-def split_heads(values, head_count, groups):
-    total_rows, full_width = values.shape
-    length = total_rows // groups
-    head_size = full_width // head_count
-    shaped = values.reshape(groups, length, head_count, head_size).transpose(0, 2, 1, 3)
-    return shaped.reshape(groups * head_count, length, head_size)
-
-
-def merge_heads(values, head_count, groups):
-    member_count, length, head_size = values.shape
-    shaped = values.reshape(groups, head_count, length, head_size).transpose(0, 2, 1, 3)
-    return shaped.reshape(groups * length, head_count * head_size)
-
-
-def attend(queries, key_rows, value_rows, usable, factor):
-
-    def single(member):
-        query_head, key_head, value_head, usable_head = member
-        scores = inner_cols(query_head, key_head) * factor
-        scores = jnp.where(usable_head[None, :], scores, -1e30)
-        maxima = jnp.max(scores, axis=1, keepdims=True)
-        raised = jnp.exp(scores - maxima)
-        totals = jnp.sum(raised, axis=1, keepdims=True)
-        shares = (raised / totals).astype(jnp.bfloat16)
-        result = product(shares, value_head)
-        return (result, (maxima + jnp.log(totals))[:, 0])
-
-    return lax.map(single, (queries, key_rows, value_rows, usable))
-
-
-def attend_back(queries, key_rows, value_rows, usable, logsum, grad_heads, factor):
-
-    def single(member):
-        query_head, key_head, value_head, usable_head, logsum_head, grad_head = member
-        scores = inner_cols(query_head, key_head) * factor
-        scores = jnp.where(usable_head[None, :], scores, -1e30)
-        shares = jnp.exp(scores - logsum_head[:, None])
-        grad_shares = inner_cols(grad_head, value_head)
-        grad_value = inner_rows(shares.astype(jnp.bfloat16), grad_head)
-        center = jnp.sum(grad_shares * shares, axis=1, keepdims=True)
-        grad_scores = (shares * (grad_shares - center)).astype(jnp.bfloat16)
-        grad_query = product(grad_scores, key_head) * factor
-        grad_key = inner_rows(grad_scores, query_head) * factor
-        return (grad_query, grad_key, grad_value)
-
-    return lax.map(single, (queries, key_rows, value_rows, usable, logsum, grad_heads))
-
-
-def attention_block(mixed, head_count, groups, usable):
-    column_span = mixed.shape[1] // 3
-    queries = split_heads(mixed[:, :column_span], head_count, groups)
-    key_rows = split_heads(mixed[:, column_span : 2 * column_span], head_count, groups)
-    value_rows = split_heads(mixed[:, 2 * column_span :], head_count, groups)
-    factor = queries.shape[2] ** (-0.5)
-    result, logsum = attend(queries, key_rows, value_rows, usable, factor)
-    return (
-        merge_heads(result.astype(jnp.bfloat16), head_count, groups),
-        (queries, key_rows, value_rows, logsum),
-    )
-
-
-def attention_block_back(saved, grad_merged, head_count, groups, usable, block_in, project):
-    queries, key_rows, value_rows, logsum = saved
-    factor = queries.shape[2] ** (-0.5)
-    grad_heads = split_heads(grad_merged, head_count, groups)
-    grad_query, grad_key, grad_value = attend_back(
-        queries, key_rows, value_rows, usable, logsum, grad_heads, factor
-    )
-    grad_mixed = jnp.concatenate(
-        [
-            merge_heads(portion.astype(jnp.bfloat16), head_count, groups)
-            for portion in (grad_query, grad_key, grad_value)
-        ],
-        axis=1,
-    )
-    return (inner_rows(block_in, grad_mixed), inner_cols(grad_mixed, project))
+BF=jnp.bfloat16; F32=jnp.float32
+LOG2E=1.4426950408889634
+NT=(((1,),(1,)),((),())); NN=(((1,),(0,)),((),()))
+def dot(a,b,dims=NN): return lax.dot_general(a,b,dims,preferred_element_type=F32)
+def chunks(n,step):
+    return [(i,min(step,n-i)) for i in range(0,n,step)]
+def lane_mask(rows,h,e):
+    lane=lax.broadcasted_iota(jnp.int32,(rows,128),1)
+    return (lane>=h*e)&(lane<(h+1)*e)
+def head_rows(values,h,e):
+    return jnp.where(lane_mask(values.shape[0],h,e),values,jnp.zeros_like(values))
+
+def fwd_kernel(e,step,masked,want_lse,*refs):
+    refs=list(refs)
+    count=refs.pop(0) if masked else None
+    q_ref,k_ref,v_ref,o_ref=refs[:4]
+    lse_ref=refs[4] if want_lse else None
+    L=q_ref.shape[0]; per=128//e; c=e**-0.5*LOG2E
+    k=k_ref[...]
+    vt=v_ref[...].T
+    live=None
+    if masked:
+        live=lax.broadcasted_iota(jnp.int32,(L,1),0)<count[0]
+    for (s0,n) in chunks(L,step):
+        outs=[]; lses=[]
+        for h in range(per):
+            q=head_rows(q_ref[s0:s0+n,:],h,e)
+            st=dot(k,q,NT)
+            if masked: st=jnp.where(live,st,-1e30)
+            m=jnp.max(st,axis=0,keepdims=True)
+            p=jnp.exp2((st-m)*c)
+            l=jnp.sum(p,axis=0,keepdims=True)
+            o=dot(vt[h*e:(h+1)*e,:],p.astype(BF))
+            outs.append(o*(1.0/l))
+            if want_lse: lses.append(m*c+jnp.log2(l))
+        o_ref[s0:s0+n,:]=jnp.concatenate(outs,axis=0).T.astype(BF)
+        if want_lse: lse_ref[0,:,s0:s0+n]=jnp.concatenate(lses,axis=0)
+
+def attn_fwd(mixed,heads,count=None,step=1280,want_lse=True):
+    L,w3=mixed.shape; Dm=w3//3; e=Dm//heads; G=Dm//128; per=128//e
+    masked=count is not None
+    spec=lambda off: pl.BlockSpec((L,128),lambda g,*_:(0,off+g))
+    out_shape=[jax.ShapeDtypeStruct((L,Dm),BF)]; out_specs=[pl.BlockSpec((L,128),lambda g,*_:(0,g))]
+    if want_lse:
+        out_shape.append(jax.ShapeDtypeStruct((G,per,L),F32)); out_specs.append(pl.BlockSpec((1,per,L),lambda g,*_:(g,0,0)))
+    gs=pltpu.PrefetchScalarGridSpec(num_scalar_prefetch=1 if masked else 0,grid=(G,),in_specs=[spec(0),spec(G),spec(2*G)],out_specs=out_specs)
+    flops=4*heads*L*L*e
+    f=pl.pallas_call(functools.partial(fwd_kernel,e,step,masked,want_lse),grid_spec=gs,out_shape=out_shape,
+        compiler_params=pltpu.CompilerParams(vmem_limit_bytes=56<<20),
+        cost_estimate=pl.CostEstimate(flops=flops,bytes_accessed=L*Dm*8,transcendentals=heads*L*L),name="attn_fwd")
+    return f(*((count,) if masked else ()),mixed,mixed,mixed)
+
+def bwd_kernel(e,step,masked,*refs):
+    refs=list(refs)
+    count=refs.pop(0) if masked else None
+    q_ref,k_ref,v_ref,o_ref,do_ref,lse_ref,g_ref,dk_ref,dv_ref=refs
+    L=q_ref.shape[0]; per=128//e; c=e**-0.5*LOG2E; f=e**-0.5
+    g=pl.program_id(0); G=pl.num_programs(0)
+    k=k_ref[...]; v=v_ref[...]
+    kt=k.T
+    live=None
+    if masked:
+        live=lax.broadcasted_iota(jnp.int32,(L,1),0)<count[0]
+    dk_ref[...]=jnp.zeros_like(dk_ref); dv_ref[...]=jnp.zeros_like(dv_ref)
+    cols=lambda part: pl.ds(pl.multiple_of((part*G+g)*128,128),128)
+    for (s0,n) in chunks(L,step):
+        do_all=do_ref[s0:s0+n,:]; q_all=q_ref[s0:s0+n,:]
+        prod=(do_all.astype(F32)*o_ref[s0:s0+n,:].astype(F32)).T
+        dqs=[]
+        for h in range(per):
+            q=head_rows(q_all,h,e); do=head_rows(do_all,h,e)
+            delta=jnp.sum(prod[h*e:(h+1)*e,:],axis=0,keepdims=True)
+            st=dot(k,q,NT)
+            p=jnp.exp2(st*c-lse_ref[0,h:h+1,s0:s0+n])
+            if masked: p=jnp.where(live,p,0.0)
+            dp=dot(v,do,NT)
+            ds=(p*(dp-delta)).astype(BF)
+            dv_ref[...]+=dot(p.astype(BF),do)
+            dk_ref[...]+=dot(ds,q)
+            dqs.append(dot(kt[h*e:(h+1)*e,:],ds))
+        g_ref[s0:s0+n,cols(0)]=(jnp.concatenate(dqs,axis=0)*f).T.astype(BF)
+    g_ref[:,cols(1)]=(dk_ref[...]*f).astype(BF)
+    g_ref[:,cols(2)]=dv_ref[...].astype(BF)
+
+def attn_bwd(mixed,o,lse,do,heads,count=None,step=256):
+    L,w3=mixed.shape; Dm=w3//3; e=Dm//heads; G=Dm//128; per=128//e
+    masked=count is not None
+    spec=lambda off: pl.BlockSpec((L,128),lambda g,*_:(0,off+g))
+    gs=pltpu.PrefetchScalarGridSpec(num_scalar_prefetch=1 if masked else 0,grid=(G,),
+        in_specs=[spec(0),spec(G),spec(2*G),spec(0),spec(0),pl.BlockSpec((1,per,L),lambda g,*_:(g,0,0))],
+        out_specs=pl.BlockSpec((L,w3),lambda g,*_:(0,0)),
+        scratch_shapes=[pltpu.VMEM((L,128),F32)]*2)
+    return pl.pallas_call(functools.partial(bwd_kernel,e,step,masked),grid_spec=gs,out_shape=jax.ShapeDtypeStruct((L,w3),BF),
+        compiler_params=pltpu.CompilerParams(vmem_limit_bytes=56<<20),
+        cost_estimate=pl.CostEstimate(flops=10*heads*L*L*e,bytes_accessed=L*Dm*16,transcendentals=heads*L*L),name="attn_bwd")(*((count,) if masked else ()),mixed,mixed,mixed,o,do,lse)
 
 
 def feed_forward(mid_rows, midnorm, expand, shrink):
@@ -221,10 +244,9 @@
         ctx_shrink_full,
     ) = gathered[6:]
     tokens_wide = tokens.astype(jnp.float32)
-    every_target = jnp.ones((clips_here * H, clip_len), dtype=jnp.bool_)
     target_in = layer_norm(tokens_wide, tgt_prenorm_full.astype(jnp.float32)).astype(jnp.bfloat16)
     target_mixed = product(target_in, tgt_project_full).astype(jnp.bfloat16)
-    target_attn, unused_saved = attention_block(target_mixed, H, clips_here, every_target)
+    target_attn = attn_fwd(target_mixed, H, want_lse=False)[0]
     target_mid = tokens_wide + product(target_attn, tgt_outward_full)
     target_normed = layer_norm(target_mid, tgt_midnorm_full.astype(jnp.float32)).astype(
         jnp.bfloat16
@@ -238,12 +260,11 @@
     token_grid = tokens.reshape(clips_here, clip_len, model_width)
     seen_rows = jnp.take_along_axis(token_grid, visible_pos[:, :, None], axis=1)
     seen_rows = seen_rows.reshape(clips_here * VMOST, model_width).astype(jnp.float32)
-    key_usable = jnp.repeat(slot_live, H, axis=0)
     ctx_prenorm_wide = ctx_prenorm_full.astype(jnp.float32)
     ctx_midnorm_wide = ctx_midnorm_full.astype(jnp.float32)
     context_in = layer_norm(seen_rows, ctx_prenorm_wide).astype(jnp.bfloat16)
     context_mixed = product(context_in, ctx_project_full).astype(jnp.bfloat16)
-    context_attn, context_saved = attention_block(context_mixed, H, clips_here, key_usable)
+    context_attn, context_lse = attn_fwd(context_mixed, H, counts_here)
     context_mid = (seen_rows + product(context_attn, ctx_outward_full)).astype(jnp.bfloat16)
     context_out, ffn_saved = feed_forward(
         context_mid, ctx_midnorm_wide, ctx_expand_full, ctx_shrink_full
@@ -257,10 +278,9 @@
     pred_prenorm_wide = predict_prenorm.astype(jnp.float32)
     pred_midnorm_wide = predict_midnorm.astype(jnp.float32)
     pred_endnorm_wide = predict_endnorm.astype(jnp.float32)
-    every_predict = jnp.ones((clips_here * PH, clip_len), dtype=jnp.bool_)
     predict_in = layer_norm(start_rows, pred_prenorm_wide).astype(jnp.bfloat16)
     predict_mixed = product(predict_in, predict_project).astype(jnp.bfloat16)
-    predict_attn, predict_saved = attention_block(predict_mixed, PH, clips_here, every_predict)
+    predict_attn, predict_lse = attn_fwd(predict_mixed, PH)
     branch_rows = start_rows + product(predict_attn, predict_outward)
     predict_normed = layer_norm(branch_rows, pred_midnorm_wide).astype(jnp.bfloat16)
     predict_raised = product(predict_normed, predict_expand)
@@ -296,9 +316,9 @@
     grad_first = grad_branch.astype(jnp.bfloat16)
     grad_pred_outward = inner_rows(predict_attn, grad_first)
     grad_pred_attn = inner_cols(grad_first, predict_outward).astype(jnp.bfloat16)
-    grad_pred_project, grad_pred_in = attention_block_back(
-        predict_saved, grad_pred_attn, PH, clips_here, every_predict, predict_in, predict_project
-    )
+    grad_pred_mixed = attn_bwd(predict_mixed, predict_attn, predict_lse, grad_pred_attn, PH)
+    grad_pred_project = inner_rows(predict_in, grad_pred_mixed)
+    grad_pred_in = inner_cols(grad_pred_mixed, predict_project)
     unused, norm_pullback = jax.vjp(layer_norm, start_rows, pred_prenorm_wide)
     grad_start_norm, grad_pred_prenorm = norm_pullback(grad_pred_in)
     grad_start = (grad_branch + grad_start_norm).reshape(clips_here, clip_len, PD)
@@ -324,9 +344,11 @@
     )
     grad_ctx_outward = inner_rows(context_attn, grad_mid)
     grad_ctx_attn = inner_cols(grad_mid, back_outward).astype(jnp.bfloat16)
-    grad_ctx_project, grad_ctx_in = attention_block_back(
-        context_saved, grad_ctx_attn, H, clips_here, key_usable, context_in, back_project
-    )
+    grad_ctx_mixed = attn_bwd(
+        context_mixed, context_attn, context_lse, grad_ctx_attn, H, counts_here
+    )
+    grad_ctx_project = inner_rows(context_in, grad_ctx_mixed)
+    grad_ctx_in = inner_cols(grad_ctx_mixed, back_project)
     unused, norm_pullback = jax.vjp(layer_norm, seen_rows, back_prenorm_wide)
     grad_seen_norm, grad_ctx_prenorm = norm_pullback(grad_ctx_in)
     grad_seen = (grad_mid.astype(jnp.float32) + grad_seen_norm).reshape(

time: 2430 us -> 2140 us (0.88)
  matrix products: 647 us -> 215 us
  waiting for transfers between devices: 1320 us -> 1530 us
  local copies, waits for them, and re-layouts: 172 us -> 35.8 us
  Pallas kernels: 0 us -> 136 us
  other arithmetic: 111 us -> 61.7 us
    dot_general x110 -> x10, matrix products: 217 us -> 48.9 us  [inner_cols(): lax.dot_general(former, latter, (((1,), (1,)), ((), ())), preferred_eleme...]
    dot_general x85 -> x13, matrix products: 256 us -> 99.1 us  [product(): return jnp.dot(former, latter, preferred_element_type=jnp.float32)]
    pallas_call x0 -> x5, Pallas kernels: none -> 136 us  [the longest x3 72.4 us: attn_fwd(): return f(*((count,) if masked else ()), mixed, mixed, mixed)]
    dot_general x66 -> x10, matrix products: 175 us -> 66.7 us  [inner_rows(): lax.dot_general(former, latter, (((0,), (0,)), ((), ())), preferred_eleme...]
    all_gather x1, waiting for transfers between devices: 0.01 us -> 95.8 us  [shards(): lax.all_gather(target_project, 'tok', axis=0, tiled=True)]
    reduce_scatter x1, waiting for transfers between devices: 165 us -> 209 us  [shards(): lax.psum_scatter(grad_ctx_project, 'tok', scatter_dimension=0, tiled=True)]
    dynamic_update_slice x28 -> x0, local copies, waits for them, and re-layouts: 38.6 us -> none  [attend(): return lax.map(single, (queries, key_rows, value_rows, usable))]
    dynamic_slice x60 -> x0, local copies, waits for them, and re-layouts: 32.8 us -> none  [the longest x28 21.2 us: attend_back(): lax.map(single, (queries, key_rows, value_rows, usable, logsum, grad_heads))]
  transfers between devices with their start and end apart: 14 -> 14, of which waited for: 8 -> 12; matrix products, arithmetic and copies ran while one was open for 22% -> 10% of each run, Pallas kernels for 0% -> 3%
where the time goes in v1:
time: 2140 us
  waiting for transfers between devices  1530 us (71%)
  matrix products  215 us (10%)
  blocking collectives  140 us (7%)
  Pallas kernels  136 us (6%)
  other arithmetic  61.7 us (3%)
  local copies, waits for them, and re-layouts  35.8 us (2%)
    reduce_scatter x1, waiting for transfers between devices, shards(): lax.psum_scatter(ffn_grads[2], 'tok', scatter_dimension=0, tiled=True)  281 us
    reduce_scatter x1, waiting for transfers between devices, shards(): lax.psum_scatter(ffn_grads[1], 'tok', scatter_dimension=0, tiled=True)  280 us
    reduce_scatter x1, waiting for transfers between devices, shards(): lax.psum_scatter(grad_ctx_project, 'tok', scatter_dimension=0, tiled=True)  209 us
    psum x1, waiting for transfers between devices, shards(): lax.psum((grad_entry, grad_mask, grad_pred_prenorm, grad_pred_project, gr...  163 us
    all_gather x1, waiting for transfers between devices, shards(): lax.all_gather(target_shrink, 'tok', axis=0, tiled=True)  125 us
    all_gather x1, waiting for transfers between devices, shards(): lax.all_gather(target_expand, 'tok', axis=0, tiled=True)  117 us
    all_gather x1, waiting for transfers between devices, shards(): lax.all_gather(context_shrink, 'tok', axis=0, tiled=True)  115 us
    dot_general x13, matrix products, product(): return jnp.dot(former, latter, preferred_element_type=jnp.float32)  99.1 us
  transfers between devices with their start and end apart: 14, of which 12 were waited for; matrix products, arithmetic and copies ran while one was open for 10% of the time, Pallas kernels for 3%

profile of v1, /device:TPU:0, one launch (start us, length us, event | category | flops | bytes accessed | tf_op | source)
XLA Modules:
  0.0 2136.4 jit_solution(14589039077977845452)
XLA Ops:
  20.2 23.0 %all-gather.2 = bf16[8,1,128]{2,1,0:T(2,128)(2,1)S(1)} all-gather(bf16[1,1,128]{2,1,0:T(2,128)(2,1)S(1)} %bitcast.78), channel_id=1, replica_groups=mesh['tok'=8,'head'=4] {'tok'}, dimensions={0}, use_global_device_ids=true | all-gather | bytes 2304 | tf_op jit(solution)/shard_map/all_gather | solution.py:217
  43.3 16.7 all-gather.3
  60.0 18.8 all-gather
  78.8 17.2 all-gather.1
  135.4 26.1 %all-gather.15.cloned.1.call-done = bf16[1024,1024]{1,0:T(8,128)(2,1)} async-done(((bf16[128,1024]{1,0:T(8,128)(2,1)}), bf16[1024,1024]{1,0:T(8,128)(2,1)}) %all-gather.15.cloned.1.call-update) | async-done | bytes 2097168 | tf_op jit(solution)/shard_map/all_gather | solution.py:225
  165.1 95.8 %all-gather.21.cloned.1.call-done = bf16[1024,3072]{1,0:T(8,128)(2,1)} async-done(((bf16[128,3072]{1,0:T(8,128)(2,1)}), bf16[1024,3072]{1,0:T(8,128)(2,1)}) %all-gather.21.cloned.1.call-update) | async-done | bytes 6291472 | tf_op jit(solution)/shard_map/all_gather | solution.py:218
  260.9 13.2 convolution_convert_fusion.refs_0_.refs_1_.refs_2_
  274.2 34.6 %attn_fwd.5 = bf16[1176,1024]{1,0:T(8,128)(2,1)} custom-call(bf16[1176,3072]{1,0:T(8,128)(2,1)} %convolution_convert_fusion.refs_0_.refs_1_.refs_2_, bf16[1176,3072]{1,0:T(8,128)(2,1)} %convolution_convert_fusion.refs_0_.refs_1_.refs_2_, bf16[1176,3072]{1,0:T(8,128)(2,1)} %convolution_convert_fusion.refs_0_.refs_1_.refs_2_), custom_call_target="tpu_custom_call" | custom-call | flops 5664669696 | bytes 9633792 | tf_op jit(solution)/shard_map/attn_fwd/pallas_call | solution.py:111
  318.3 116.9 %all-gather.25.cloned.1.call-done = bf16[1024,4096]{1,0:T(8,128)(2,1)} async-done(((bf16[128,4096]{1,0:T(8,128)(2,1)}), bf16[1024,4096]{1,0:T(8,128)(2,1)}) %all-gather.25.cloned.1.call-update) | async-done | bytes 8388624 | tf_op jit(solution)/shard_map/all_gather | solution.py:221
  435.2 124.7 %all-gather.27.cloned.1.call-done = bf16[4096,1024]{1,0:T(8,128)(2,1)} async-done(((bf16[512,1024]{1,0:T(8,128)(2,1)}), bf16[4096,1024]{1,0:T(8,128)(2,1)}) %all-gather.27.cloned.1.call-update) | async-done | bytes 8388624 | tf_op jit(solution)/shard_map/all_gather | solution.py:222
  559.9 32.0 %fusion.105 = (f32[1176]{0:T(1024)S(1)}, f32[1176,1024]{1,0:T(8,128)}) fusion(f32[1176,1024]{1,0:T(8,128)} %copy-done.15, bf16[4096,1024]{1,0:T(8,128)(2,1)} %all-gather.27.cloned.1.call-done, bf16[1024,4096]{1,0:T(8,128)(2,1)} %all-gather.25.cloned.1.call-done, f32[1024]{0:T(1024)S(1)} %bitcast.76, f32[1176]{0:T(1024)S(1)} %add_rsqrt_fusion.1, ...), kind=kOutput, calls=%fused_computation.199 | convolution fusion | flops 19780581376 | bytes 26429216 | tf_op jit(solution)/shard_map/dot_general | solution.py:46
  591.8 92.9 %all-gather.17.cloned.1.call-done = bf16[1024,4096]{1,0:T(8,128)(2,1)} async-done(((bf16[128,4096]{1,0:T(8,128)(2,1)}), bf16[1024,4096]{1,0:T(8,128)(2,1)}) %all-gather.17.cloned.1.call-update) | async-done | bytes 8388624 | tf_op jit(solution)/shard_map/all_gather | solution.py:227
  694.6 114.9 %all-gather.19.cloned.1.call-done = bf16[4096,1024]{1,0:T(8,128)(2,1)} async-done(((bf16[512,1024]{1,0:T(8,128)(2,1)}), bf16[4096,1024]{1,0:T(8,128)(2,1)}) %all-gather.19.cloned.1.call-update) | async-done | bytes 8388624 | tf_op jit(solution)/shard_map/all_gather | solution.py:228
  832.7 25.5 %attn_fwd.4 = (bf16[1176,384]{1,0:T(8,128)(2,1)}, f32[3,4,1176]{2,1,0:T(4,128)}) custom-call(bf16[1176,1152]{1,0:T(8,128)(2,1)} %convolution_convert_fusion.1.refs_0_.refs_1_.refs_2_, bf16[1176,1152]{1,0:T(8,128)(2,1)} %convolution_convert_fusion.1.refs_0_.refs_1_.refs_2_, bf16[1176,1152]{1,0:T(8,128)(2,1)} %convolution_convert_fusion.1.refs_0_.refs_1_.refs_2_), custom_call_target="tpu_custom_call" | custom-call | flops 2124251136 | bytes 3612672 | tf_op jit(solution)/shard_map/attn_fwd/pallas_call | solution.py:111
  890.5 47.4 %attn_bwd.2 = bf16[1176,1152]{1,0:T(8,128)(2,1)} custom-call(bf16[1176,1152]{1,0:T(8,128)(2,1)} %convolution_convert_fusion.1.refs_0_.refs_1_.refs_2_, bf16[1176,1152]{1,0:T(8,128)(2,1)} %convolution_convert_fusion.1.refs_0_.refs_1_.refs_2_, bf16[1176,1152]{1,0:T(8,128)(2,1)} %convolution_convert_fusion.1.refs_0_.refs_1_.refs_2_, ...), custom_call_target="tpu_custom_call" | custom-call | flops 5310627840 | bytes 7225344 | tf_op jit(solution)/shard_map/attn_bwd/pallas_call | solution.py:153
  978.5 16.4 attn_bwd.3
  1003.7 14.4 fusion.99
  1042.1 18.1 reduce-scatter.7.cloned.1.call-done
  1062.0 208.8 %reduce-scatter.5.cloned.1.call-done = f32[128,3072]{1,0:T(8,128)} async-done(((f32[1024,3072]{1,0:T(8,128)}), f32[128,3072]{1,0:T(8,128)}) %reduce-scatter.5.cloned.1.call-update) | async-done | bytes 1572880 | tf_op jit(solution)/shard_map/reduce_scatter | solution.py:365
  1273.2 280.7 %reduce-scatter.11.cloned.1.call-done = f32[512,1024]{1,0:T(8,128)} async-done(((f32[4096,1024]{1,0:T(8,128)}), f32[512,1024]{1,0:T(8,128)}) %reduce-scatter.11.cloned.1.call-update) | async-done | bytes 2097168 | tf_op jit(solution)/shard_map/reduce_scatter | solution.py:369
  1556.6 280.3 %reduce-scatter.9.cloned.1.call-done = f32[128,4096]{1,0:T(8,128)} async-done(((f32[1024,4096]{1,0:T(8,128)}), f32[128,4096]{1,0:T(8,128)}) %reduce-scatter.9.cloned.1.call-update) | async-done | bytes 2097168 | tf_op jit(solution)/shard_map/reduce_scatter | solution.py:368
  1867.1 19.2 all-reduce.4
  1903.8 38.2 %all-reduce.2 = (f32[384]{0:T(512)}, f32[384]{0:T(512)}, f32[384]{0:T(512)}, f32[384]{0:T(512)}) all-reduce(f32[384]{0:T(512)S(1)} %get-tuple-element.58, f32[384]{0:T(512)S(1)} %get-tuple-element.32, f32[384]{0:T(512)S(1)} %get-tuple-element.30, f32[384]{0:T(512)S(1)} %copy-done.57), channel_id=1, replica_groups=mesh['tok'=8,'head'=4] {'tok','head'}, use_global_device_ids=true, to_apply=%region_45.46 | all-reduce | flops 1536 | bytes 12288 | tf_op jit(solution)/shard_map/psum | solution.py:379
  1954.1 163.0 %all-reduce.10.cloned.1.call-done = (f32[1024,384]{1,0:T(8,128)}, f32[384,1152]{1,0:T(8,128)}, f32[384,384]{1,0:T(8,128)}, f32[384,1536]{1,0:T(8,128)}, f32[1536,384]{1,0:T(8,128)}, /*index=5*/f32[384,1024]{1,0:T(8,128)}) async-done(((f32[1024,384]{1,0:T(8,128)}, f32[384,1152]{1,0:T(8,128)}, f32[384,384]{1,0:T(8,128)}, f32[384,1536]{1,0:T(8,128)}, f32[1536,384]{1,0:T(8,128)}, ...) | async-done | bytes 10223632 | tf_op jit(solution)/shard_map/psum | solution.py:379
  (313 shorter events, 279.2 us)
Async XLA Ops:
  7.2 856.7 %copy-start = (bf16[384,1536]{1,0:T(8,128)(2,1)S(1)}, bf16[384,1536]{1,0:T(8,128)(2,1)}, u32[]{:S(2)}) copy-start(bf16[384,1536]{1,0:T(8,128)(2,1)} %param.44) | copy-start | bytes 3538948
  7.2 108.1 %all-gather.13.cloned.1.call-start = ((), (), s32[]{:S(2)}) async-start(), calls=%async_computation.4 | async-start | bytes 7077888 | tf_op jit(solution)/shard_map/all_gather | solution.py:224
  7.9 153.5 %all-gather.15.cloned.1.call-start = ((), (), s32[]{:S(2)}) async-start(), calls=%async_computation.5 | async-start | bytes 2359296 | tf_op jit(solution)/shard_map/all_gather | solution.py:225
  8.7 252.2 %all-gather.21.cloned.1.call-start = ((), (), s32[]{:S(2)}) async-start(), calls=%async_computation.8 | async-start | bytes 7077888 | tf_op jit(solution)/shard_map/all_gather | solution.py:218
  9.4 300.8 %all-gather.23.cloned.1.call-start = ((), (), s32[]{:S(2)}) async-start(), calls=%async_computation.9 | async-start | bytes 2359296 | tf_op jit(solution)/shard_map/all_gather | solution.py:219
  10.1 425.1 %all-gather.25.cloned.1.call-start = ((), (), s32[]{:S(2)}) async-start(), calls=%async_computation.10 | async-start | bytes 9437184 | tf_op jit(solution)/shard_map/all_gather | solution.py:221
  10.7 68.1 %copy-start.65 = (bf16[128]{0:T(256)(128)(2,1)S(1)}, bf16[128]{0:T(256)(128)(2,1)}, u32[]{:S(2)}) copy-start(bf16[128]{0:T(256)(128)(2,1)} %param.35) | copy-start | bytes 772
  10.7 85.3 %copy-start.70 = (s32[32]{0:T(128)S(1)}, s32[32]{0:T(128)}, u32[]{:S(2)}) copy-start(s32[32]{0:T(128)} %param.49) | copy-start | bytes 388
  10.7 549.2 %all-gather.27.cloned.1.call-start = ((), (), s32[]{:S(2)}) async-start(), calls=%async_computation.11 | async-start | bytes 9437184 | tf_op jit(solution)/shard_map/all_gather | solution.py:222
  11.3 673.4 %all-gather.17.cloned.1.call-start = ((), (), s32[]{:S(2)}) async-start(), calls=%async_computation.6 | async-start | bytes 9437184 | tf_op jit(solution)/shard_map/all_gather | solution.py:227
  12.0 797.5 %all-gather.19.cloned.1.call-start = ((), (), s32[]{:S(2)}) async-start(), calls=%async_computation.7 | async-start | bytes 9437184 | tf_op jit(solution)/shard_map/all_gather | solution.py:228
  12.8 1047.4 %reduce-scatter.7.cloned.1.call-start = ((), (), s32[]{:S(2)}) async-start(), calls=%async_computation.13 | async-start | bytes 4718592 | tf_op jit(solution)/shard_map/reduce_scatter | solution.py:366
  18.9 79.0 %copy-start.32 = (s32[1,1176]{1,0:T(1,128)}, s32[1,1176]{1,0:T(1,128)S(1)}, u32[]{:S(2)}) copy-start(s32[1,1176]{1,0:T(1,128)S(1)} %get-tuple-element.23) | copy-start | bytes 14116
  20.1 84.6 %copy-start.51 = (s32[1024]{0:T(1024)}, s32[1024]{0:T(1024)S(1)}, u32[]{:S(2)}) copy-start(s32[1024]{0:T(1024)S(1)} %pad_clamp_fusion.1) | copy-start | bytes 12292
  20.2 141.3 %copy-start.53 = (pred[464]{0:T(512)(128)(4,1)}, pred[464]{0:T(512)(128)(4,1)S(1)}, u32[]{:S(2)}) copy-start(pred[464]{0:T(512)(128)(4,1)S(1)} %compare_and_fusion.1) | copy-start | bytes 1396
  97.9 723.6 %copy-start.34 = (s32[2048]{0:T(1024)}, s32[2048]{0:T(1024)S(1)}, u32[]{:S(2)}) copy-start(s32[2048]{0:T(1024)S(1)} %pad_clamp_fusion) | copy-start | bytes 24580
  97.9 727.8 %copy-start.44 = (pred[1176]{0:T(1024)(128)(4,1)}, pred[1176]{0:T(1024)(128)(4,1)S(1)}, u32[]{:S(2)}) copy-start(pred[1176]{0:T(1024)(128)(4,1)S(1)} %compare_and_fusion) | copy-start | bytes 3532
  164.6 644.9 %copy-start.10 = (bf16[464,1024]{1,0:T(8,128)(2,1)}, bf16[464,1024]{1,0:T(8,128)(2,1)S(1)}, u32[]{:S(2)}) copy-start(bf16[464,1024]{1,0:T(8,128)(2,1)S(1)} %get-tuple-element.77) | copy-start | bytes 2850820
  165.0 109.1 %copy-start.48 = (f32[464]{0:T(512)}, f32[464]{0:T(512)S(1)}, u32[]{:S(2)}) copy-start(f32[464]{0:T(512)S(1)} %fusion.65) | copy-start | bytes 5572
  973.6 297.2 %reduce-scatter.5.cloned.1.call-start = ((), (), s32[]{:S(2)}) async-start(), calls=%async_computation.12 | async-start | bytes 14155776 | tf_op jit(solution)/shard_map/reduce_scatter | solution.py:365
  1003.5 550.4 %reduce-scatter.11.cloned.1.call-start = ((), (), s32[]{:S(2)}) async-start(), calls=%async_computation.15 | async-start | bytes 18874368 | tf_op jit(solution)/shard_map/reduce_scatter | solution.py:369
  1018.2 818.8 %reduce-scatter.9.cloned.1.call-start = ((), (), s32[]{:S(2)}) async-start(), calls=%async_computation.14 | async-start | bytes 18874368 | tf_op jit(solution)/shard_map/reduce_scatter | solution.py:368
  1031.0 915.6 %all-reduce.12.cloned.1.call-start = ((), (), s32[]{:S(2)}) async-start(), calls=%async_computation.17 | async-start | bytes 6291456 | tf_op jit(solution)/shard_map/psum | solution.py:373
  1839.6 277.4 %all-reduce.10.cloned.1.call-start = ((), (), s32[]{:S(2)}) async-start(), calls=%async_computation.16 | async-start | bytes 20447232 | tf_op jit(solution)/shard_map/psum | solution.py:379
  (68 other events, 724.6 us)
Sparse Core Ops, SparseCore 0:
  10.2 101.6 all-gather.12
  114.0 47.4 all-gather.14
  163.6 97.2 all-gather.20
  262.9 47.2 all-gather.22
  312.2 122.9 all-gather.24
  437.2 122.6 all-gather.26
  562.0 122.6 all-gather.16
  686.8 122.6 all-gather.18
  973.7 86.4 reduce-scatter.6
  1063.6 207.0 reduce-scatter.4
  1274.5 279.3 reduce-scatter.10
  1557.5 279.3 reduce-scatter.8
  1840.1 67.7 all-reduce.11
  1915.3 201.7 all-reduce.9

commit v2 on v1

--- a/solution.py
+++ b/solution.py
@@ -153,6 +153,345 @@
     return pl.pallas_call(functools.partial(bwd_kernel,e,step,masked),grid_spec=gs,out_shape=jax.ShapeDtypeStruct((L,w3),BF),
         compiler_params=pltpu.CompilerParams(vmem_limit_bytes=56<<20),
         cost_estimate=pl.CostEstimate(flops=10*heads*L*L*e,bytes_accessed=L*Dm*16,transcendentals=heads*L*L),name="attn_bwd")(*((count,) if masked else ()),mixed,mixed,mixed,o,do,lse)
+
+
+MESH = pl.DeviceIdType.MESH
+ANY = pl.BlockSpec(memory_space=pl.ANY)
+
+def place():
+    tok=lax.axis_index("tok"); head=lax.axis_index("head")
+    return tok//2, tok%2, head//2, head%2
+
+def peer(z,y,x,c): return (z*2+y, x*2+c)
+
+def greet(barrier_peers):
+    barrier=pltpu.get_barrier_semaphore()
+    for p in barrier_peers:
+        pl.semaphore_signal(barrier,inc=1,device_id=p,device_id_type=MESH)
+    pl.semaphore_wait(barrier,len(barrier_peers))
+
+def gather_steps(shard, full, own, cut, quarter, local, send, recv):
+    z,y,x,c=place()
+    xs = x if quarter else slice(None)
+    rows, cols = cut
+    def rcopy(i,src,dst,dev):
+        return pltpu.make_async_remote_copy(src_ref=src,dst_ref=dst,send_sem=send.at[i],recv_sem=recv.at[i],device_id=dev,device_id_type=MESH)
+    mine=shard.at[xs,c,rows,cols]
+    def load(): return pltpu.make_async_copy(mine,own,local.at[0])
+    def put(): return pltpu.make_async_copy(own,full.at[z,y,xs,c,rows,cols],local.at[1])
+    def zc(k,out):
+        dst=full.at[z,y,xs,c,rows,cols] if out else full.at[(z+4-k)%4,y,xs,c,rows,cols]
+        return rcopy(k-1,mine,dst,peer((z+k)%4,y,x,c))
+    def yc(out):
+        yy=y if out else 1-y
+        return rcopy(3,full.at[:,y,xs,c,rows,cols],full.at[:,yy,xs,c,rows,cols],peer(z,1-y,x,c))
+    def xc(out):
+        xx=x if out else 1-x
+        return rcopy(4,full.at[:,:,x,c,rows,cols],full.at[:,:,xx,c,rows,cols],peer(z,y,1-x,c))
+    def cc(out):
+        cz=c if out else 1-c
+        return rcopy(5,full.at[:,:,:,c,rows,cols],full.at[:,:,:,cz,rows,cols],peer(z,y,x,1-c))
+    def s0():
+        load().start()
+        for k in (2,1,3): zc(k,True).start()
+    def s1():
+        load().wait(); put().start()
+        for k in (1,2,3): zc(k,False).wait_recv()
+        put().wait()
+        yc(True).start()
+    def s2():
+        yc(False).wait_recv()
+        if quarter: xc(True).start()
+        else: cc(True).start()
+    def s3():
+        if quarter:
+            xc(False).wait_recv(); cc(True).start()
+    def s4():
+        cc(False).wait_recv()
+        for k in (1,2,3): zc(k,True).wait_send()
+        yc(True).wait_send()
+        if quarter: xc(True).wait_send()
+        cc(True).wait_send()
+    return [s0,s1,s2,s3,s4]
+
+def gains_steps(src,out,send,recv):
+    z,y,x,c=place()
+    def cp(k,outgoing):
+        dz,dy=k//2,k%2
+        t=z*2+y
+        pz=(z+dz)%4; py=(y+dy)%2
+        sz=(z+4-dz)%4; sy=(y+2-dy)%2
+        dst=out.at[t] if outgoing else out.at[sz*2+sy]
+        return pltpu.make_async_remote_copy(src_ref=src,dst_ref=dst,send_sem=send.at[k-1],recv_sem=recv.at[k-1],device_id=peer(pz,py,x,c),device_id_type=MESH)
+    def start():
+        for k in range(1,8): cp(k,True).start()
+    def finish():
+        for k in range(1,8): cp(k,False).wait_recv()
+        for k in range(1,8): cp(k,True).wait_send()
+    return start,finish
+
+def everyone_on_tok():
+    z,y,x,c=place()
+    peers=[peer((z+k//2)%4,(y+k%2)%2,x,c) for k in range(1,8)]
+    return peers+[peer(z,y,1-x,c),peer(z,y,x,1-c)]
+
+def interleave(chunks):
+    n=len(chunks); depth=len(chunks[0])
+    order=[]
+    for t in range(n+depth-1):
+        for s in range(depth):
+            i=t-s
+            if 0<=i<n: order.append(chunks[i][s])
+    return order
+
+def ag_kernel(plan,n,*refs):
+    shards=refs[:n]; gain=refs[n]; fulls=refs[n+1:2*n+1]; gout=refs[2*n+1]
+    rest=refs[2*n+2:]
+    owns=rest[:len(plan)]; gown,local,send,recv,gsend,grecv,glocal=rest[len(plan):]
+    z,y,x,c=place()
+    greet(everyone_on_tok())
+    gs,gf=gains_steps(gain,gout,gsend,grecv)
+    gs()
+    g0=pltpu.make_async_copy(gain,gown,glocal.at[0]); g0.start()
+    steps=[]
+    for i,(w,r0,rn,c0,cn,quarter) in enumerate(plan):
+        steps.append(gather_steps(shards[w],fulls[w],owns[i],(pl.ds(r0,rn),pl.ds(c0,cn)),quarter,local.at[i],send.at[i],recv.at[i]))
+    for f in interleave(steps): f()
+    g0.wait()
+    g1=pltpu.make_async_copy(gown,gout.at[z*2+y],glocal.at[1]); g1.start(); g1.wait()
+    gf()
+
+def gather_weights(shards, gains, plan, cid):
+    n=len(shards)
+    views=[s.reshape(2,2,s.shape[0]//4,s.shape[1]) for s in shards]
+    outs=[jax.ShapeDtypeStruct((4,2,2,2,s.shape[0]//4,s.shape[1]),s.dtype) for s in shards]
+    outs.append(jax.ShapeDtypeStruct((8,)+gains.shape,gains.dtype))
+    owns=[pltpu.VMEM(((rn,cn) if q else (2,rn,cn)),jnp.bfloat16) for (w,r0,rn,c0,cn,q) in plan]
+    k=len(plan)
+    res=pl.pallas_call(functools.partial(ag_kernel,plan,n),out_shape=outs,in_specs=[ANY]*(n+1),out_specs=[ANY]*(n+1),
+        scratch_shapes=owns+[pltpu.VMEM(gains.shape,gains.dtype),pltpu.SemaphoreType.DMA((k,2)),pltpu.SemaphoreType.DMA((k,6)),pltpu.SemaphoreType.DMA((k,6)),
+            pltpu.SemaphoreType.DMA((7,)),pltpu.SemaphoreType.DMA((7,)),pltpu.SemaphoreType.DMA((2,))],
+        compiler_params=pltpu.CompilerParams(collective_id=cid,has_side_effects=True),name="gather_weights")(*views,gains)
+    return [o.reshape(8*s.shape[0],s.shape[1]) for o,s in zip(res[:n],shards)],res[n]
+
+
+def reduce_steps(grad, out, rn, rows, bufs, order, everywhere, local, send, recv):
+    z,y,x,c=place()
+    M,C,A,B,Z,T=bufs
+    def rcopy(i,src,dst,dev):
+        return pltpu.make_async_remote_copy(src_ref=src,dst_ref=dst,send_sem=send.at[i],recv_sem=recv.at[i],device_id=dev,device_id_type=MESH)
+    xfirst=order=="xy"
+    side={"x":peer(z,y,1-x,c),"y":peer(z,1-y,x,c)}
+    first,second=order
+    load=lambda: pltpu.make_async_copy(grad.at[:,:,:,c,rows],M,local.at[0])
+    cc=lambda: rcopy(0,grad.at[:,:,:,1-c,rows],C,side_c)
+    side_c=peer(z,y,x,1-c)
+    ac=lambda: rcopy(1,M.at[:,:,1-x] if xfirst else M.at[:,1-y],A,side[first])
+    bc=lambda: rcopy(2,M.at[:,1-y,x] if xfirst else M.at[:,y,1-x],B,side[second])
+    zc=lambda k: rcopy(2+k,M.at[(z+k)%4,y,x],Z.at[k-1],peer((z+k)%4,y,x,c))
+    def add(target,source):
+        target[...]=(target[...].astype(F32)+source[...].astype(F32)).astype(BF)
+    def s0():
+        cc().start(); load().start()
+    def s1():
+        load().wait(); cc().wait_recv()
+        @pl.loop(0,16)
+        def _(i):
+            at=(i//4,(i//2)%2,i%2)
+            add(M.at[at],C.at[at])
+        ac().start()
+    def s2():
+        ac().wait_recv()
+        @pl.loop(0,8)
+        def _(i):
+            if xfirst: add(M.at[i//2,i%2,x],A.at[i//2,i%2])
+            else: add(M.at[i//2,y,i%2],A.at[i//2,i%2])
+        bc().start()
+    def s3():
+        bc().wait_recv()
+        @pl.loop(0,4)
+        def _(i):
+            add(M.at[i,y,x],B.at[i])
+        for k in (2,1,3): zc(k).start()
+    if everywhere:
+        home=out.at[z,y,x,c,rows]
+        spread=[]
+        for k in (1,2,3):
+            spread.append((5+k,lambda o,k=k:(T,out.at[z,y,x,c,rows] if o else out.at[(z+4-k)%4,y,x,c,rows],peer((z+k)%4,y,x,c))))
+        sy=(9,lambda o:(out.at[:,y,x,c,rows],out.at[:,y if o else 1-y,x,c,rows],side["y"]))
+        sx=(10,lambda o:(out.at[:,:,x,c,rows],out.at[:,:,x if o else 1-x,c,rows],side["x"]))
+        if xfirst: stages=[spread,[sy],[sx]]
+        else:
+            sx=(9,lambda o:(out.at[:,y,x,c,rows],out.at[:,y,x if o else 1-x,c,rows],side["x"]))
+            sy=(10,lambda o:(out.at[:,y,:,c,rows],out.at[:,y if o else 1-y,:,c,rows],side["y"]))
+            stages=[spread,[sx],[sy]]
+        stages.append([(11,lambda o:(out.at[:,:,:,c,rows],out.at[:,:,:,c if o else 1-c,rows],side_c))])
+    else:
+        home=out.at[x,c,rows]
+        stages=[[(6,lambda o:(T,out.at[x if o else 1-x,c,rows],side["x"]))],[(7,lambda o:(out.at[:,c,rows],out.at[:,c if o else 1-c,rows],side_c))]]
+    def run(entry,o):
+        i,f=entry; src,dst,dev=f(o); return rcopy(i,src,dst,dev)
+    put=lambda: pltpu.make_async_copy(T,home,local.at[1])
+    def s4():
+        for k in (1,2,3): zc(k).wait_recv()
+        T[...]=(M[z,y,x].astype(F32)+Z[0].astype(F32)+Z[1].astype(F32)+Z[2].astype(F32)).astype(BF)
+        put().start()
+        for e in stages[0]: run(e,True).start()
+    def later(n):
+        def s():
+            if n==1: put().wait()
+            for e in stages[n-1]: run(e,False).wait_recv()
+            for e in stages[n]: run(e,True).start()
+        return s
+    def last():
+        for e in stages[-1]: run(e,False).wait_recv()
+        cc().wait_send(); ac().wait_send(); bc().wait_send()
+        for k in (1,2,3): zc(k).wait_send()
+        for st in stages:
+            for e in st: run(e,True).wait_send()
+    mids=[later(n) for n in range(1,len(stages))]
+    if not everywhere: mids=mids+[lambda:None]*2
+    return [s0,s1,s2,s3,s4]+mids+[last]
+
+def vector_steps(src,out,bufs,local,send,recv):
+    z,y,x,c=place()
+    V,R=bufs
+    dev=[peer(z,y,x,1-c),peer(z,y,1-x,c),peer(z,1-y,x,c)]+[peer((z+k)%4,y,x,c) for k in (1,2,3)]
+    def rc(i): return pltpu.make_async_remote_copy(src_ref=V.at[min(i,3)],dst_ref=R.at[i],send_sem=send.at[i],recv_sem=recv.at[i],device_id=dev[i],device_id_type=MESH)
+    load=lambda: pltpu.make_async_copy(src,V.at[0],local.at[0])
+    def s0():
+        load().start(); load().wait(); rc(0).start()
+    def mid(n):
+        def s():
+            rc(n-1).wait_recv()
+            V[n]=V[n-1]+R[n-1]
+            if n<3: rc(n).start()
+            else:
+                for i in (3,4,5): rc(i).start()
+        return s
+    def fin():
+        for i in (3,4,5): rc(i).wait_recv()
+        V[4]=V[3]+R[3]+R[4]+R[5]
+        cp=pltpu.make_async_copy(V.at[4],out,local.at[1]); cp.start(); cp.wait()
+        for i in range(6): rc(i).wait_send()
+    nothing=lambda:None
+    return [s0,mid(1),mid(2),mid(3),fin,nothing,nothing,nothing,nothing]
+
+def rs_kernel(plan,n,*refs):
+    grads=refs[:n]; vec=refs[n]; outs=refs[n+1:2*n+1]; vout=refs[2*n+1]; rest=refs[2*n+2:]
+    k=len(plan)
+    bufs=[rest[6*i:6*i+6] for i in range(k)]
+    V,R,local,send,recv,vlocal,vsend,vrecv=rest[6*k:]
+    z,y,x,c=place()
+    greet([peer((z+j)%4,y,x,c) for j in (1,2,3)]+[peer(z,1-y,x,c),peer(z,y,1-x,c),peer(z,y,x,1-c)])
+    steps=[reduce_steps(grads[w],outs[w],rn,pl.ds(r0,rn),bufs[i],order,ev,local.at[i],send.at[i],recv.at[i]) for i,(w,r0,rn,order,ev) in enumerate(plan)]
+    steps.append(vector_steps(vec,vout,(V,R),vlocal,vsend,vrecv))
+    for st in steps: st[0]()
+    for f in interleave([st[1:] for st in steps]): f()
+
+def reduce_grads(grads, vec, plan, cid):
+    n=len(grads)
+    every={w:ev for w,_,_,_,ev in plan}
+    views=[g.reshape(4,2,2,2,g.shape[0]//32,g.shape[1]) for g in grads]
+    outs=[jax.ShapeDtypeStruct(v.shape if every[w] else v.shape[2:],BF) for w,v in enumerate(views)]
+    outs.append(jax.ShapeDtypeStruct(vec.shape,F32))
+    scratch=[]
+    for (w,r0,rn,order,ev) in plan:
+        N=grads[w].shape[1]
+        scratch+=[pltpu.VMEM((4,2,2,rn,N),BF),pltpu.VMEM((4,2,2,rn,N),BF),pltpu.VMEM((4,2,rn,N),BF),pltpu.VMEM((4,rn,N),BF),pltpu.VMEM((3,rn,N),BF),pltpu.VMEM((rn,N),BF)]
+    k=len(plan)
+    S=pltpu.SemaphoreType.DMA
+    scratch+=[pltpu.VMEM((5,)+vec.shape,F32),pltpu.VMEM((6,)+vec.shape,F32),S((k,2)),S((k,12)),S((k,12)),S((2,)),S((6,)),S((6,))]
+    res=pl.pallas_call(functools.partial(rs_kernel,plan,n),out_shape=outs,in_specs=[ANY]*(n+1),out_specs=[ANY]*(n+1),scratch_shapes=scratch,
+        compiler_params=pltpu.CompilerParams(collective_id=cid,has_side_effects=True,vmem_limit_bytes=60<<20),name="reduce_grads")(*views,vec)
+    flat=[]
+    for w,r in enumerate(res[:n]):
+        rows=grads[w].shape[0]
+        flat.append(r.reshape(rows if every[w] else rows//8,grads[w].shape[1]))
+    return flat,res[n]
+
+
+def gather_plan(shards):
+    quarter = lambda w: shards[w].shape[0] // 4
+    wide = lambda w: shards[w].shape[1]
+    plan = [(1, 0, quarter(1), 0, wide(1), True)]
+    for w, sliced in ((0, True), (4, True), (2, True), (6, False), (3, True), (7, False)):
+        half = quarter(w) // 2
+        plan += [(w, part * half, half, 0, wide(w), sliced) for part in (0, 1)]
+    return plan + [(5, 0, quarter(5), 0, wide(5), True)]
+
+
+def every_weight(tuned, gains, shards):
+    if not tuned:
+        return tuple(lax.all_gather(v, "tok", axis=0, tiled=True) for v in gains + shards)
+    packed = jnp.pad(jnp.stack(gains), ((0, 12), (0, 0)))
+    full, norms = gather_weights(list(shards), packed, gather_plan(shards), 1)
+    return tuple(norms[:, i, :].reshape(-1) for i in range(4)) + tuple(full)
+
+
+def every_grad(tuned, context, predict):
+    if not tuned:
+        parts = [lax.psum_scatter(v, "tok", scatter_dimension=0, tiled=True) for v in context]
+        return (
+            tuple(lax.psum(v.astype(jnp.bfloat16), "head").astype(jnp.float32) for v in parts),
+            lax.psum(predict, ("tok", "head")),
+        )
+    entry, mask, prenorm, project, outward, midnorm, expand, shrink, endnorm, leave = predict
+    model_width, width = entry.shape
+    wide = jnp.concatenate([project, outward, expand, leave], axis=1).astype(BF)
+    blocks = wide.shape[1] // model_width
+    wide = jnp.concatenate(
+        [wide[:, i * model_width : (i + 1) * model_width] for i in range(blocks)], axis=0
+    )
+    tall = jnp.concatenate([entry, shrink], axis=0).astype(BF)
+    small = (mask, prenorm, midnorm, endnorm, context[0], context[3])
+    line = jnp.concatenate(small)
+    vector = jnp.pad(line, (0, -line.shape[0] % 1024)).reshape(-1, 128)
+    grads = [context[1], context[2], context[4], context[5]]
+    grads = [v.astype(BF) for v in grads] + [wide, tall]
+    piece = [v.shape[0] // 32 for v in grads]
+    plan = [
+        (4, 0, piece[4], "yx", True),
+        (5, 0, piece[5], "xy", True),
+        (3, 0, piece[3] // 2, "xy", False),
+        (3, piece[3] // 2, piece[3] // 2, "yx", False),
+        (2, 0, piece[2] // 2, "xy", False),
+        (2, piece[2] // 2, piece[2] // 2, "yx", False),
+        (1, 0, piece[1], "xy", False),
+        (0, 0, piece[0] // 2, "yx", False),
+        (0, piece[0] // 2, piece[0] // 2, "xy", False),
+    ]
+    sums, vector = reduce_grads(grads, vector, plan, 2)
+    sums = [v.astype(F32) for v in sums]
+    line = vector.reshape(-1)
+    lines = []
+    for v in small:
+        lines.append(line[: v.shape[0]])
+        line = line[v.shape[0] :]
+    share = model_width // lax.axis_size("tok")
+    mine = lambda v: lax.dynamic_slice_in_dim(v, lax.axis_index("tok") * share, share)
+    wide = jnp.concatenate(
+        [sums[4][i * width : (i + 1) * width] for i in range(blocks)], axis=1
+    )
+    cuts = [0]
+    for v in (project, outward, expand, leave):
+        cuts.append(cuts[-1] + v.shape[1])
+    project, outward, expand, leave = (wide[:, a:b] for a, b in zip(cuts, cuts[1:]))
+    return (
+        (mine(lines[4]), sums[0], sums[1], mine(lines[5]), sums[2], sums[3]),
+        (
+            sums[5][:model_width],
+            lines[0],
+            lines[1],
+            project,
+            outward,
+            lines[2],
+            expand,
+            sums[5][model_width:],
+            lines[3],
+            leave,
+        ),
+    )
 
 
 def feed_forward(mid_rows, midnorm, expand, shrink):
@@ -213,36 +552,34 @@
     head_index = lax.axis_index("head")
     device_index = lane_index * head_devices + head_index
     counts_here = lax.dynamic_slice_in_dim(visible_count, device_index * clips_here, clips_here)
-    gathered = (
-        lax.all_gather(target_prenorm, "tok", axis=0, tiled=True),
-        lax.all_gather(target_project, "tok", axis=0, tiled=True),
-        lax.all_gather(target_outward, "tok", axis=0, tiled=True),
-        lax.all_gather(target_midnorm, "tok", axis=0, tiled=True),
-        lax.all_gather(target_expand, "tok", axis=0, tiled=True),
-        lax.all_gather(target_shrink, "tok", axis=0, tiled=True),
-        lax.all_gather(context_prenorm, "tok", axis=0, tiled=True),
-        lax.all_gather(context_project, "tok", axis=0, tiled=True),
-        lax.all_gather(context_outward, "tok", axis=0, tiled=True),
-        lax.all_gather(context_midnorm, "tok", axis=0, tiled=True),
-        lax.all_gather(context_expand, "tok", axis=0, tiled=True),
-        lax.all_gather(context_shrink, "tok", axis=0, tiled=True),
-    )
+    tuned = lax.axis_size("tok") == 8 and head_devices == 4
     (
         tgt_prenorm_full,
+        tgt_midnorm_full,
+        ctx_prenorm_full,
+        ctx_midnorm_full,
         tgt_project_full,
         tgt_outward_full,
-        tgt_midnorm_full,
         tgt_expand_full,
         tgt_shrink_full,
-    ) = gathered[:6]
-    (
-        ctx_prenorm_full,
         ctx_project_full,
         ctx_outward_full,
-        ctx_midnorm_full,
         ctx_expand_full,
         ctx_shrink_full,
-    ) = gathered[6:]
+    ) = every_weight(
+        tuned,
+        (target_prenorm, target_midnorm, context_prenorm, context_midnorm),
+        (
+            target_project,
+            target_outward,
+            target_expand,
+            target_shrink,
+            context_project,
+            context_outward,
+            context_expand,
+            context_shrink,
+        ),
+    )
     tokens_wide = tokens.astype(jnp.float32)
     target_in = layer_norm(tokens_wide, tgt_prenorm_full.astype(jnp.float32)).astype(jnp.bfloat16)
     target_mixed = product(target_in, tgt_project_full).astype(jnp.bfloat16)
@@ -328,17 +665,9 @@
     grad_entry_rows = grad_entry_rows.reshape(clips_here * VMOST, PD).astype(jnp.bfloat16)
     grad_entry = inner_rows(context_out, grad_entry_rows)
     grad_context_out = inner_cols(grad_entry_rows, predict_entry).astype(jnp.bfloat16)
-    refetched = (
-        lax.all_gather(context_prenorm, "tok", axis=0, tiled=True),
-        lax.all_gather(context_project, "tok", axis=0, tiled=True),
-        lax.all_gather(context_outward, "tok", axis=0, tiled=True),
-        lax.all_gather(context_midnorm, "tok", axis=0, tiled=True),
-        lax.all_gather(context_expand, "tok", axis=0, tiled=True),
-        lax.all_gather(context_shrink, "tok", axis=0, tiled=True),
-    )
-    back_prenorm, back_project, back_outward, back_midnorm, back_expand, back_shrink = refetched
-    back_prenorm_wide = back_prenorm.astype(jnp.float32)
-    back_midnorm_wide = back_midnorm.astype(jnp.float32)
+    back_project, back_outward = ctx_project_full, ctx_outward_full
+    back_expand, back_shrink = ctx_expand_full, ctx_shrink_full
+    back_prenorm_wide, back_midnorm_wide = ctx_prenorm_wide, ctx_midnorm_wide
     grad_mid, ffn_grads = feed_forward_back(
         grad_context_out, ffn_saved, back_midnorm_wide, back_expand, back_shrink
     )
@@ -360,23 +689,16 @@
     tokens_grad = jnp.where(visible[:, :, None], grad_grid, 0.0).reshape(
         clips_here * clip_len, model_width
     )
-    lane_parts = (
-        lax.psum_scatter(grad_ctx_prenorm, "tok", scatter_dimension=0, tiled=True),
-        lax.psum_scatter(grad_ctx_project, "tok", scatter_dimension=0, tiled=True),
-        lax.psum_scatter(grad_ctx_outward, "tok", scatter_dimension=0, tiled=True),
-        lax.psum_scatter(ffn_grads[0], "tok", scatter_dimension=0, tiled=True),
-        lax.psum_scatter(ffn_grads[1], "tok", scatter_dimension=0, tiled=True),
-        lax.psum_scatter(ffn_grads[2], "tok", scatter_dimension=0, tiled=True),
-    )
-    context_sums = (
-        lax.psum(lane_parts[0].astype(jnp.bfloat16), "head").astype(jnp.float32),
-        lax.psum(lane_parts[1].astype(jnp.bfloat16), "head").astype(jnp.float32),
-        lax.psum(lane_parts[2].astype(jnp.bfloat16), "head").astype(jnp.float32),
-        lax.psum(lane_parts[3].astype(jnp.bfloat16), "head").astype(jnp.float32),
-        lax.psum(lane_parts[4].astype(jnp.bfloat16), "head").astype(jnp.float32),
-        lax.psum(lane_parts[5].astype(jnp.bfloat16), "head").astype(jnp.float32),
-    )
-    predict_sums = lax.psum(
+    context_sums, predict_sums = every_grad(
+        tuned,
+        (
+            grad_ctx_prenorm,
+            grad_ctx_project,
+            grad_ctx_outward,
+            ffn_grads[0],
+            ffn_grads[1],
+            ffn_grads[2],
+        ),
         (
             grad_entry,
             grad_mask,
@@ -389,7 +711,6 @@
             grad_endnorm,
             grad_exit,
         ),
-        ("tok", "head"),
     )
     return (
         clip_loss,

time: 2140 us -> 879 us (0.41)
  waiting for transfers between devices: 1530 us -> 0 us
  Pallas kernels: 136 us -> 600 us
  blocking collectives: 140 us -> 0 us
  matrix products: 215 us -> 168 us
    reduce_scatter x4 -> x0, waiting for transfers between devices: 788 us -> none  [the longest x1 281 us: shards(): lax.psum_scatter(ffn_grads[2], 'tok', scatter_dimension=0, tiled=True)]
    all_gather x8 -> x0, waiting for transfers between devices: 573 us -> none  [the longest x1 125 us: shards(): lax.all_gather(target_shrink, 'tok', axis=0, tiled=True)]
    pallas_call x0 -> x2, Pallas kernels: none -> 464 us  [the longest x1 253 us: gather_weights(): pl.pallas_call(functools.partial(ag_kernel, plan, n), out_shape=outs, in_...]
    psum x2 -> x0, waiting for transfers between devices: 163 us -> none  [the longest x1 163 us: shards(): lax.psum((grad_entry, grad_mask, grad_pred_prenorm, grad_pred_project, gr...]
    all_gather x4 -> x0, blocking collectives: 75.8 us -> none  [the longest x1 23 us: shards(): lax.all_gather(target_prenorm, 'tok', axis=0, tiled=True)]
    psum x2 -> x0, blocking collectives: 44.9 us -> none  [the longest x1 38.2 us: shards(): lax.psum((grad_entry, grad_mask, grad_pred_prenorm, grad_pred_project, gr...]
    dot_general x10, matrix products: 66.7 us -> 43.7 us  [inner_rows(): lax.dot_general(former, latter, (((0,), (0,)), ((), ())), preferred_eleme...]
  transfers between devices with their start and end apart: 14 -> 0, of which waited for: 12 -> 0; matrix products, arithmetic and copies ran while one was open for 10% -> 0% of each run, Pallas kernels for 3% -> 0%
where the time goes in v2:
time: 879 us; the launch traced here: 872 us
  Pallas kernels  600 us (68%)
  matrix products  168 us (19%)
  other arithmetic  62.2 us (7%)
  local copies, waits for them, and re-layouts  37.3 us (4%)
    pallas_call x1, Pallas kernels, gather_weights(): pl.pallas_call(functools.partial(ag_kernel, plan, n), out_shape=outs, in_...  253 us
    pallas_call x1, Pallas kernels, reduce_grads(): pl.pallas_call(functools.partial(rs_kernel, plan, n), out_shape=outs, in_...  211 us
    dot_general x13, matrix products, product(): return jnp.dot(former, latter, preferred_element_type=jnp.float32)  83.3 us
    pallas_call x3, Pallas kernels, attn_fwd(): return f(*((count,) if masked else ()), mixed, mixed, mixed)  72.3 us
    pallas_call x2, Pallas kernels, attn_bwd(): pl.pallas_call(functools.partial(bwd_kernel, e, step, masked), grid_spec=...  63.5 us
    dot_general x10, matrix products, inner_rows(): lax.dot_general(former, latter, (((0,), (0,)), ((), ())), preferred_eleme...  43.7 us
    dot_general x10, matrix products, inner_cols(): lax.dot_general(former, latter, (((1,), (1,)), ((), ())), preferred_eleme...  41.2 us

profile of v2, /device:TPU:0, one launch (start us, length us, event | category | flops | bytes accessed | tf_op | source)
XLA Modules:
  0.0 872.0 jit_solution(8149590760916727064)
XLA Ops:
  10.5 6.6 sort.17
  21.5 5.3 gather_fusion
  27.7 5.4 fusion.72
  33.2 253.0 %gather_weights.1 = (bf16[4,2,2,2,32,3072]{5,4,3,2,1,0:T(8,128)(2,1)}, bf16[4,2,2,2,32,1024]{5,4,3,2,1,0:T(8,128)(2,1)}, bf16[4,2,2,2,32,4096]{5,4,3,2,1,0:T(8,1...) custom-call(bf16[2,2,32,3072]{3,2,1,0:T(8,128)(2,1)} %bitcast.141, ...), custom_call_target="tpu_custom_call" | custom-call | tf_op jit(solution)/shard_map/gather_weights/pallas_call | solution.py:271
  287.1 13.2 %convolution_convert_fusion.refs_0_.refs_1_.refs_2_ = bf16[1176,3072]{1,0:T(8,128)(2,1)} fusion(bf16[1024,3072]{1,0:T(8,128)(2,1)} %bitcast.177, bf16[1176,1024]{1,0:T(8,128)(2,1)} %param.25, f32[1024]{0:T(1024)S(1)} %bitcast.158, f32[1176]{0:T(1024)S(1)} %add_rsqrt_fusion.2, f32[1176]{0:T(1024)S(1)} %broadcast_multiply_fusion.3), kind=kOutput, calls=%fused_computation.13 | convolution fusion | flops 7408386048 | bytes 15938752 | tf_op jit(solution)/shard_map/dot_general | solution.py:46
  300.4 34.6 %attn_fwd.5 = bf16[1176,1024]{1,0:T(8,128)(2,1)} custom-call(bf16[1176,3072]{1,0:T(8,128)(2,1)} %convolution_convert_fusion.refs_0_.refs_1_.refs_2_, bf16[1176,3072]{1,0:T(8,128)(2,1)} %convolution_convert_fusion.refs_0_.refs_1_.refs_2_, bf16[1176,3072]{1,0:T(8,128)(2,1)} %convolution_convert_fusion.refs_0_.refs_1_.refs_2_), custom_call_target="tpu_custom_call" | custom-call | flops 5664669696 | bytes 9633792 | tf_op jit(solution)/shard_map/attn_fwd/pallas_call | solution.py:111
  335.0 4.5 fusion.117
  341.7 31.6 %fusion.118 = (f32[1176]{0:T(1024)S(1)}, f32[1176,1024]{1,0:T(8,128)}) fusion(f32[1176,1024]{1,0:T(8,128)} %copy-done.9, bf16[4096,1024]{1,0:T(8,128)(2,1)} %bitcast.174, bf16[1024,4096]{1,0:T(8,128)(2,1)} %bitcast.173, f32[1024]{0:T(1024)S(1)} %bitcast.157, f32[1176]{0:T(1024)S(1)} %add_rsqrt_fusion.1, f32[1176]{0:T(1024)S(1)} %broadcast_multiply_fusion.2), kind=kOutput, calls=%fused_computation.250 | convolution fusion | flops 19780581376 | bytes 26429216 | tf_op jit(solution)/shard_map/dot_general | solution.py:46
  376.4 7.6 convolution_convert_fusion.5.refs_1_.refs_2_.refs_3_
  384.0 12.7 %attn_fwd.3 = (bf16[464,1024]{1,0:T(8,128)(2,1)}, f32[8,2,464]{2,1,0:T(2,128)}) custom-call(s32[1]{0:T(128)} %dynamic_slice.9.refs_0_, bf16[464,3072]{1,0:T(8,128)(2,1)} %convolution_convert_fusion.5.refs_1_.refs_2_.refs_3_, bf16[464,3072]{1,0:T(8,128)(2,1)} %convolution_convert_fusion.5.refs_1_.refs_2_.refs_3_, ...), custom_call_target="tpu_custom_call" | custom-call | flops 881852416 | bytes 3801088 | tf_op jit(solution)/shard_map/attn_fwd/pallas_call | solution.py:111
  404.7 4.8 fusion.70
  422.8 25.0 %attn_fwd.4 = (bf16[1176,384]{1,0:T(8,128)(2,1)}, f32[3,4,1176]{2,1,0:T(4,128)}) custom-call(bf16[1176,1152]{1,0:T(8,128)(2,1)} %convolution_convert_fusion.3.refs_0_.refs_1_.refs_2_, bf16[1176,1152]{1,0:T(8,128)(2,1)} %convolution_convert_fusion.3.refs_0_.refs_1_.refs_2_, bf16[1176,1152]{1,0:T(8,128)(2,1)} %convolution_convert_fusion.3.refs_0_.refs_1_.refs_2_), custom_call_target="tpu_custom_call" | custom-call | flops 2124251136 | bytes 3612672 | tf_op jit(solution)/shard_map/attn_fwd/pallas_call | solution.py:111
  470.9 6.5 fusion.23
  486.4 47.2 %attn_bwd.2 = bf16[1176,1152]{1,0:T(8,128)(2,1)} custom-call(bf16[1176,1152]{1,0:T(8,128)(2,1)} %convolution_convert_fusion.3.refs_0_.refs_1_.refs_2_, bf16[1176,1152]{1,0:T(8,128)(2,1)} %convolution_convert_fusion.3.refs_0_.refs_1_.refs_2_, bf16[1176,1152]{1,0:T(8,128)(2,1)} %convolution_convert_fusion.3.refs_0_.refs_1_.refs_2_, ...), custom_call_target="tpu_custom_call" | custom-call | flops 5310627840 | bytes 7225344 | tf_op jit(solution)/shard_map/attn_bwd/pallas_call | solution.py:153
  533.6 4.6 convolution_convert_fusion.8
  548.9 12.1 %fusion.16 = bf16[464,4096]{1,0:T(8,128)(2,1)S(1)} fusion(f32[464,4096]{1,0:T(8,128)} %copy-done.55, bf16[464,1024]{1,0:T(8,128)(2,1)S(1)} %convolution_convert_fusion.12, bf16[4096,1024]{1,0:T(8,128)(2,1)} %bitcast.169), kind=kOutput, calls=%fused_computation.25 | convolution fusion | flops 3930324992 | bytes 20742144 | tf_op jit(solution)/shard_map/dot_general | solution.py:56
  570.0 16.4 %attn_bwd.3 = bf16[464,3072]{1,0:T(8,128)(2,1)} custom-call(s32[1]{0:T(128)} %dynamic_slice.9.refs_0_, bf16[464,3072]{1,0:T(8,128)(2,1)} %convolution_convert_fusion.5.refs_1_.refs_2_.refs_3_, bf16[464,3072]{1,0:T(8,128)(2,1)} %convolution_convert_fusion.5.refs_1_.refs_2_.refs_3_, bf16[464,3072]{1,0:T(8,128)(2,1)} %convolution_convert_fusion.5.refs_1_.refs_2_.refs_3_, ...), custom_call_target="tpu_custom_call" | custom-call | flops 2204631040 | bytes 7602176 | tf_op jit(solution)/shard_map/attn_bwd/pallas_call | solution.py:153
  586.4 6.5 fusion.66
  593.0 11.9 %convolution_convert_fusion.1 = bf16[4096,1024]{1,0:T(8,128)(2,1)} fusion(bf16[464,1024]{1,0:T(8,128)(2,1)S(1)} %convolution_convert_fusion.12, f32[464,4096]{1,0:T(8,128)} %copy-done.55), kind=kOutput, calls=%fused_computation.27 | convolution fusion | flops 3913613312 | bytes 16941056 | tf_op jit(solution)/shard_map/dot_general | solution.py:50
  614.5 5.8 convolution_convert_fusion.4
  620.3 5.0 gather_fusion.3
  625.3 4.7 select_select_fusion
  630.0 7.3 convolution_convert_fusion.2
  637.3 211.0 %reduce_grads.1 = (bf16[2,2,32,3072]{3,2,1,0:T(8,128)(2,1)}, bf16[2,2,32,1024]{3,2,1,0:T(8,128)(2,1)}, bf16[2,2,32,4096]{3,2,1,0:T(8,128)(2,1)}, bf16[2,2,128,10...) custom-call(bf16[4,2,2,2,32,3072]{5,4,3,2,1,0:T(8,128)(2,1)} %bitcas, ...), custom_call_target="tpu_custom_call" | custom-call | tf_op jit(solution)/shard_map/reduce_grads/pallas_call | solution.py:405
  (255 shorter events, 124.1 us)
Async XLA Ops:
  0.7 449.8 %copy-start = (bf16[384,1536]{1,0:T(8,128)(2,1)S(1)}, bf16[384,1536]{1,0:T(8,128)(2,1)}, u32[]{:S(2)}) copy-start(bf16[384,1536]{1,0:T(8,128)(2,1)} %param.44) | copy-start | bytes 3538948
  8.4 13.0 %copy-start.44 = (s32[1024]{0:T(1024)}, s32[1024]{0:T(1024)S(1)}, u32[]{:S(2)}) copy-start(s32[1024]{0:T(1024)S(1)} %pad_clamp_fusion.1) | copy-start | bytes 12292
  18.5 392.6 %copy-start.28 = (s32[2048]{0:T(1024)}, s32[2048]{0:T(1024)S(1)}, u32[]{:S(2)}) copy-start(s32[2048]{0:T(1024)S(1)} %pad_clamp_fusion) | copy-start | bytes 24580
  18.6 396.7 %copy-start.37 = (pred[1176]{0:T(1024)(128)(4,1)}, pred[1176]{0:T(1024)(128)(4,1)S(1)}, u32[]{:S(2)}) copy-start(pred[1176]{0:T(1024)(128)(4,1)S(1)} %compare_and_fusion) | copy-start | bytes 3532
  26.8 369.8 %copy-start.4 = (bf16[464,1024]{1,0:T(8,128)(2,1)}, bf16[464,1024]{1,0:T(8,128)(2,1)S(1)}, u32[]{:S(2)}) copy-start(bf16[464,1024]{1,0:T(8,128)(2,1)S(1)} %gather_fusion) | copy-start | bytes 2850820
  27.2 349.1 %copy-start.32 = (f32[464]{0:T(512)}, f32[464]{0:T(512)S(1)}, u32[]{:S(2)}) copy-start(f32[464]{0:T(512)S(1)} %broadcast_multiply_fusion.8) | copy-start | bytes 5572
  27.7 258.5 %copy-start.39 = (f32[464]{0:T(512)}, f32[464]{0:T(512)S(1)}, u32[]{:S(2)}) copy-start(f32[464]{0:T(512)S(1)} %fusion.65) | copy-start | bytes 5572
  27.7 348.6 %copy-start.35 = (f32[464]{0:T(512)}, f32[464]{0:T(512)S(1)}, u32[]{:S(2)}) copy-start(f32[464]{0:T(512)S(1)} %fusion.97) | copy-start | bytes 5572
  287.1 89.2 %copy-start.30 = (f32[8,1,128]{2,1,0:T(1,128)}, f32[8,1,128]{2,1,0:T(1,128)S(1)}, u32[]{:S(2)}) copy-start(f32[8,1,128]{2,1,0:T(1,128)S(1)} %get-tuple-element.89) | copy-start | bytes 12292
  300.3 34.6 %copy-start.2 = (bf16[1176,1024]{1,0:T(8,128)(2,1)S(1)}, bf16[1176,1024]{1,0:T(8,128)(2,1)}, u32[]{:S(2)}) copy-start(bf16[1176,1024]{1,0:T(8,128)(2,1)} %param.25) | copy-start | bytes 7225348
  300.4 34.7 %copy-start.49 = (bf16[4,2,2,2,32,1024]{5,4,3,2,1,0:T(8,128)(2,1)S(1)}, bf16[4,2,2,2,32,1024]{5,4,3,2,1,0:T(8,128)(2,1)}, u32[]{:S(2)}) copy-start(bf16[4,2,2,2,32,1024]{5,4,3,2,1,0:T(8,128)(2,1)} %get-tuple-element.48) | copy-start | bytes 6291460
  384.0 16.4 %slice-start.4 = ((s8[8388608]{0:T(1024)(128)(4,1)}), s8[4194304]{0:T(1024)(128)(4,1)S(1)}, s32[]{:S(2)}) async-start(s8[8388608]{0:T(1024)(128)(4,1)} %bitcast.163), calls=%async_computation.4 | async-start | bytes 8388608
  396.7 8.0 slice-start.8
  400.0 166.3 %copy-start.6 = (bf16[464,1024]{1,0:T(8,128)(2,1)}, bf16[464,1024]{1,0:T(8,128)(2,1)S(1)}, u32[]{:S(2)}) copy-start(bf16[464,1024]{1,0:T(8,128)(2,1)S(1)} %get-tuple-element.103) | copy-start | bytes 2850820
  422.8 25.0 %copy-start.16 = (bf16[384,384]{1,0:T(8,128)(2,1)S(1)}, bf16[384,384]{1,0:T(8,128)(2,1)}, u32[]{:S(2)}) copy-start(bf16[384,384]{1,0:T(8,128)(2,1)} %param.42) | copy-start | bytes 884740
  546.7 14.3 %slice-start.6 = ((s8[8388608]{0:T(1024)(128)(4,1)}), s8[4194304]{0:T(1024)(128)(4,1)S(1)}, s32[]{:S(2)}) async-start(s8[8388608]{0:T(1024)(128)(4,1)} %bitcast.166), calls=%async_computation.6 | async-start | bytes 8388608
  548.9 12.1 %slice-start.7 = ((s8[8388608]{0:T(1024)(128)(4,1)}), s8[4194304]{0:T(1024)(128)(4,1)S(1)}, s32[]{:S(2)}) async-start(s8[8388608]{0:T(1024)(128)(4,1)} %bitcast.166), calls=%async_computation.7 | async-start | bytes 8388608
  570.0 16.4 %copy-start.5 = (bf16[464,1024]{1,0:T(8,128)(2,1)S(1)}, bf16[464,1024]{1,0:T(8,128)(2,1)}, u32[]{:S(2)}) copy-start(bf16[464,1024]{1,0:T(8,128)(2,1)} %copy-done.4) | copy-start | bytes 2850820
  570.0 16.4 %copy-start.31 = (f32[8,1,128]{2,1,0:T(1,128)S(1)}, f32[8,1,128]{2,1,0:T(1,128)}, u32[]{:S(2)}) copy-start(f32[8,1,128]{2,1,0:T(1,128)} %copy-done.30) | copy-start | bytes 12292
  570.0 16.4 %copy-start.33 = (f32[464]{0:T(512)S(1)}, f32[464]{0:T(512)}, u32[]{:S(2)}) copy-start(f32[464]{0:T(512)} %copy-done.32) | copy-start | bytes 5572
  593.0 11.9 %copy-start.40 = (f32[464]{0:T(512)S(1)}, f32[464]{0:T(512)}, u32[]{:S(2)}) copy-start(f32[464]{0:T(512)} %copy-done.39) | copy-start | bytes 5572
  593.0 12.0 %copy-start.36 = (f32[464]{0:T(512)S(1)}, f32[464]{0:T(512)}, u32[]{:S(2)}) copy-start(f32[464]{0:T(512)} %copy-done.35) | copy-start | bytes 5572
  614.5 5.8 copy-start.29
  848.3 7.6 copy-start.19
  (44 other events, 137.2 us)

commit v3 on v2

--- a/solution.py
+++ b/solution.py
@@ -34,12 +34,17 @@
     return jnp.where(magnitude < HUBER, 0.5 * differ * differ / HUBER, magnitude - 0.5 * HUBER)
 
 
-def positions(length, breadth):
+def positions(length, breadth, block=32):
     half_width = breadth // 2
-    places = jnp.arange(length, dtype=jnp.float32)[:, None]
     freqs = jnp.exp(-jnp.log(10000.0) * jnp.arange(half_width, dtype=jnp.float32) / half_width)
-    angles = places * freqs[None, :]
-    return jnp.concatenate([jnp.sin(angles), jnp.cos(angles)], axis=1)
+    coarse = jnp.arange(0, length, block, dtype=jnp.float32)[:, None, None] * freqs
+    fine = jnp.arange(block, dtype=jnp.float32)[None, :, None] * freqs
+    sines = lax.optimization_barrier((jnp.sin(coarse), jnp.cos(coarse), jnp.sin(fine), jnp.cos(fine)))
+    sin_far, cos_far, sin_near, cos_near = sines
+    table = jnp.concatenate(
+        [sin_far * cos_near + cos_far * sin_near, cos_far * cos_near - sin_far * sin_near], axis=2
+    )
+    return table.reshape(-1, breadth)[:length]
 
 
 def product(former, latter):
@@ -235,6 +240,13 @@
     peers=[peer((z+k//2)%4,(y+k%2)%2,x,c) for k in range(1,8)]
     return peers+[peer(z,y,1-x,c),peer(z,y,x,1-c)]
 
+def together(members):
+    def stage(s):
+        def run():
+            for m in members: m[s]()
+        return run
+    return [stage(s) for s in range(len(members[0]))]
+
 def interleave(chunks):
     n=len(chunks); depth=len(chunks[0])
     order=[]
@@ -256,7 +268,9 @@
     steps=[]
     for i,(w,r0,rn,c0,cn,quarter) in enumerate(plan):
         steps.append(gather_steps(shards[w],fulls[w],owns[i],(pl.ds(r0,rn),pl.ds(c0,cn)),quarter,local.at[i],send.at[i],recv.at[i]))
-    for f in interleave(steps): f()
+    groups={}
+    for st,entry in zip(steps,plan): groups.setdefault(entry[:3],[]).append(st)
+    for f in interleave([together(m) for m in groups.values()]): f()
     g0.wait()
     g1=pltpu.make_async_copy(gown,gout.at[z*2+y],glocal.at[1]); g1.start(); g1.wait()
     gf()
@@ -384,19 +398,23 @@
     V,R,local,send,recv,vlocal,vsend,vrecv=rest[6*k:]
     z,y,x,c=place()
     greet([peer((z+j)%4,y,x,c) for j in (1,2,3)]+[peer(z,1-y,x,c),peer(z,y,1-x,c),peer(z,y,x,1-c)])
-    steps=[reduce_steps(grads[w],outs[w],rn,pl.ds(r0,rn),bufs[i],order,ev,local.at[i],send.at[i],recv.at[i]) for i,(w,r0,rn,order,ev) in enumerate(plan)]
+    steps=[reduce_steps(grads[w],outs[w],rn,pl.ds(r0,rn),bufs[i],order,ev,local.at[i],send.at[i],recv.at[i]) for i,(w,r0,rn,order,ev,_) in enumerate(plan)]
     steps.append(vector_steps(vec,vout,(V,R),vlocal,vsend,vrecv))
-    for st in steps: st[0]()
-    for f in interleave([st[1:] for st in steps]): f()
+    groups={}
+    for st,entry in zip(steps,plan): groups.setdefault(entry[5],[]).append(st)
+    groups[plan[0][5]].append(steps[-1])
+    groups=[together(m) for m in groups.values()]
+    for st in groups: st[0]()
+    for f in interleave([st[1:] for st in groups]): f()
 
 def reduce_grads(grads, vec, plan, cid):
     n=len(grads)
-    every={w:ev for w,_,_,_,ev in plan}
+    every={w:ev for w,_,_,_,ev,_ in plan}
     views=[g.reshape(4,2,2,2,g.shape[0]//32,g.shape[1]) for g in grads]
     outs=[jax.ShapeDtypeStruct(v.shape if every[w] else v.shape[2:],BF) for w,v in enumerate(views)]
     outs.append(jax.ShapeDtypeStruct(vec.shape,F32))
     scratch=[]
-    for (w,r0,rn,order,ev) in plan:
+    for (w,r0,rn,order,ev,_) in plan:
         N=grads[w].shape[1]
         scratch+=[pltpu.VMEM((4,2,2,rn,N),BF),pltpu.VMEM((4,2,2,rn,N),BF),pltpu.VMEM((4,2,rn,N),BF),pltpu.VMEM((4,rn,N),BF),pltpu.VMEM((3,rn,N),BF),pltpu.VMEM((rn,N),BF)]
     k=len(plan)
@@ -412,13 +430,16 @@
 
 
 def gather_plan(shards):
-    quarter = lambda w: shards[w].shape[0] // 4
-    wide = lambda w: shards[w].shape[1]
-    plan = [(1, 0, quarter(1), 0, wide(1), True)]
-    for w, sliced in ((0, True), (4, True), (2, True), (6, False), (3, True), (7, False)):
-        half = quarter(w) // 2
-        plan += [(w, part * half, half, 0, wide(w), sliced) for part in (0, 1)]
-    return plan + [(5, 0, quarter(5), 0, wide(5), True)]
+    plan = []
+    for w in (1, 0, 2, 3, 4, 6, 7, 5):
+        rows, wide = shards[w].shape[0] // 4, shards[w].shape[1]
+        rest = (wide // 3 + 64) // 128 * 128
+        parts = 1 if wide == shards[w].shape[0] * 8 else 2
+        for part in range(parts):
+            r0, rn = part * rows // parts, rows // parts
+            plan.append((w, r0, rn, 0, wide - rest, True))
+            plan.append((w, r0, rn, wide - rest, rest, False))
+    return plan
 
 
 def every_weight(tuned, gains, shards):
@@ -450,17 +471,10 @@
     grads = [context[1], context[2], context[4], context[5]]
     grads = [v.astype(BF) for v in grads] + [wide, tall]
     piece = [v.shape[0] // 32 for v in grads]
-    plan = [
-        (4, 0, piece[4], "yx", True),
-        (5, 0, piece[5], "xy", True),
-        (3, 0, piece[3] // 2, "xy", False),
-        (3, piece[3] // 2, piece[3] // 2, "yx", False),
-        (2, 0, piece[2] // 2, "xy", False),
-        (2, piece[2] // 2, piece[2] // 2, "yx", False),
-        (1, 0, piece[1], "xy", False),
-        (0, 0, piece[0] // 2, "yx", False),
-        (0, piece[0] // 2, piece[0] // 2, "xy", False),
-    ]
+    plan = [(4, 0, piece[4], "yx", True, 4), (5, 0, piece[5], "xy", True, 4)]
+    for w in (1, 0, 2, 3):
+        half = piece[w] // 2
+        plan += [(w, 0, half, "xy", False, w), (w, half, half, "yx", False, w)]
     sums, vector = reduce_grads(grads, vector, plan, 2)
     sums = [v.astype(F32) for v in sums]
     line = vector.reshape(-1)
@@ -492,6 +506,48 @@
             leave,
         ),
     )
+
+
+def ffn_kernel(mid_ref, gain_ref, expand_ref, shrink_ref, out_ref, normed_ref, sum_ref):
+    step = pl.program_id(0)
+
+    @pl.when(step == 0)
+    def _():
+        normed_ref[...] = layer_norm(mid_ref[...], gain_ref[...]).astype(BF)
+        sum_ref[...] = mid_ref[...]
+
+    active = jax.nn.gelu(dot(normed_ref[...], expand_ref[...])).astype(BF)
+    sum_ref[...] += dot(active, shrink_ref[...])
+
+    @pl.when(step == pl.num_programs(0) - 1)
+    def _():
+        out_ref[...] = plain_norm(sum_ref[...])
+
+
+def target_ffn(mid_rows, gain, expand, shrink, block=1024):
+    length, width = mid_rows.shape
+    hidden = expand.shape[1]
+    whole = pl.BlockSpec((length, width), lambda j: (0, 0))
+    return pl.pallas_call(
+        ffn_kernel,
+        grid=(hidden // block,),
+        in_specs=[
+            whole,
+            pl.BlockSpec((1, width), lambda j: (0, 0)),
+            pl.BlockSpec((width, block), lambda j: (0, j)),
+            pl.BlockSpec((block, width), lambda j: (j, 0)),
+        ],
+        out_specs=whole,
+        out_shape=jax.ShapeDtypeStruct((length, width), F32),
+        scratch_shapes=[pltpu.VMEM((length, width), BF), pltpu.VMEM((length, width), F32)],
+        compiler_params=pltpu.CompilerParams(vmem_limit_bytes=60 << 20),
+        cost_estimate=pl.CostEstimate(
+            flops=4 * length * width * hidden,
+            bytes_accessed=8 * length * width + 4 * width * hidden,
+            transcendentals=length * hidden,
+        ),
+        name="target_ffn",
+    )(mid_rows, gain.reshape(1, -1), expand, shrink)
 
 
 def feed_forward(mid_rows, midnorm, expand, shrink):
@@ -585,18 +641,21 @@
     target_mixed = product(target_in, tgt_project_full).astype(jnp.bfloat16)
     target_attn = attn_fwd(target_mixed, H, want_lse=False)[0]
     target_mid = tokens_wide + product(target_attn, tgt_outward_full)
-    target_normed = layer_norm(target_mid, tgt_midnorm_full.astype(jnp.float32)).astype(
-        jnp.bfloat16
-    )
-    target_active = jax.nn.gelu(product(target_normed, tgt_expand_full)).astype(jnp.bfloat16)
-    target_out = plain_norm(target_mid + product(target_active, tgt_shrink_full))
-    order_rank = jnp.argsort(clip_order, axis=1)
-    visible = order_rank < counts_here[:, None]
+    target_out = target_ffn(
+        target_mid, tgt_midnorm_full.astype(jnp.float32), tgt_expand_full, tgt_shrink_full
+    )
     visible_pos = clip_order[:, :VMOST]
     slot_live = jnp.arange(VMOST, dtype=jnp.int32)[None, :] < counts_here[:, None]
+    holds = visible_pos[:, :, None] == jnp.arange(clip_len, dtype=jnp.int32)[None, None, :]
+    holds = jnp.logical_and(holds, slot_live[:, :, None])
+    visible = jnp.any(holds, axis=1)
+    slot = jnp.arange(VMOST, dtype=jnp.int32)[None, :, None]
+    order_rank = jnp.sum(jnp.where(holds, slot, 0), axis=1)
     token_grid = tokens.reshape(clips_here, clip_len, model_width)
-    seen_rows = jnp.take_along_axis(token_grid, visible_pos[:, :, None], axis=1)
-    seen_rows = seen_rows.reshape(clips_here * VMOST, model_width).astype(jnp.float32)
+    seen_rows = jnp.einsum(
+        "csl,cld->csd", holds.astype(BF), token_grid, preferred_element_type=jnp.float32
+    )
+    seen_rows = seen_rows.reshape(clips_here * VMOST, model_width)
     ctx_prenorm_wide = ctx_prenorm_full.astype(jnp.float32)
     ctx_midnorm_wide = ctx_midnorm_full.astype(jnp.float32)
     context_in = layer_norm(seen_rows, ctx_prenorm_wide).astype(jnp.bfloat16)
@@ -607,7 +666,7 @@
         context_mid, ctx_midnorm_wide, ctx_expand_full, ctx_shrink_full
     )
     entry_rows = product(context_out, predict_entry).reshape(clips_here, VMOST, -1)
-    placed = jnp.take_along_axis(entry_rows, jnp.minimum(order_rank, VMOST - 1)[:, :, None], axis=1)
+    placed = jnp.take_along_axis(entry_rows, order_rank[:, :, None], axis=1)
     start_rows = jnp.where(
         visible[:, :, None], placed, mask_token.astype(jnp.float32)[None, None, :]
     )
@@ -684,7 +743,7 @@
         clips_here, VMOST, model_width
     )
     grad_grid = jnp.take_along_axis(
-        grad_seen, jnp.minimum(order_rank, VMOST - 1)[:, :, None], axis=1
+        grad_seen, order_rank[:, :, None], axis=1
     )
     tokens_grad = jnp.where(visible[:, :, None], grad_grid, 0.0).reshape(
         clips_here * clip_len, model_width

time: 879 us -> 814 us (0.926)
  matrix products: 168 us -> 143 us
  Pallas kernels: 600 us -> 580 us
  other arithmetic: 62.2 us -> 46.1 us
    pallas_call x1, Pallas kernels: 211 us -> 177 us  [reduce_grads(): pl.pallas_call(functools.partial(rs_kernel, plan, n), out_shape=outs, in_...]
    pallas_call x0 -> x1, Pallas kernels: none -> 31.1 us  [target_ffn(): pl.pallas_call(ffn_kernel, grid=(hidden // block,), in_specs=[whole, pl.B...]
    dot_general x13 -> x12, matrix products: 83.3 us -> 55.7 us  [product(): return jnp.dot(former, latter, preferred_element_type=jnp.float32)]
    pallas_call x1, Pallas kernels: 253 us -> 236 us  [gather_weights(): pl.pallas_call(functools.partial(ag_kernel, plan, n), out_shape=outs, in_...]
where the time goes in v3:
time: 814 us; the launch traced here: 805 us
  Pallas kernels  580 us (71%)
  matrix products  143 us (18%)
  other arithmetic  46.1 us (6%)
  local copies, waits for them, and re-layouts  31 us (4%)
    pallas_call x1, Pallas kernels, gather_weights(): pl.pallas_call(functools.partial(ag_kernel, plan, n), out_shape=outs, in_...  236 us
    pallas_call x1, Pallas kernels, reduce_grads(): pl.pallas_call(functools.partial(rs_kernel, plan, n), out_shape=outs, in_...  177 us
    pallas_call x3, Pallas kernels, attn_fwd(): return f(*((count,) if masked else ()), mixed, mixed, mixed)  72.4 us
    pallas_call x2, Pallas kernels, attn_bwd(): pl.pallas_call(functools.partial(bwd_kernel, e, step, masked), grid_spec=...  63.6 us
    dot_general x12, matrix products, product(): return jnp.dot(former, latter, preferred_element_type=jnp.float32)  55.7 us
    dot_general x10, matrix products, inner_rows(): lax.dot_general(former, latter, (((0,), (0,)), ((), ())), preferred_eleme...  43.2 us
    dot_general x10, matrix products, inner_cols(): lax.dot_general(former, latter, (((1,), (1,)), ((), ())), preferred_eleme...  41 us
    pallas_call x1, Pallas kernels, target_ffn(): pl.pallas_call(ffn_kernel, grid=(hidden // block,), in_specs=[whole, pl.B...  31.1 us

profile of v3, /device:TPU:0, one launch (start us, length us, event | category | flops | bytes accessed | tf_op | source)
XLA Modules:
  0.0 804.5 jit_solution(2621517508609458097)
XLA Ops:
  19.7 235.7 %gather_weights.1 = (bf16[4,2,2,2,32,3072]{5,4,3,2,1,0:T(8,128)(2,1)}, bf16[4,2,2,2,32,1024]{5,4,3,2,1,0:T(8,128)(2,1)}, bf16[4,2,2,2,32,4096]{5,4,3,2,1,0:T(8,1...) custom-call(bf16[2,2,32,3072]{3,2,1,0:T(8,128)(2,1)} %bitcast.138, ...), custom_call_target="tpu_custom_call" | custom-call | tf_op jit(solution)/shard_map/gather_weights/pallas_call | solution.py:285
  256.8 13.7 %convolution_convert_fusion.refs_0_.refs_1_.refs_2_ = bf16[1176,3072]{1,0:T(8,128)(2,1)} fusion(bf16[1024,3072]{1,0:T(8,128)(2,1)} %bitcast.177, bf16[1176,1024]{1,0:T(8,128)(2,1)} %param.25, f32[1024]{0:T(1024)S(1)} %bitcast.160, f32[1176]{0:T(1024)S(1)} %add_rsqrt_fusion, f32[1176]{0:T(1024)S(1)} %broadcast_multiply_fusion), kind=kOutput, calls=%fused_computation.3 | convolution fusion | flops 7408386048 | bytes 15938752 | tf_op jit(solution)/shard_map/dot_general | solution.py:51
  270.5 34.5 %attn_fwd.5 = bf16[1176,1024]{1,0:T(8,128)(2,1)} custom-call(bf16[1176,3072]{1,0:T(8,128)(2,1)} %convolution_convert_fusion.refs_0_.refs_1_.refs_2_, bf16[1176,3072]{1,0:T(8,128)(2,1)} %convolution_convert_fusion.refs_0_.refs_1_.refs_2_, bf16[1176,3072]{1,0:T(8,128)(2,1)} %convolution_convert_fusion.refs_0_.refs_1_.refs_2_), custom_call_target="tpu_custom_call" | custom-call | flops 5664669696 | bytes 9633792 | tf_op jit(solution)/shard_map/attn_fwd/pallas_call | solution.py:116
  305.1 6.0 convert_add_fusion.mid_ref
  311.1 31.1 %target_ffn.1 = f32[1176,1024]{1,0:T(8,128)} custom-call(f32[1176,1024]{1,0:T(8,128)} %convert_add_fusion.mid_ref, f32[1,1024]{1,0:T(1,128)} %get-tuple-element.95.gain_ref, bf16[1024,4096]{1,0:T(8,128)(2,1)} %bitcast.173, bf16[4096,1024]{1,0:T(8,128)(2,1)} %bitcast.174), custom_call_target="tpu_custom_call" | custom-call | flops 19730006016 | bytes 26411008 | tf_op jit(solution)/shard_map/target_ffn/pallas_call | solution.py:531
  342.2 7.5 convolution_convert_fusion.5.refs_1_.refs_2_.refs_3_
  349.7 12.9 %attn_fwd.3 = (bf16[464,1024]{1,0:T(8,128)(2,1)}, f32[8,2,464]{2,1,0:T(2,128)}) custom-call(s32[1]{0:T(128)} %dynamic_slice.9.refs_0_, bf16[464,3072]{1,0:T(8,128)(2,1)} %convolution_convert_fusion.5.refs_1_.refs_2_.refs_3_, bf16[464,3072]{1,0:T(8,128)(2,1)} %convolution_convert_fusion.5.refs_1_.refs_2_.refs_3_, ...), custom_call_target="tpu_custom_call" | custom-call | flops 881852416 | bytes 3801088 | tf_op jit(solution)/shard_map/attn_fwd/pallas_call | solution.py:116
  365.7 7.3 fusion.66
  373.0 4.8 fusion.44
  379.5 4.2 gather_fusion
  390.7 25.0 %attn_fwd.4 = (bf16[1176,384]{1,0:T(8,128)(2,1)}, f32[3,4,1176]{2,1,0:T(4,128)}) custom-call(bf16[1176,1152]{1,0:T(8,128)(2,1)} %convolution_convert_fusion.3.refs_0_.refs_1_.refs_2_, bf16[1176,1152]{1,0:T(8,128)(2,1)} %convolution_convert_fusion.3.refs_0_.refs_1_.refs_2_, bf16[1176,1152]{1,0:T(8,128)(2,1)} %convolution_convert_fusion.3.refs_0_.refs_1_.refs_2_), custom_call_target="tpu_custom_call" | custom-call | flops 2124251136 | bytes 3612672 | tf_op jit(solution)/shard_map/attn_fwd/pallas_call | solution.py:116
  437.8 6.5 fusion.13
  453.2 47.2 %attn_bwd.2 = bf16[1176,1152]{1,0:T(8,128)(2,1)} custom-call(bf16[1176,1152]{1,0:T(8,128)(2,1)} %convolution_convert_fusion.3.refs_0_.refs_1_.refs_2_, bf16[1176,1152]{1,0:T(8,128)(2,1)} %convolution_convert_fusion.3.refs_0_.refs_1_.refs_2_, bf16[1176,1152]{1,0:T(8,128)(2,1)} %convolution_convert_fusion.3.refs_0_.refs_1_.refs_2_, ...), custom_call_target="tpu_custom_call" | custom-call | flops 5310627840 | bytes 7225344 | tf_op jit(solution)/shard_map/attn_bwd/pallas_call | solution.py:158
  500.4 4.6 convolution_convert_fusion.8
  515.5 12.1 %fusion.6 = bf16[464,4096]{1,0:T(8,128)(2,1)S(1)} fusion(f32[464,4096]{1,0:T(8,128)} %copy-done.54, bf16[464,1024]{1,0:T(8,128)(2,1)S(1)} %convolution_convert_fusion.12, bf16[4096,1024]{1,0:T(8,128)(2,1)} %bitcast.169), kind=kOutput, calls=%fused_computation.14 | convolution fusion | flops 3930324992 | bytes 20742144 | tf_op jit(solution)/shard_map/dot_general | solution.py:61
  527.6 4.3 fusion.43
  536.6 16.4 %attn_bwd.3 = bf16[464,3072]{1,0:T(8,128)(2,1)} custom-call(s32[1]{0:T(128)} %dynamic_slice.9.refs_0_, bf16[464,3072]{1,0:T(8,128)(2,1)} %convolution_convert_fusion.5.refs_1_.refs_2_.refs_3_, bf16[464,3072]{1,0:T(8,128)(2,1)} %convolution_convert_fusion.5.refs_1_.refs_2_.refs_3_, bf16[464,3072]{1,0:T(8,128)(2,1)} %convolution_convert_fusion.5.refs_1_.refs_2_.refs_3_, ...), custom_call_target="tpu_custom_call" | custom-call | flops 2204631040 | bytes 7602176 | tf_op jit(solution)/shard_map/attn_bwd/pallas_call | solution.py:158
  553.1 6.7 multiply_reduce_fusion
  559.8 11.9 %convolution_convert_fusion.1 = bf16[4096,1024]{1,0:T(8,128)(2,1)} fusion(bf16[464,1024]{1,0:T(8,128)(2,1)S(1)} %convolution_convert_fusion.12, f32[464,4096]{1,0:T(8,128)} %copy-done.54), kind=kOutput, calls=%fused_computation.16 | convolution fusion | flops 3913613312 | bytes 16941056 | tf_op jit(solution)/shard_map/dot_general | solution.py:55
  580.9 5.7 convolution_convert_fusion.4
  586.6 5.0 gather_fusion.2
  591.6 4.7 select_select_fusion
  596.3 7.3 convolution_convert_fusion.2
  603.6 177.2 %reduce_grads.1 = (bf16[2,2,32,3072]{3,2,1,0:T(8,128)(2,1)}, bf16[2,2,32,1024]{3,2,1,0:T(8,128)(2,1)}, bf16[2,2,32,4096]{3,2,1,0:T(8,128)(2,1)}, bf16[2,2,128,10...) custom-call(bf16[4,2,2,2,32,3072]{5,4,3,2,1,0:T(8,128)(2,1)} %bitcas, ...), custom_call_target="tpu_custom_call" | custom-call | tf_op jit(solution)/shard_map/reduce_grads/pallas_call | solution.py:423
  (242 shorter events, 108.0 us)
Async XLA Ops:
  0.7 417.6 %copy-start = (bf16[384,1536]{1,0:T(8,128)(2,1)S(1)}, bf16[384,1536]{1,0:T(8,128)(2,1)}, u32[]{:S(2)}) copy-start(bf16[384,1536]{1,0:T(8,128)(2,1)} %param.44) | copy-start | bytes 3538948
  0.7 12.4 %copy-start.3 = (bf16[1176,1024]{1,0:T(8,128)(2,1)S(1)}, bf16[1176,1024]{1,0:T(8,128)(2,1)}, u32[]{:S(2)}) copy-start(bf16[1176,1024]{1,0:T(8,128)(2,1)} %param.25) | copy-start | bytes 7225348
  10.9 372.7 %copy-start.32 = (pred[1176]{0:T(1024)(128)(4,1)}, pred[1176]{0:T(1024)(128)(4,1)S(1)}, u32[]{:S(2)}) copy-start(pred[1176]{0:T(1024)(128)(4,1)S(1)} %compare_and_fusion) | copy-start | bytes 3532
  11.0 368.5 %copy-start.28 = (s32[2048]{0:T(1024)}, s32[2048]{0:T(1024)S(1)}, u32[]{:S(2)}) copy-start(s32[2048]{0:T(1024)S(1)} %pad_clamp_fusion) | copy-start | bytes 24580
  17.5 324.7 %copy-start.7 = (f32[464,1024]{1,0:T(8,128)}, f32[464,1024]{1,0:T(8,128)S(1)}, u32[]{:S(2)}) copy-start(f32[464,1024]{1,0:T(8,128)S(1)} %get-tuple-element.109) | copy-start | bytes 5701636
  17.5 324.7 %copy-start.30 = (f32[464]{0:T(512)}, f32[464]{0:T(512)S(1)}, u32[]{:S(2)}) copy-start(f32[464]{0:T(512)S(1)} %broadcast_multiply_fusion.5) | copy-start | bytes 5572
  17.8 237.5 %copy-start.36 = (f32[464]{0:T(512)}, f32[464]{0:T(512)S(1)}, u32[]{:S(2)}) copy-start(f32[464]{0:T(512)S(1)} %multiply_reduce_fusion.2) | copy-start | bytes 5572
  17.9 324.3 %copy-start.42 = (f32[464]{0:T(512)}, f32[464]{0:T(512)S(1)}, u32[]{:S(2)}) copy-start(f32[464]{0:T(512)S(1)} %fusion.63) | copy-start | bytes 5572
  256.8 85.4 %copy-start.38 = (f32[8,1,128]{2,1,0:T(1,128)}, f32[8,1,128]{2,1,0:T(1,128)S(1)}, u32[]{:S(2)}) copy-start(f32[8,1,128]{2,1,0:T(1,128)S(1)} %get-tuple-element.97) | copy-start | bytes 12292
  270.5 34.5 %copy-start.4 = (bf16[1176,1024]{1,0:T(8,128)(2,1)S(1)}, bf16[1176,1024]{1,0:T(8,128)(2,1)}, u32[]{:S(2)}) copy-start(bf16[1176,1024]{1,0:T(8,128)(2,1)} %param.25) | copy-start | bytes 7225348
  270.5 34.5 %copy-start.49 = (bf16[4,2,2,2,32,1024]{5,4,3,2,1,0:T(8,128)(2,1)S(1)}, bf16[4,2,2,2,32,1024]{5,4,3,2,1,0:T(8,128)(2,1)}, u32[]{:S(2)}) copy-start(bf16[4,2,2,2,32,1024]{5,4,3,2,1,0:T(8,128)(2,1)} %get-tuple-element.54) | copy-start | bytes 6291460
  349.7 12.9 %copy-start.8 = (f32[464,1024]{1,0:T(8,128)S(1)}, f32[464,1024]{1,0:T(8,128)}, u32[]{:S(2)}) copy-start(f32[464,1024]{1,0:T(8,128)} %copy-done.7) | copy-start | bytes 5701636
  349.7 12.9 %copy-start.47 = (bf16[4,2,2,2,32,1024]{5,4,3,2,1,0:T(8,128)(2,1)S(1)}, bf16[4,2,2,2,32,1024]{5,4,3,2,1,0:T(8,128)(2,1)}, u32[]{:S(2)}) copy-start(bf16[4,2,2,2,32,1024]{5,4,3,2,1,0:T(8,128)(2,1)} %get-tuple-element.45) | copy-start | bytes 6291460
  362.6 10.4 %slice-start.4 = ((s8[8388608]{0:T(1024)(128)(4,1)}), s8[4194304]{0:T(1024)(128)(4,1)S(1)}, s32[]{:S(2)}) async-start(s8[8388608]{0:T(1024)(128)(4,1)} %bitcast.170), calls=%async_computation.4 | async-start | bytes 8388608
  365.2 167.6 %copy-start.5 = (bf16[464,1024]{1,0:T(8,128)(2,1)}, bf16[464,1024]{1,0:T(8,128)(2,1)S(1)}, u32[]{:S(2)}) copy-start(bf16[464,1024]{1,0:T(8,128)(2,1)S(1)} %get-tuple-element.111) | copy-start | bytes 2850820
  390.7 25.0 %copy-start.17 = (bf16[384,384]{1,0:T(8,128)(2,1)S(1)}, bf16[384,384]{1,0:T(8,128)(2,1)}, u32[]{:S(2)}) copy-start(bf16[384,384]{1,0:T(8,128)(2,1)} %param.42) | copy-start | bytes 884740
  513.3 14.3 %slice-start.2 = ((s8[8388608]{0:T(1024)(128)(4,1)}), s8[4194304]{0:T(1024)(128)(4,1)S(1)}, s32[]{:S(2)}) async-start(s8[8388608]{0:T(1024)(128)(4,1)} %bitcast.166), calls=%async_computation.2 | async-start | bytes 8388608
  515.5 12.1 %slice-start.3 = ((s8[8388608]{0:T(1024)(128)(4,1)}), s8[4194304]{0:T(1024)(128)(4,1)S(1)}, s32[]{:S(2)}) async-start(s8[8388608]{0:T(1024)(128)(4,1)} %bitcast.166), calls=%async_computation.3 | async-start | bytes 8388608
  536.6 16.4 %copy-start.9 = (f32[464,1024]{1,0:T(8,128)S(1)}, f32[464,1024]{1,0:T(8,128)}, u32[]{:S(2)}) copy-start(f32[464,1024]{1,0:T(8,128)} %copy-done.7) | copy-start | bytes 5701636
  536.6 16.5 %copy-start.31 = (f32[464]{0:T(512)S(1)}, f32[464]{0:T(512)}, u32[]{:S(2)}) copy-start(f32[464]{0:T(512)} %copy-done.30) | copy-start | bytes 5572
  536.6 16.5 %copy-start.39 = (f32[8,1,128]{2,1,0:T(1,128)S(1)}, f32[8,1,128]{2,1,0:T(1,128)}, u32[]{:S(2)}) copy-start(f32[8,1,128]{2,1,0:T(1,128)} %copy-done.38) | copy-start | bytes 12292
  536.6 16.5 %copy-start.43 = (f32[464]{0:T(512)S(1)}, f32[464]{0:T(512)}, u32[]{:S(2)}) copy-start(f32[464]{0:T(512)} %copy-done.42) | copy-start | bytes 5572
  559.8 12.6 %copy-start.37 = (f32[464]{0:T(512)S(1)}, f32[464]{0:T(512)}, u32[]{:S(2)}) copy-start(f32[464]{0:T(512)} %copy-done.36) | copy-start | bytes 5572
  780.8 7.6 copy-start.20
  (41 other events, 134.9 us)

commit v4 on v3

--- a/solution.py
+++ b/solution.py
@@ -75,31 +75,34 @@
 def head_rows(values,h,e):
     return jnp.where(lane_mask(values.shape[0],h,e),values,jnp.zeros_like(values))
 
+def attend_group(q_all,k,v,e,live,step):
+    L=q_all.shape[0]; per=128//e; c=e**-0.5*LOG2E
+    vt=v.T
+    results=[]; sums=[]
+    for (s0,n) in chunks(L,step):
+        outs=[]; lses=[]
+        for h in range(per):
+            q=head_rows(q_all[s0:s0+n,:],h,e)
+            st=dot(k,q,NT)
+            if live is not None: st=jnp.where(live,st,-1e30)
+            m=jnp.max(st,axis=0,keepdims=True)
+            p=jnp.exp2((st-m)*c)
+            l=jnp.sum(p,axis=0,keepdims=True)
+            outs.append(dot(vt[h*e:(h+1)*e,:],p.astype(BF))*(1.0/l))
+            lses.append(m*c+jnp.log2(l))
+        results.append(jnp.concatenate(outs,axis=0).T.astype(BF))
+        sums.append(jnp.concatenate(lses,axis=0))
+    if len(results)==1: return results[0],sums[0]
+    return jnp.concatenate(results,axis=0),jnp.concatenate(sums,axis=1)
+
 def fwd_kernel(e,step,masked,want_lse,*refs):
     refs=list(refs)
     count=refs.pop(0) if masked else None
     q_ref,k_ref,v_ref,o_ref=refs[:4]
-    lse_ref=refs[4] if want_lse else None
-    L=q_ref.shape[0]; per=128//e; c=e**-0.5*LOG2E
-    k=k_ref[...]
-    vt=v_ref[...].T
-    live=None
-    if masked:
-        live=lax.broadcasted_iota(jnp.int32,(L,1),0)<count[0]
-    for (s0,n) in chunks(L,step):
-        outs=[]; lses=[]
-        for h in range(per):
-            q=head_rows(q_ref[s0:s0+n,:],h,e)
-            st=dot(k,q,NT)
-            if masked: st=jnp.where(live,st,-1e30)
-            m=jnp.max(st,axis=0,keepdims=True)
-            p=jnp.exp2((st-m)*c)
-            l=jnp.sum(p,axis=0,keepdims=True)
-            o=dot(vt[h*e:(h+1)*e,:],p.astype(BF))
-            outs.append(o*(1.0/l))
-            if want_lse: lses.append(m*c+jnp.log2(l))
-        o_ref[s0:s0+n,:]=jnp.concatenate(outs,axis=0).T.astype(BF)
-        if want_lse: lse_ref[0,:,s0:s0+n]=jnp.concatenate(lses,axis=0)
+    L=q_ref.shape[0]
+    live=lax.broadcasted_iota(jnp.int32,(L,1),0)<count[0] if masked else None
+    o_ref[...],lse=attend_group(q_ref[...],k_ref[...],v_ref[...],e,live,step)
+    if want_lse: refs[4][0]=lse
 
 def attn_fwd(mixed,heads,count=None,step=1280,want_lse=True):
     L,w3=mixed.shape; Dm=w3//3; e=Dm//heads; G=Dm//128; per=128//e
@@ -256,38 +259,97 @@
             if 0<=i<n: order.append(chunks[i][s])
     return order
 
-def ag_kernel(plan,n,*refs):
-    shards=refs[:n]; gain=refs[n]; fulls=refs[n+1:2*n+1]; gout=refs[2*n+1]
-    rest=refs[2*n+2:]
-    owns=rest[:len(plan)]; gown,local,send,recv,gsend,grecv,glocal=rest[len(plan):]
+def by_turn(chunks):
+    turns=[[] for _ in range(len(chunks)+len(chunks[0])-1)]
+    for i,chunk in enumerate(chunks):
+        for s,stage in enumerate(chunk): turns[i+s].append((s,stage))
+    return [[stage for _,stage in sorted(t,key=lambda p:p[0])] for t in turns]
+
+def scaled_norm(values,gain_blocks,row,out_ref):
+    normed=plain_norm(values.astype(F32))
+    for t in range(gain_blocks.shape[0]):
+        cols=slice(t*128,(t+1)*128)
+        out_ref[:,cols]=(normed[:,cols]*gain_blocks[t,row:row+1,:].astype(F32)).astype(BF)
+
+def ag_kernel(plan,n,heads,first,*refs):
+    shards=refs[:n]; gain,tok_ref,seen_ref,live_ref=refs[n:n+4]
+    fulls=refs[n+4:2*n+4]; gout,tattn,cin,cmixed,cattn,clse=refs[2*n+4:2*n+10]
+    rest=refs[2*n+10:]
+    k=len(plan)
+    owns=rest[:k]; gown,local,send,recv,gsend,grecv,glocal,gv,tin,tw,cw,wsem=rest[k:]
     z,y,x,c=place()
-    greet(everyone_on_tok())
-    gs,gf=gains_steps(gain,gout,gsend,grecv)
-    gs()
-    g0=pltpu.make_async_copy(gain,gown,glocal.at[0]); g0.start()
+    turn=pl.program_id(0)
     steps=[]
     for i,(w,r0,rn,c0,cn,quarter) in enumerate(plan):
         steps.append(gather_steps(shards[w],fulls[w],owns[i],(pl.ds(r0,rn),pl.ds(c0,cn)),quarter,local.at[i],send.at[i],recv.at[i]))
     groups={}
     for st,entry in zip(steps,plan): groups.setdefault(entry[:3],[]).append(st)
-    for f in interleave([together(m) for m in groups.values()]): f()
-    g0.wait()
-    g1=pltpu.make_async_copy(gown,gout.at[z*2+y],glocal.at[1]); g1.start(); g1.wait()
-    gf()
-
-def gather_weights(shards, gains, plan, cid):
-    n=len(shards)
+    turns=by_turn([together(m) for m in groups.values()])
+    done={w:i+len(steps[0])-1 for i,(w,_,_) in enumerate(groups)}
+    gs,gf=gains_steps(gain,gout,gsend,grecv)
+    width=tok_ref.shape[1]; G=width//128; e=width//heads
+    take=lambda w,dst,i: pltpu.make_async_copy(fulls[w],dst,wsem.at[i])
+    for t,fs in enumerate(turns):
+        @pl.when(turn==t)
+        def _(t=t,fs=fs):
+            if t==0: greet(everyone_on_tok())
+            for f in fs: f()
+            if t==0:
+                gs()
+                g0=pltpu.make_async_copy(gain,gown,glocal.at[0]); g0.start(); g0.wait()
+                pltpu.make_async_copy(gown,gout.at[z*2+y],glocal.at[1]).start()
+            if t==2:
+                pltpu.make_async_copy(gown,gout.at[z*2+y],glocal.at[1]).wait()
+                gf()
+                g2=pltpu.make_async_copy(gout,gv,glocal.at[2]); g2.start(); g2.wait()
+            if t==3: scaled_norm(tok_ref[...],gv,0,tin)
+            if t==4: scaled_norm(seen_ref[...],gv,2,cin)
+            if t==done[0]:
+                take(0,tw,0).start(); take(0,tw,0).wait()
+            if t==done[4]:
+                take(4,cw,1).start(); take(4,cw,1).wait()
+    def block(ref,part,g): return ref[:,:,:,:,:,pl.ds(pl.multiple_of((part*G+g)*128,128),128)].reshape(width,128)
+    @pl.when((turn>=first)&(turn<first+G))
+    def _():
+        g=turn-first
+        q,key,v=[dot(tin[...],block(tw,part,g)).astype(BF) for part in range(3)]
+        o,_=attend_group(q,key,v,e,None,1280)
+        tattn[:,pl.ds(pl.multiple_of(g*128,128),128)]=o
+    later=first+G
+    each=G//(len(turns)-later)
+    @pl.when(turn>=later)
+    def _():
+        live=live_ref[...]!=0
+        for j in range(each):
+            g=(turn-later)*each+j
+            parts=[dot(cin[...],block(cw,part,g)).astype(BF) for part in range(3)]
+            for part in range(3):
+                cmixed[:,pl.ds(pl.multiple_of((part*G+g)*128,128),128)]=parts[part]
+            o,lse=attend_group(*parts,e,live,1280)
+            cattn[:,pl.ds(pl.multiple_of(g*128,128),128)]=o
+            clse[g]=lse
+
+def gather_and_attend(shards,gains,tokens,seen,live,heads,plan,cid):
+    n=len(shards); k=len(plan)
     views=[s.reshape(2,2,s.shape[0]//4,s.shape[1]) for s in shards]
     outs=[jax.ShapeDtypeStruct((4,2,2,2,s.shape[0]//4,s.shape[1]),s.dtype) for s in shards]
     outs.append(jax.ShapeDtypeStruct((8,)+gains.shape,gains.dtype))
-    owns=[pltpu.VMEM(((rn,cn) if q else (2,rn,cn)),jnp.bfloat16) for (w,r0,rn,c0,cn,q) in plan]
-    k=len(plan)
-    res=pl.pallas_call(functools.partial(ag_kernel,plan,n),out_shape=outs,in_specs=[ANY]*(n+1),out_specs=[ANY]*(n+1),
-        scratch_shapes=owns+[pltpu.VMEM(gains.shape,gains.dtype),pltpu.SemaphoreType.DMA((k,2)),pltpu.SemaphoreType.DMA((k,6)),pltpu.SemaphoreType.DMA((k,6)),
-            pltpu.SemaphoreType.DMA((7,)),pltpu.SemaphoreType.DMA((7,)),pltpu.SemaphoreType.DMA((2,))],
-        compiler_params=pltpu.CompilerParams(collective_id=cid,has_side_effects=True),name="gather_weights")(*views,gains)
-    return [o.reshape(8*s.shape[0],s.shape[1]) for o,s in zip(res[:n],shards)],res[n]
-
+    (L,width),slots=tokens.shape,seen.shape[0]
+    G=width//128
+    extra=[((L,width),BF),((slots,width),BF),((slots,3*width),BF),((slots,width),BF),((G,heads//G,slots),F32)]
+    outs+=[jax.ShapeDtypeStruct(s,d) for s,d in extra]
+    whole=lambda s: pl.BlockSpec(s,lambda t: (0,)*len(s))
+    owns=[pltpu.VMEM(((rn,cn) if q else (2,rn,cn)),BF) for (w,r0,rn,c0,cn,q) in plan]
+    S=pltpu.SemaphoreType.DMA
+    turns=len({entry[:3] for entry in plan})+4
+    scratch=owns+[pltpu.VMEM(gains.shape,BF),S((k,2)),S((k,6)),S((k,6)),S((7,)),S((7,)),S((3,)),
+        pltpu.VMEM((8,)+gains.shape,BF),pltpu.VMEM((L,width),BF),pltpu.VMEM(outs[0].shape,BF),pltpu.VMEM(outs[4].shape,BF),S((2,))]
+    first=turns-G-4
+    res=pl.pallas_call(functools.partial(ag_kernel,plan,n,heads,first),grid=(turns,),out_shape=outs,
+        in_specs=[ANY]*(n+1)+[whole(tokens.shape),whole(seen.shape),whole(live.shape)],
+        out_specs=[ANY]*(n+1)+[whole(s) for s,_ in extra],scratch_shapes=scratch,
+        compiler_params=pltpu.CompilerParams(collective_id=cid,has_side_effects=True,vmem_limit_bytes=60<<20),name="gather_and_attend")(*views,gains,tokens,seen,live)
+    return [o.reshape(8*s.shape[0],s.shape[1]) for o,s in zip(res[:n],shards)],res[n],res[n+1:]
 
 def reduce_steps(grad, out, rn, rows, bufs, order, everywhere, local, send, recv):
     z,y,x,c=place()
@@ -431,7 +493,7 @@
 
 def gather_plan(shards):
     plan = []
-    for w in (1, 0, 2, 3, 4, 6, 7, 5):
+    for w in (0, 4, 1, 2, 3, 6, 7, 5):
         rows, wide = shards[w].shape[0] // 4, shards[w].shape[1]
         rest = (wide // 3 + 64) // 128 * 128
         parts = 1 if wide == shards[w].shape[0] * 8 else 2
@@ -442,12 +504,21 @@
     return plan
 
 
-def every_weight(tuned, gains, shards):
-    if not tuned:
-        return tuple(lax.all_gather(v, "tok", axis=0, tiled=True) for v in gains + shards)
-    packed = jnp.pad(jnp.stack(gains), ((0, 12), (0, 0)))
-    full, norms = gather_weights(list(shards), packed, gather_plan(shards), 1)
-    return tuple(norms[:, i, :].reshape(-1) for i in range(4)) + tuple(full)
+def every_weight(tuned, gains, shards, tokens, seen, live, heads):
+    if tuned:
+        packed = jnp.pad(jnp.stack(gains), ((0, 12), (0, 0)))
+        full, norms, attended = gather_and_attend(
+            list(shards), packed, tokens, seen, live, heads, gather_plan(shards), 1
+        )
+        return tuple(norms[:, i, :].reshape(-1) for i in range(4)) + tuple(full), attended
+    full = tuple(lax.all_gather(v, "tok", axis=0, tiled=True) for v in gains + shards)
+    target_in = layer_norm(tokens.astype(F32), full[0].astype(F32)).astype(BF)
+    target_attn = attn_fwd(product(target_in, full[4]).astype(BF), heads, want_lse=False)[0]
+    context_in = layer_norm(seen.astype(F32), full[2].astype(F32)).astype(BF)
+    context_mixed = product(context_in, full[8]).astype(BF)
+    count = jnp.sum(live, axis=0)
+    context_attn, context_lse = attn_fwd(context_mixed, heads, count)
+    return full, (target_attn, context_in, context_mixed, context_attn, context_lse)
 
 
 def every_grad(tuned, context, predict):
@@ -609,6 +680,39 @@
     device_index = lane_index * head_devices + head_index
     counts_here = lax.dynamic_slice_in_dim(visible_count, device_index * clips_here, clips_here)
     tuned = lax.axis_size("tok") == 8 and head_devices == 4
+    visible_pos = clip_order[:, :VMOST]
+    slot_live = jnp.arange(VMOST, dtype=jnp.int32)[None, :] < counts_here[:, None]
+    holds = visible_pos[:, :, None] == jnp.arange(clip_len, dtype=jnp.int32)[None, None, :]
+    holds = jnp.logical_and(holds, slot_live[:, :, None])
+    visible = jnp.any(holds, axis=1)
+    slot = jnp.arange(VMOST, dtype=jnp.int32)[None, :, None]
+    order_rank = jnp.sum(jnp.where(holds, slot, 0), axis=1)
+    token_grid = tokens.reshape(clips_here, clip_len, model_width)
+    seen_rows = jnp.einsum(
+        "csl,cld->csd", holds.astype(BF), token_grid, preferred_element_type=jnp.float32
+    )
+    seen_rows = seen_rows.reshape(clips_here * VMOST, model_width)
+    seen_low = seen_rows.astype(BF)
+    live_column = slot_live.astype(jnp.int32).reshape(-1, 1)
+    weights, attended = every_weight(
+        tuned,
+        (target_prenorm, target_midnorm, context_prenorm, context_midnorm),
+        (
+            target_project,
+            target_outward,
+            target_expand,
+            target_shrink,
+            context_project,
+            context_outward,
+            context_expand,
+            context_shrink,
+        ),
+        tokens,
+        seen_low,
+        live_column,
+        H,
+    )
+    target_attn, context_in, context_mixed, context_attn, context_lse = attended
     (
         tgt_prenorm_full,
         tgt_midnorm_full,
@@ -622,45 +726,14 @@
         ctx_outward_full,
         ctx_expand_full,
         ctx_shrink_full,
-    ) = every_weight(
-        tuned,
-        (target_prenorm, target_midnorm, context_prenorm, context_midnorm),
-        (
-            target_project,
-            target_outward,
-            target_expand,
-            target_shrink,
-            context_project,
-            context_outward,
-            context_expand,
-            context_shrink,
-        ),
-    )
+    ) = weights
     tokens_wide = tokens.astype(jnp.float32)
-    target_in = layer_norm(tokens_wide, tgt_prenorm_full.astype(jnp.float32)).astype(jnp.bfloat16)
-    target_mixed = product(target_in, tgt_project_full).astype(jnp.bfloat16)
-    target_attn = attn_fwd(target_mixed, H, want_lse=False)[0]
     target_mid = tokens_wide + product(target_attn, tgt_outward_full)
     target_out = target_ffn(
         target_mid, tgt_midnorm_full.astype(jnp.float32), tgt_expand_full, tgt_shrink_full
     )
-    visible_pos = clip_order[:, :VMOST]
-    slot_live = jnp.arange(VMOST, dtype=jnp.int32)[None, :] < counts_here[:, None]
-    holds = visible_pos[:, :, None] == jnp.arange(clip_len, dtype=jnp.int32)[None, None, :]
-    holds = jnp.logical_and(holds, slot_live[:, :, None])
-    visible = jnp.any(holds, axis=1)
-    slot = jnp.arange(VMOST, dtype=jnp.int32)[None, :, None]
-    order_rank = jnp.sum(jnp.where(holds, slot, 0), axis=1)
-    token_grid = tokens.reshape(clips_here, clip_len, model_width)
-    seen_rows = jnp.einsum(
-        "csl,cld->csd", holds.astype(BF), token_grid, preferred_element_type=jnp.float32
-    )
-    seen_rows = seen_rows.reshape(clips_here * VMOST, model_width)
     ctx_prenorm_wide = ctx_prenorm_full.astype(jnp.float32)
     ctx_midnorm_wide = ctx_midnorm_full.astype(jnp.float32)
-    context_in = layer_norm(seen_rows, ctx_prenorm_wide).astype(jnp.bfloat16)
-    context_mixed = product(context_in, ctx_project_full).astype(jnp.bfloat16)
-    context_attn, context_lse = attn_fwd(context_mixed, H, counts_here)
     context_mid = (seen_rows + product(context_attn, ctx_outward_full)).astype(jnp.bfloat16)
     context_out, ffn_saved = feed_forward(
         context_mid, ctx_midnorm_wide, ctx_expand_full, ctx_shrink_full

time: 814 us -> 753 us (0.925)
  Pallas kernels: 580 us -> 537 us
  matrix products: 143 us -> 127 us
    pallas_call x3 -> x1, Pallas kernels: 72.4 us -> 25.3 us  [attn_fwd(): return f(*((count,) if masked else ()), mixed, mixed, mixed)]
    dot_general x12 -> x10, matrix products: 55.7 us -> 39.8 us  [product(): return jnp.dot(former, latter, preferred_element_type=jnp.float32)]
where the time goes in v4:
time: 753 us; the launch traced here: 746 us
  Pallas kernels  537 us (71%)
  matrix products  127 us (17%)
  other arithmetic  46.3 us (6%)
  local copies, waits for them, and re-layouts  31.6 us (4%)
    pallas_call x1, Pallas kernels, gather_and_attend(): pl.pallas_call(functools.partial(ag_kernel, plan, n, heads, first), grid=...  236 us
    pallas_call x1, Pallas kernels, reduce_grads(): pl.pallas_call(functools.partial(rs_kernel, plan, n), out_shape=outs, in_...  181 us
    pallas_call x2, Pallas kernels, attn_bwd(): pl.pallas_call(functools.partial(bwd_kernel, e, step, masked), grid_spec=...  63.6 us
    dot_general x10, matrix products, inner_rows(): lax.dot_general(former, latter, (((0,), (0,)), ((), ())), preferred_eleme...  43.1 us
    dot_general x10, matrix products, inner_cols(): lax.dot_general(former, latter, (((1,), (1,)), ((), ())), preferred_eleme...  41 us
    dot_general x10, matrix products, product(): return jnp.dot(former, latter, preferred_element_type=jnp.float32)  39.8 us
    pallas_call x1, Pallas kernels, target_ffn(): pl.pallas_call(ffn_kernel, grid=(hidden // block,), in_specs=[whole, pl.B...  30.9 us
    pallas_call x1, Pallas kernels, attn_fwd(): return f(*((count,) if masked else ()), mixed, mixed, mixed)  25.3 us

profile of v4, /device:TPU:0, one launch (start us, length us, event | category | flops | bytes accessed | tf_op | source)
XLA Modules:
  0.0 745.9 jit_solution(8522881351434540499)
XLA Ops:
  19.8 236.2 %gather_and_attend.1 = (bf16[4,2,2,2,32,3072]{5,4,3,2,1,0:T(8,128)(2,1)}, bf16[4,2,2,2,32,1024]{5,4,3,2,1,0:T(8,128)(2,1)}, bf16[4,2,2,2,32,4096]{5,4,3,2,1,0:T(...) custom-call(bf16[2,2,32,3072]{3,2,1,0:T(8,128)(2,1)} %bitcast.135, ...), custom_call_target="tpu_custom_call" | custom-call | tf_op jit(solution)/shard_map/gather_and_attend/pallas_call | solution.py:348
  257.5 3.8 convert_reduce_fusion
  262.0 4.3 convert_add_fusion.mid_ref
  266.4 30.9 %target_ffn.1 = f32[1176,1024]{1,0:T(8,128)} custom-call(f32[1176,1024]{1,0:T(8,128)} %convert_add_fusion.mid_ref, f32[1,1024]{1,0:T(1,128)} %get-tuple-element.101.gain_ref, bf16[1024,4096]{1,0:T(8,128)(2,1)} %bitcast.165, bf16[4096,1024]{1,0:T(8,128)(2,1)} %bitcast.166), custom_call_target="tpu_custom_call" | custom-call | flops 19730006016 | bytes 26411008 | tf_op jit(solution)/shard_map/target_ffn/pallas_call | solution.py:602
  297.3 6.9 fusion.58
  304.2 11.0 %fusion.35 = bf16[464,1024]{1,0:T(8,128)(2,1)S(1)} fusion(bf16[464,1024]{1,0:T(8,128)(2,1)S(1)} %get-tuple-element.116, bf16[4096,1024]{1,0:T(8,128)(2,1)} %bitcast.163, f32[464,4096]{1,0:T(8,128)S(1)} %fusion.58), kind=kOutput, calls=%fused_computation.74 | convolution fusion | flops 3910844416 | bytes 17891328 | tf_op jit(solution)/shard_map/dot_general | solution.py:51
  316.8 4.2 gather_fusion
  321.0 3.2 fusion.67
  324.6 3.3 convolution_convert_fusion.2.refs_0_.refs_1_.refs_2_
  328.0 25.3 %attn_fwd.1 = (bf16[1176,384]{1,0:T(8,128)(2,1)}, f32[3,4,1176]{2,1,0:T(4,128)}) custom-call(bf16[1176,1152]{1,0:T(8,128)(2,1)} %convolution_convert_fusion.2.refs_0_.refs_1_.refs_2_, bf16[1176,1152]{1,0:T(8,128)(2,1)} %convolution_convert_fusion.2.refs_0_.refs_1_.refs_2_, bf16[1176,1152]{1,0:T(8,128)(2,1)} %convolution_convert_fusion.2.refs_0_.refs_1_.refs_2_), custom_call_target="tpu_custom_call" | custom-call | flops 2124251136 | bytes 3612672 | tf_op jit(solution)/shard_map/attn_fwd/pallas_call | solution.py:119
  371.3 4.0 convolution_convert_fusion.4
  375.3 6.5 fusion.13
  390.7 47.2 %attn_bwd.2 = bf16[1176,1152]{1,0:T(8,128)(2,1)} custom-call(bf16[1176,1152]{1,0:T(8,128)(2,1)} %convolution_convert_fusion.2.refs_0_.refs_1_.refs_2_, bf16[1176,1152]{1,0:T(8,128)(2,1)} %convolution_convert_fusion.2.refs_0_.refs_1_.refs_2_, bf16[1176,1152]{1,0:T(8,128)(2,1)} %convolution_convert_fusion.2.refs_0_.refs_1_.refs_2_, ...), custom_call_target="tpu_custom_call" | custom-call | flops 5310627840 | bytes 7225344 | tf_op jit(solution)/shard_map/attn_bwd/pallas_call | solution.py:161
  438.0 4.6 convolution_convert_fusion.6
  453.0 12.1 %fusion.6 = bf16[464,4096]{1,0:T(8,128)(2,1)S(1)} fusion(f32[464,4096]{1,0:T(8,128)} %copy-done.51, bf16[464,1024]{1,0:T(8,128)(2,1)S(1)} %convolution_convert_fusion.10, bf16[4096,1024]{1,0:T(8,128)(2,1)} %bitcast.164), kind=kOutput, calls=%fused_computation.13 | convolution fusion | flops 3930324992 | bytes 20742144 | tf_op jit(solution)/shard_map/dot_general | solution.py:61
  465.1 4.3 fusion.34
  474.2 16.4 %attn_bwd.3 = bf16[464,3072]{1,0:T(8,128)(2,1)} custom-call(s32[1]{0:T(128)} %dynamic_slice.9.refs_0_, bf16[464,3072]{1,0:T(8,128)(2,1)} %get-tuple-element.59.refs_1_.refs_2_.refs_3_, bf16[464,3072]{1,0:T(8,128)(2,1)} %get-tuple-element.59.refs_1_.refs_2_.refs_3_, bf16[464,3072]{1,0:T(8,128)(2,1)} %get-tuple-element.59.refs_1_.refs_2_.refs_3_, ...), custom_call_target="tpu_custom_call" | custom-call | flops 2204631040 | bytes 7602176 | tf_op jit(solution)/shard_map/attn_bwd/pallas_call | solution.py:161
  490.6 6.7 multiply_reduce_fusion
  497.3 11.9 %convolution_convert_fusion = bf16[4096,1024]{1,0:T(8,128)(2,1)} fusion(bf16[464,1024]{1,0:T(8,128)(2,1)S(1)} %convolution_convert_fusion.10, f32[464,4096]{1,0:T(8,128)} %copy-done.51), kind=kOutput, calls=%fused_computation.15 | convolution fusion | flops 3913613312 | bytes 16941056 | tf_op jit(solution)/shard_map/dot_general | solution.py:55
  518.9 5.5 convolution_convert_fusion.3
  524.4 5.0 gather_fusion.2
  529.4 4.7 select_select_fusion
  534.1 7.4 convolution_convert_fusion.1
  541.5 180.7 %reduce_grads.1 = (bf16[2,2,32,3072]{3,2,1,0:T(8,128)(2,1)}, bf16[2,2,32,1024]{3,2,1,0:T(8,128)(2,1)}, bf16[2,2,32,4096]{3,2,1,0:T(8,128)(2,1)}, bf16[2,2,128,10...) custom-call(bf16[4,2,2,2,32,3072]{5,4,3,2,1,0:T(8,128)(2,1)} %bitcas, ...), custom_call_target="tpu_custom_call" | custom-call | tf_op jit(solution)/shard_map/reduce_grads/pallas_call | solution.py:485
  (224 shorter events, 95.5 us)
Async XLA Ops:
  0.7 355.2 %copy-start = (bf16[384,1536]{1,0:T(8,128)(2,1)S(1)}, bf16[384,1536]{1,0:T(8,128)(2,1)}, u32[]{:S(2)}) copy-start(bf16[384,1536]{1,0:T(8,128)(2,1)} %param.44) | copy-start | bytes 3538948
  8.5 7.3 copy-start.40
  10.8 310.1 %copy-start.30 = (pred[1176]{0:T(1024)(128)(4,1)}, pred[1176]{0:T(1024)(128)(4,1)S(1)}, u32[]{:S(2)}) copy-start(pred[1176]{0:T(1024)(128)(4,1)S(1)} %compare_and_fusion) | copy-start | bytes 3532
  10.9 305.9 %copy-start.26 = (s32[2048]{0:T(1024)}, s32[2048]{0:T(1024)S(1)}, u32[]{:S(2)}) copy-start(s32[2048]{0:T(1024)S(1)} %pad_clamp_fusion) | copy-start | bytes 24580
  17.4 238.6 %copy-start.34 = (f32[464]{0:T(512)}, f32[464]{0:T(512)S(1)}, u32[]{:S(2)}) copy-start(f32[464]{0:T(512)S(1)} %get-tuple-element.96) | copy-start | bytes 5572
  261.4 209.0 %copy-start.3 = (bf16[464,1024]{1,0:T(8,128)(2,1)}, bf16[464,1024]{1,0:T(8,128)(2,1)S(1)}, u32[]{:S(2)}) copy-start(bf16[464,1024]{1,0:T(8,128)(2,1)S(1)} %get-tuple-element.116) | copy-start | bytes 2850820
  304.2 11.0 %copy-start.51 = (f32[464,4096]{1,0:T(8,128)}, f32[464,4096]{1,0:T(8,128)S(1)}, u32[]{:S(2)}) copy-start(f32[464,4096]{1,0:T(8,128)S(1)} %fusion.58) | copy-start | bytes 22806532
  304.2 11.9 %copy-start.22 = (bf16[1024,384]{1,0:T(8,128)(2,1)S(1)}, bf16[1024,384]{1,0:T(8,128)(2,1)}, u32[]{:S(2)}) copy-start(bf16[1024,384]{1,0:T(8,128)(2,1)} %param.38) | copy-start | bytes 2359300
  328.0 25.3 %copy-start.15 = (bf16[384,384]{1,0:T(8,128)(2,1)S(1)}, bf16[384,384]{1,0:T(8,128)(2,1)}, u32[]{:S(2)}) copy-start(bf16[384,384]{1,0:T(8,128)(2,1)} %param.42) | copy-start | bytes 884740
  355.9 5.5 slice-start.4
  383.7 5.3 copy-start.9
  437.9 4.6 copy-start.12
  450.8 14.3 %slice-start.2 = ((s8[8388608]{0:T(1024)(128)(4,1)}), s8[4194304]{0:T(1024)(128)(4,1)S(1)}, s32[]{:S(2)}) async-start(s8[8388608]{0:T(1024)(128)(4,1)} %bitcast.160), calls=%async_computation.2 | async-start | bytes 8388608
  453.0 12.1 %slice-start.3 = ((s8[8388608]{0:T(1024)(128)(4,1)}), s8[4194304]{0:T(1024)(128)(4,1)S(1)}, s32[]{:S(2)}) async-start(s8[8388608]{0:T(1024)(128)(4,1)} %bitcast.160), calls=%async_computation.3 | async-start | bytes 8388608
  474.2 16.4 %copy-start.6 = (f32[464,1024]{1,0:T(8,128)S(1)}, f32[464,1024]{1,0:T(8,128)}, u32[]{:S(2)}) copy-start(f32[464,1024]{1,0:T(8,128)} %copy-done.5) | copy-start | bytes 5701636
  474.2 16.4 %copy-start.29 = (f32[464]{0:T(512)S(1)}, f32[464]{0:T(512)}, u32[]{:S(2)}) copy-start(f32[464]{0:T(512)} %copy-done.28) | copy-start | bytes 5572
  474.2 16.4 %copy-start.36 = (f32[8,1,128]{2,1,0:T(1,128)S(1)}, f32[8,1,128]{2,1,0:T(1,128)}, u32[]{:S(2)}) copy-start(f32[8,1,128]{2,1,0:T(1,128)} %get-tuple-element.100) | copy-start | bytes 12292
  474.2 16.4 %copy-start.39 = (f32[464]{0:T(512)S(1)}, f32[464]{0:T(512)}, u32[]{:S(2)}) copy-start(f32[464]{0:T(512)} %fusion.56) | copy-start | bytes 5572
  497.3 12.6 %copy-start.35 = (f32[464]{0:T(512)S(1)}, f32[464]{0:T(512)}, u32[]{:S(2)}) copy-start(f32[464]{0:T(512)} %copy-done.34) | copy-start | bytes 5572
  518.9 5.5 copy-start.27
  524.4 5.0 copy-start.31
  529.4 4.7 copy-start.4
  529.4 4.7 copy-start.53
  722.2 7.6 %copy-start.18 = (bf16[2,2,32,4096]{3,2,1,0:T(8,128)(2,1)S(1)}, bf16[2,2,32,4096]{3,2,1,0:T(8,128)(2,1)}, u32[]{:S(2)}) copy-start(bf16[2,2,32,4096]{3,2,1,0:T(8,128)(2,1)} %get-tuple-element.66) | copy-start | bytes 3145732
  (36 other events, 97.2 us)

commit v5 on v4

--- a/solution.py
+++ b/solution.py
@@ -271,12 +271,12 @@
         cols=slice(t*128,(t+1)*128)
         out_ref[:,cols]=(normed[:,cols]*gain_blocks[t,row:row+1,:].astype(F32)).astype(BF)
 
-def ag_kernel(plan,n,heads,first,*refs):
+def ag_kernel(plan,n,heads,*refs):
     shards=refs[:n]; gain,tok_ref,seen_ref,live_ref=refs[n:n+4]
-    fulls=refs[n+4:2*n+4]; gout,tattn,cin,cmixed,cattn,clse=refs[2*n+4:2*n+10]
+    fulls=refs[n+4:2*n+4]; gout,tout,cin,cmixed,cattn,clse=refs[2*n+4:2*n+10]
     rest=refs[2*n+10:]
     k=len(plan)
-    owns=rest[:k]; gown,local,send,recv,gsend,grecv,glocal,gv,tin,tw,cw,wsem=rest[k:]
+    owns=rest[:k]; gown,local,send,recv,gsend,grecv,glocal,gv,tin,tattn,total,pw,ow,ew,sw,wsem=rest[k:]
     z,y,x,c=place()
     turn=pl.program_id(0)
     steps=[]
@@ -288,11 +288,22 @@
     done={w:i+len(steps[0])-1 for i,(w,_,_) in enumerate(groups)}
     gs,gf=gains_steps(gain,gout,gsend,grecv)
     width=tok_ref.shape[1]; G=width//128; e=width//heads
+    first=done[0]+1; outward=first+G//2; dense=done[3]+1; end=len(turns)-1
+    blocks=8//(end-dense); block_width=ew.shape[-1]
+    assert done[1]<outward and done[4]<outward and done[2]<dense and outward+G==end+1
     take=lambda w,dst,i: pltpu.make_async_copy(fulls[w],dst,wsem.at[i])
+    def take_block(j):
+        b=(turn-dense)*blocks+j
+        cols=pl.ds(pl.multiple_of(b*block_width,128),block_width)
+        return (pltpu.make_async_copy(fulls[2].at[:,:,:,:,:,cols],ew.at[j],wsem.at[2+2*j]),
+                pltpu.make_async_copy(fulls[3].at[b//2,b%2],sw.at[j],wsem.at[3+2*j]))
     for t,fs in enumerate(turns):
         @pl.when(turn==t)
         def _(t=t,fs=fs):
             if t==0: greet(everyone_on_tok())
+            if t==first: take(0,pw,0).start()
+            if t==outward:
+                take(4,pw,0).start(); take(1,ow,1).start()
             for f in fs: f()
             if t==0:
                 gs()
@@ -304,30 +315,41 @@
                 g2=pltpu.make_async_copy(gout,gv,glocal.at[2]); g2.start(); g2.wait()
             if t==3: scaled_norm(tok_ref[...],gv,0,tin)
             if t==4: scaled_norm(seen_ref[...],gv,2,cin)
-            if t==done[0]:
-                take(0,tw,0).start(); take(0,tw,0).wait()
-            if t==done[4]:
-                take(4,cw,1).start(); take(4,cw,1).wait()
-    def block(ref,part,g): return ref[:,:,:,:,:,pl.ds(pl.multiple_of((part*G+g)*128,128),128)].reshape(width,128)
-    @pl.when((turn>=first)&(turn<first+G))
+            if t==first: take(0,pw,0).wait()
+            if t==outward:
+                take(4,pw,0).wait(); take(1,ow,1).wait()
+                total[...]=tok_ref[...].astype(F32)+dot(tattn[...],ow[...].reshape(width,width))
+                scaled_norm(total[...],gv,1,tin)
+    def block(part,g): return pw[:,:,:,:,:,pl.ds(pl.multiple_of((part*G+g)*128,128),128)].reshape(width,128)
+    @pl.when((turn>=first)&(turn<outward))
     def _():
-        g=turn-first
-        q,key,v=[dot(tin[...],block(tw,part,g)).astype(BF) for part in range(3)]
-        o,_=attend_group(q,key,v,e,None,1280)
-        tattn[:,pl.ds(pl.multiple_of(g*128,128),128)]=o
-    later=first+G
-    each=G//(len(turns)-later)
-    @pl.when(turn>=later)
+        @pl.loop(0,2)
+        def _(j):
+            g=(turn-first)*2+j
+            q,key,v=[dot(tin[...],block(part,g)).astype(BF) for part in range(3)]
+            o,_=attend_group(q,key,v,e,None,1280)
+            tattn[:,pl.ds(pl.multiple_of(g*128,128),128)]=o
+    @pl.when(turn>=outward)
     def _():
-        live=live_ref[...]!=0
-        for j in range(each):
-            g=(turn-later)*each+j
-            parts=[dot(cin[...],block(cw,part,g)).astype(BF) for part in range(3)]
-            for part in range(3):
-                cmixed[:,pl.ds(pl.multiple_of((part*G+g)*128,128),128)]=parts[part]
-            o,lse=attend_group(*parts,e,live,1280)
-            cattn[:,pl.ds(pl.multiple_of(g*128,128),128)]=o
-            clse[g]=lse
+        g=turn-outward
+        parts=[dot(cin[...],block(part,g)).astype(BF) for part in range(3)]
+        for part in range(3):
+            cmixed[:,pl.ds(pl.multiple_of((part*G+g)*128,128),128)]=parts[part]
+        o,lse=attend_group(*parts,e,live_ref[...]!=0,1280)
+        cattn[:,pl.ds(pl.multiple_of(g*128,128),128)]=o
+        clse[g]=lse
+    @pl.when((turn>=dense)&(turn<end))
+    def _():
+        for j in range(blocks):
+            for copy in take_block(j): copy.start()
+        for j in range(blocks):
+            for copy in take_block(j): copy.wait()
+            active=jax.nn.gelu(dot(tin[...],ew[j].reshape(width,block_width))).astype(BF)
+            total[...]+=dot(active,sw[j].reshape(block_width,width))
+    @pl.when(turn==end)
+    def _():
+        total[...]=plain_norm(total[...])
+        put=pltpu.make_async_copy(total,tout,wsem.at[0]); put.start(); put.wait()
 
 def gather_and_attend(shards,gains,tokens,seen,live,heads,plan,cid):
     n=len(shards); k=len(plan)
@@ -336,18 +358,19 @@
     outs.append(jax.ShapeDtypeStruct((8,)+gains.shape,gains.dtype))
     (L,width),slots=tokens.shape,seen.shape[0]
     G=width//128
-    extra=[((L,width),BF),((slots,width),BF),((slots,3*width),BF),((slots,width),BF),((G,heads//G,slots),F32)]
+    extra=[((L,width),F32),((slots,width),BF),((slots,3*width),BF),((slots,width),BF),((G,heads//G,slots),F32)]
     outs+=[jax.ShapeDtypeStruct(s,d) for s,d in extra]
     whole=lambda s: pl.BlockSpec(s,lambda t: (0,)*len(s))
     owns=[pltpu.VMEM(((rn,cn) if q else (2,rn,cn)),BF) for (w,r0,rn,c0,cn,q) in plan]
     S=pltpu.SemaphoreType.DMA
     turns=len({entry[:3] for entry in plan})+4
     scratch=owns+[pltpu.VMEM(gains.shape,BF),S((k,2)),S((k,6)),S((k,6)),S((7,)),S((7,)),S((3,)),
-        pltpu.VMEM((8,)+gains.shape,BF),pltpu.VMEM((L,width),BF),pltpu.VMEM(outs[0].shape,BF),pltpu.VMEM(outs[4].shape,BF),S((2,))]
-    first=turns-G-4
-    res=pl.pallas_call(functools.partial(ag_kernel,plan,n,heads,first),grid=(turns,),out_shape=outs,
+        pltpu.VMEM((8,)+gains.shape,BF),pltpu.VMEM((L,width),BF),pltpu.VMEM((L,width),BF),pltpu.VMEM((L,width),F32),
+        pltpu.VMEM(outs[0].shape,BF),pltpu.VMEM(outs[1].shape,BF),
+        pltpu.VMEM((2,)+outs[2].shape[:-1]+(outs[2].shape[-1]//8,),BF),pltpu.VMEM((2,)+outs[3].shape[2:],BF),S((6,))]
+    res=pl.pallas_call(functools.partial(ag_kernel,plan,n,heads),grid=(turns,),out_shape=outs,
         in_specs=[ANY]*(n+1)+[whole(tokens.shape),whole(seen.shape),whole(live.shape)],
-        out_specs=[ANY]*(n+1)+[whole(s) for s,_ in extra],scratch_shapes=scratch,
+        out_specs=[ANY]*(n+2)+[whole(s) for s,_ in extra[1:]],scratch_shapes=scratch,
         compiler_params=pltpu.CompilerParams(collective_id=cid,has_side_effects=True,vmem_limit_bytes=60<<20),name="gather_and_attend")(*views,gains,tokens,seen,live)
     return [o.reshape(8*s.shape[0],s.shape[1]) for o,s in zip(res[:n],shards)],res[n],res[n+1:]
 
@@ -514,11 +537,13 @@
     full = tuple(lax.all_gather(v, "tok", axis=0, tiled=True) for v in gains + shards)
     target_in = layer_norm(tokens.astype(F32), full[0].astype(F32)).astype(BF)
     target_attn = attn_fwd(product(target_in, full[4]).astype(BF), heads, want_lse=False)[0]
+    target_mid = tokens.astype(F32) + product(target_attn, full[5])
+    target_out = target_ffn(target_mid, full[1].astype(F32), full[6], full[7])
     context_in = layer_norm(seen.astype(F32), full[2].astype(F32)).astype(BF)
     context_mixed = product(context_in, full[8]).astype(BF)
     count = jnp.sum(live, axis=0)
     context_attn, context_lse = attn_fwd(context_mixed, heads, count)
-    return full, (target_attn, context_in, context_mixed, context_attn, context_lse)
+    return full, (target_out, context_in, context_mixed, context_attn, context_lse)
 
 
 def every_grad(tuned, context, predict):
@@ -543,9 +568,12 @@
     grads = [v.astype(BF) for v in grads] + [wide, tall]
     piece = [v.shape[0] // 32 for v in grads]
     plan = [(4, 0, piece[4], "yx", True, 4), (5, 0, piece[5], "xy", True, 4)]
-    for w in (1, 0, 2, 3):
-        half = piece[w] // 2
-        plan += [(w, 0, half, "xy", False, w), (w, half, half, "yx", False, w)]
+    for w in (3, 2, 0, 1):
+        parts = 2 if piece[w] >= 64 else 1
+        rows = piece[w] // (2 * parts)
+        for part in range(parts):
+            at, key = 2 * part * rows, (w, part)
+            plan += [(w, at, rows, "xy", False, key), (w, at + rows, rows, "yx", False, key)]
     sums, vector = reduce_grads(grads, vector, plan, 2)
     sums = [v.astype(F32) for v in sums]
     line = vector.reshape(-1)
@@ -712,26 +740,9 @@
         live_column,
         H,
     )
-    target_attn, context_in, context_mixed, context_attn, context_lse = attended
-    (
-        tgt_prenorm_full,
-        tgt_midnorm_full,
-        ctx_prenorm_full,
-        ctx_midnorm_full,
-        tgt_project_full,
-        tgt_outward_full,
-        tgt_expand_full,
-        tgt_shrink_full,
-        ctx_project_full,
-        ctx_outward_full,
-        ctx_expand_full,
-        ctx_shrink_full,
-    ) = weights
-    tokens_wide = tokens.astype(jnp.float32)
-    target_mid = tokens_wide + product(target_attn, tgt_outward_full)
-    target_out = target_ffn(
-        target_mid, tgt_midnorm_full.astype(jnp.float32), tgt_expand_full, tgt_shrink_full
-    )
+    target_out, context_in, context_mixed, context_attn, context_lse = attended
+    ctx_prenorm_full, ctx_midnorm_full = weights[2:4]
+    ctx_project_full, ctx_outward_full, ctx_expand_full, ctx_shrink_full = weights[8:]
     ctx_prenorm_wide = ctx_prenorm_full.astype(jnp.float32)
     ctx_midnorm_wide = ctx_midnorm_full.astype(jnp.float32)
     context_mid = (seen_rows + product(context_attn, ctx_outward_full)).astype(jnp.bfloat16)

time: 753 us -> 732 us (0.972)
  matrix products: 127 us -> 114 us
    dot_general x10 -> x9, matrix products: 39.8 us -> 26.7 us  [product(): return jnp.dot(former, latter, preferred_element_type=jnp.float32)]
    pallas_call x2 -> x1, Pallas kernels: 267 us -> 264 us  [gather_and_attend(): pl.pallas_call(functools.partial(ag_kernel, plan, n, heads), grid=(turns,...]
where the time goes in v5:
time: 732 us; the launch traced here: 728 us
  Pallas kernels  532 us (73%)
  matrix products  114 us (16%)
  other arithmetic  45.4 us (6%)
  local copies, waits for them, and re-layouts  31.7 us (4%)
    pallas_call x1, Pallas kernels, gather_and_attend(): pl.pallas_call(functools.partial(ag_kernel, plan, n, heads), grid=(turns,...  264 us
    pallas_call x1, Pallas kernels, reduce_grads(): pl.pallas_call(functools.partial(rs_kernel, plan, n), out_shape=outs, in_...  180 us
    pallas_call x2, Pallas kernels, attn_bwd(): pl.pallas_call(functools.partial(bwd_kernel, e, step, masked), grid_spec=...  63.6 us
    dot_general x10, matrix products, inner_rows(): lax.dot_general(former, latter, (((0,), (0,)), ((), ())), preferred_eleme...  43 us
    dot_general x10, matrix products, inner_cols(): lax.dot_general(former, latter, (((1,), (1,)), ((), ())), preferred_eleme...  41 us
    dot_general x9, matrix products, product(): return jnp.dot(former, latter, preferred_element_type=jnp.float32)  26.7 us
    pallas_call x1, Pallas kernels, attn_fwd(): return f(*((count,) if masked else ()), mixed, mixed, mixed)  25 us

profile of v5, /device:TPU:0, one launch (start us, length us, event | category | flops | bytes accessed | tf_op | source)
XLA Modules:
  0.0 727.7 jit_solution(16517865781239144360)
XLA Ops:
  11.6 3.2 fusion.70
  18.7 264.2 %gather_and_attend.1 = (bf16[4,2,2,2,32,3072]{5,4,3,2,1,0:T(8,128)(2,1)}, bf16[4,2,2,2,32,1024]{5,4,3,2,1,0:T(8,128)(2,1)}, bf16[4,2,2,2,32,4096]{5,4,3,2,1,0:T(...) custom-call(bf16[2,2,32,3072]{3,2,1,0:T(8,128)(2,1)} %bitcast.127, ...), custom_call_target="tpu_custom_call" | custom-call | tf_op jit(solution)/shard_map/gather_and_attend/pallas_call | solution.py:371
  284.4 3.8 convert_reduce_fusion
  289.3 4.3 fusion.58
  293.6 4.8 fusion.35
  300.0 4.2 gather_fusion
  304.2 3.4 fusion.67
  308.1 3.3 convolution_convert_fusion.2.refs_0_.refs_1_.refs_2_
  311.4 25.0 %attn_fwd.1 = (bf16[1176,384]{1,0:T(8,128)(2,1)}, f32[3,4,1176]{2,1,0:T(4,128)}) custom-call(bf16[1176,1152]{1,0:T(8,128)(2,1)} %convolution_convert_fusion.2.refs_0_.refs_1_.refs_2_, bf16[1176,1152]{1,0:T(8,128)(2,1)} %convolution_convert_fusion.2.refs_0_.refs_1_.refs_2_, bf16[1176,1152]{1,0:T(8,128)(2,1)} %convolution_convert_fusion.2.refs_0_.refs_1_.refs_2_), custom_call_target="tpu_custom_call" | custom-call | flops 2124251136 | bytes 3612672 | tf_op jit(solution)/shard_map/attn_fwd/pallas_call | solution.py:119
  341.2 2.9 fusion.72
  354.6 4.0 convolution_convert_fusion.4
  358.6 6.5 fusion.13
  374.0 47.2 %attn_bwd.2 = bf16[1176,1152]{1,0:T(8,128)(2,1)} custom-call(bf16[1176,1152]{1,0:T(8,128)(2,1)} %convolution_convert_fusion.2.refs_0_.refs_1_.refs_2_, bf16[1176,1152]{1,0:T(8,128)(2,1)} %convolution_convert_fusion.2.refs_0_.refs_1_.refs_2_, bf16[1176,1152]{1,0:T(8,128)(2,1)} %convolution_convert_fusion.2.refs_0_.refs_1_.refs_2_, ...), custom_call_target="tpu_custom_call" | custom-call | flops 5310627840 | bytes 7225344 | tf_op jit(solution)/shard_map/attn_bwd/pallas_call | solution.py:161
  421.3 4.6 convolution_convert_fusion.6
  436.0 12.1 %fusion.6 = bf16[464,4096]{1,0:T(8,128)(2,1)S(1)} fusion(f32[464,4096]{1,0:T(8,128)} %copy-done.44, bf16[464,1024]{1,0:T(8,128)(2,1)S(1)} %convolution_convert_fusion.10, bf16[4096,1024]{1,0:T(8,128)(2,1)} %bitcast.155), kind=kOutput, calls=%fused_computation.13 | convolution fusion | flops 3930324992 | bytes 20742144 | tf_op jit(solution)/shard_map/dot_general | solution.py:61
  448.1 4.3 fusion.34
  457.1 16.4 %attn_bwd.3 = bf16[464,3072]{1,0:T(8,128)(2,1)} custom-call(s32[1]{0:T(128)} %dynamic_slice.9.refs_0_, bf16[464,3072]{1,0:T(8,128)(2,1)} %get-tuple-element.53.refs_1_.refs_2_.refs_3_, bf16[464,3072]{1,0:T(8,128)(2,1)} %get-tuple-element.53.refs_1_.refs_2_.refs_3_, bf16[464,3072]{1,0:T(8,128)(2,1)} %get-tuple-element.53.refs_1_.refs_2_.refs_3_, ...), custom_call_target="tpu_custom_call" | custom-call | flops 2204631040 | bytes 7602176 | tf_op jit(solution)/shard_map/attn_bwd/pallas_call | solution.py:161
  473.6 6.7 multiply_reduce_fusion
  480.3 11.9 %convolution_convert_fusion = bf16[4096,1024]{1,0:T(8,128)(2,1)} fusion(bf16[464,1024]{1,0:T(8,128)(2,1)S(1)} %convolution_convert_fusion.10, f32[464,4096]{1,0:T(8,128)} %copy-done.44), kind=kOutput, calls=%fused_computation.15 | convolution fusion | flops 3913613312 | bytes 16941056 | tf_op jit(solution)/shard_map/dot_general | solution.py:55
  501.9 5.5 convolution_convert_fusion.3
  507.4 5.0 gather_fusion.2
  512.4 4.7 select_select_fusion
  517.1 7.3 %convolution_convert_fusion.1 = bf16[1024,4096]{1,0:T(8,128)(2,1)} fusion(bf16[464,4096]{1,0:T(8,128)(2,1)S(1)} %copy-done.46, bf16[464,1024]{1,0:T(8,128)(2,1)S(1)} %copy-done.4, f32[1024]{0:T(1024)S(1)} %bitcast.139, f32[464]{0:T(512)S(1)} %fusion.55, f32[464]{0:T(512)S(1)} %broadcast_multiply_fusion.4), kind=kOutput, calls=%fused_computation.16 | convolution fusion | flops 3898884096 | bytes 13147776 | tf_op jit(solution)/shard_map/dot_general | solution.py:55
  524.4 179.6 %reduce_grads.1 = (bf16[2,2,32,3072]{3,2,1,0:T(8,128)(2,1)}, bf16[2,2,32,1024]{3,2,1,0:T(8,128)(2,1)}, bf16[2,2,32,4096]{3,2,1,0:T(8,128)(2,1)}, bf16[2,2,128,10...) custom-call(bf16[4,2,2,2,32,3072]{5,4,3,2,1,0:T(8,128)(2,1)} %bitcas, ...), custom_call_target="tpu_custom_call" | custom-call | tf_op jit(solution)/shard_map/reduce_grads/pallas_call | solution.py:508
  (213 shorter events, 88.6 us)
Async XLA Ops:
  0.7 338.3 %copy-start = (bf16[384,1536]{1,0:T(8,128)(2,1)S(1)}, bf16[384,1536]{1,0:T(8,128)(2,1)}, u32[]{:S(2)}) copy-start(bf16[384,1536]{1,0:T(8,128)(2,1)} %param.44) | copy-start | bytes 3538948
  9.8 294.5 %copy-start.29 = (pred[1176]{0:T(1024)(128)(4,1)}, pred[1176]{0:T(1024)(128)(4,1)S(1)}, u32[]{:S(2)}) copy-start(pred[1176]{0:T(1024)(128)(4,1)S(1)} %compare_and_fusion) | copy-start | bytes 3532
  9.8 290.2 %copy-start.25 = (s32[2048]{0:T(1024)}, s32[2048]{0:T(1024)S(1)}, u32[]{:S(2)}) copy-start(s32[2048]{0:T(1024)S(1)} %pad_clamp_fusion) | copy-start | bytes 24580
  16.3 266.6 %copy-start.33 = (f32[464]{0:T(512)}, f32[464]{0:T(512)S(1)}, u32[]{:S(2)}) copy-start(f32[464]{0:T(512)S(1)} %get-tuple-element.90) | copy-start | bytes 5572
  284.4 4.9 copy-start.37
  288.2 165.2 %copy-start.3 = (bf16[464,1024]{1,0:T(8,128)(2,1)}, bf16[464,1024]{1,0:T(8,128)(2,1)S(1)}, u32[]{:S(2)}) copy-start(bf16[464,1024]{1,0:T(8,128)(2,1)S(1)} %get-tuple-element.109) | copy-start | bytes 2850820
  288.2 5.3 slice-start.4
  288.6 4.9 copy-start.31
  293.6 4.8 copy-start.44
  293.6 5.8 copy-start.21
  311.4 25.0 %copy-start.14 = (bf16[384,384]{1,0:T(8,128)(2,1)S(1)}, bf16[384,384]{1,0:T(8,128)(2,1)}, u32[]{:S(2)}) copy-start(bf16[384,384]{1,0:T(8,128)(2,1)} %param.42) | copy-start | bytes 884740
  339.0 5.5 slice-start.6
  367.0 5.3 copy-start.9
  433.8 14.3 %slice-start.2 = ((s8[8388608]{0:T(1024)(128)(4,1)}), s8[4194304]{0:T(1024)(128)(4,1)S(1)}, s32[]{:S(2)}) async-start(s8[8388608]{0:T(1024)(128)(4,1)} %bitcast.152), calls=%async_computation.2 | async-start | bytes 8388608
  436.0 12.1 %slice-start.3 = ((s8[8388608]{0:T(1024)(128)(4,1)}), s8[4194304]{0:T(1024)(128)(4,1)S(1)}, s32[]{:S(2)}) async-start(s8[8388608]{0:T(1024)(128)(4,1)} %bitcast.152), calls=%async_computation.3 | async-start | bytes 8388608
  457.1 16.4 %copy-start.6 = (f32[464,1024]{1,0:T(8,128)S(1)}, f32[464,1024]{1,0:T(8,128)}, u32[]{:S(2)}) copy-start(f32[464,1024]{1,0:T(8,128)} %copy-done.5) | copy-start | bytes 5701636
  457.1 16.4 %copy-start.28 = (f32[464]{0:T(512)S(1)}, f32[464]{0:T(512)}, u32[]{:S(2)}) copy-start(f32[464]{0:T(512)} %copy-done.27) | copy-start | bytes 5572
  457.1 16.4 %copy-start.35 = (f32[8,1,128]{2,1,0:T(1,128)S(1)}, f32[8,1,128]{2,1,0:T(1,128)}, u32[]{:S(2)}) copy-start(f32[8,1,128]{2,1,0:T(1,128)} %get-tuple-element.94) | copy-start | bytes 12292
  457.1 16.4 %copy-start.36 = (f32[464]{0:T(512)S(1)}, f32[464]{0:T(512)}, u32[]{:S(2)}) copy-start(f32[464]{0:T(512)} %fusion.56) | copy-start | bytes 5572
  480.3 12.6 %copy-start.34 = (f32[464]{0:T(512)S(1)}, f32[464]{0:T(512)}, u32[]{:S(2)}) copy-start(f32[464]{0:T(512)} %copy-done.33) | copy-start | bytes 5572
  501.9 5.5 copy-start.26
  507.4 5.0 copy-start.30
  512.4 4.7 copy-start.46
  704.0 7.6 %copy-start.17 = (bf16[2,2,32,4096]{3,2,1,0:T(8,128)(2,1)S(1)}, bf16[2,2,32,4096]{3,2,1,0:T(8,128)(2,1)}, u32[]{:S(2)}) copy-start(bf16[2,2,32,4096]{3,2,1,0:T(8,128)(2,1)} %get-tuple-element.60) | copy-start | bytes 3145732
  (31 other events, 85.7 us)

commit v6 on v5

--- a/solution.py
+++ b/solution.py
@@ -263,7 +263,7 @@
     turns=[[] for _ in range(len(chunks)+len(chunks[0])-1)]
     for i,chunk in enumerate(chunks):
         for s,stage in enumerate(chunk): turns[i+s].append((s,stage))
-    return [[stage for _,stage in sorted(t,key=lambda p:p[0])] for t in turns]
+    return [[stage for _,stage in sorted(t,key=lambda p:-p[0])] for t in turns]
 
 def scaled_norm(values,gain_blocks,row,out_ref):
     normed=plain_norm(values.astype(F32))
@@ -288,9 +288,10 @@
     done={w:i+len(steps[0])-1 for i,(w,_,_) in enumerate(groups)}
     gs,gf=gains_steps(gain,gout,gsend,grecv)
     width=tok_ref.shape[1]; G=width//128; e=width//heads
-    first=done[0]+1; outward=first+G//2; dense=done[3]+1; end=len(turns)-1
-    blocks=8//(end-dense); block_width=ew.shape[-1]
-    assert done[1]<outward and done[4]<outward and done[2]<dense and outward+G==end+1
+    first=done[0]+1; outward=first+G//2; dense=outward+1; end=len(turns)-1
+    blocks,block_width=2,ew.shape[-1]; finish=dense+8//blocks
+    other=end+1-G//2
+    assert done[1]<outward and max(done[2],done[3])<dense and outward<done[4]+1<=other and finish<end
     take=lambda w,dst,i: pltpu.make_async_copy(fulls[w],dst,wsem.at[i])
     def take_block(j):
         b=(turn-dense)*blocks+j
@@ -302,8 +303,8 @@
         def _(t=t,fs=fs):
             if t==0: greet(everyone_on_tok())
             if t==first: take(0,pw,0).start()
-            if t==outward:
-                take(4,pw,0).start(); take(1,ow,1).start()
+            if t==outward: take(1,ow,1).start()
+            if t==done[4]+1: take(4,pw,0).start()
             for f in fs: f()
             if t==0:
                 gs()
@@ -317,9 +318,14 @@
             if t==4: scaled_norm(seen_ref[...],gv,2,cin)
             if t==first: take(0,pw,0).wait()
             if t==outward:
-                take(4,pw,0).wait(); take(1,ow,1).wait()
+                take(1,ow,1).wait()
                 total[...]=tok_ref[...].astype(F32)+dot(tattn[...],ow[...].reshape(width,width))
                 scaled_norm(total[...],gv,1,tin)
+            if t==done[4]+1: take(4,pw,0).wait()
+            if t==finish:
+                total[...]=plain_norm(total[...])
+                pltpu.make_async_copy(total,tout,wsem.at[1]).start()
+            if t==end: pltpu.make_async_copy(total,tout,wsem.at[1]).wait()
     def block(part,g): return pw[:,:,:,:,:,pl.ds(pl.multiple_of((part*G+g)*128,128),128)].reshape(width,128)
     @pl.when((turn>=first)&(turn<outward))
     def _():
@@ -329,16 +335,19 @@
             q,key,v=[dot(tin[...],block(part,g)).astype(BF) for part in range(3)]
             o,_=attend_group(q,key,v,e,None,1280)
             tattn[:,pl.ds(pl.multiple_of(g*128,128),128)]=o
-    @pl.when(turn>=outward)
+    @pl.when(turn>=other)
     def _():
-        g=turn-outward
-        parts=[dot(cin[...],block(part,g)).astype(BF) for part in range(3)]
-        for part in range(3):
-            cmixed[:,pl.ds(pl.multiple_of((part*G+g)*128,128),128)]=parts[part]
-        o,lse=attend_group(*parts,e,live_ref[...]!=0,1280)
-        cattn[:,pl.ds(pl.multiple_of(g*128,128),128)]=o
-        clse[g]=lse
-    @pl.when((turn>=dense)&(turn<end))
+        live=live_ref[...]!=0
+        @pl.loop(0,2)
+        def _(j):
+            g=(turn-other)*2+j
+            parts=[dot(cin[...],block(part,g)).astype(BF) for part in range(3)]
+            for part in range(3):
+                cmixed[:,pl.ds(pl.multiple_of((part*G+g)*128,128),128)]=parts[part]
+            o,lse=attend_group(*parts,e,live,1280)
+            cattn[:,pl.ds(pl.multiple_of(g*128,128),128)]=o
+            clse[g]=lse
+    @pl.when((turn>=dense)&(turn<finish))
     def _():
         for j in range(blocks):
             for copy in take_block(j): copy.start()
@@ -346,10 +355,6 @@
             for copy in take_block(j): copy.wait()
             active=jax.nn.gelu(dot(tin[...],ew[j].reshape(width,block_width))).astype(BF)
             total[...]+=dot(active,sw[j].reshape(block_width,width))
-    @pl.when(turn==end)
-    def _():
-        total[...]=plain_norm(total[...])
-        put=pltpu.make_async_copy(total,tout,wsem.at[0]); put.start(); put.wait()
 
 def gather_and_attend(shards,gains,tokens,seen,live,heads,plan,cid):
     n=len(shards); k=len(plan)
@@ -516,7 +521,7 @@
 
 def gather_plan(shards):
     plan = []
-    for w in (0, 4, 1, 2, 3, 6, 7, 5):
+    for w in (0, 1, 2, 3, 4, 6, 7, 5):
         rows, wide = shards[w].shape[0] // 4, shards[w].shape[1]
         rest = (wide // 3 + 64) // 128 * 128
         parts = 1 if wide == shards[w].shape[0] * 8 else 2

time: 732 us -> 721 us (0.985)
  Pallas kernels: 532 us -> 521 us
    pallas_call x1, Pallas kernels: 180 us -> 171 us  [reduce_grads(): pl.pallas_call(functools.partial(rs_kernel, plan, n), out_shape=outs, in_...]
where the time goes in v6:
time: 721 us; the launch traced here: 716 us
  Pallas kernels  521 us (72%)
  matrix products  114 us (16%)
  other arithmetic  45.4 us (6%)
  local copies, waits for them, and re-layouts  31.7 us (4%)
    pallas_call x1, Pallas kernels, gather_and_attend(): pl.pallas_call(functools.partial(ag_kernel, plan, n, heads), grid=(turns,...  261 us
    pallas_call x1, Pallas kernels, reduce_grads(): pl.pallas_call(functools.partial(rs_kernel, plan, n), out_shape=outs, in_...  171 us
    pallas_call x2, Pallas kernels, attn_bwd(): pl.pallas_call(functools.partial(bwd_kernel, e, step, masked), grid_spec=...  63.6 us
    dot_general x10, matrix products, inner_rows(): lax.dot_general(former, latter, (((0,), (0,)), ((), ())), preferred_eleme...  43 us
    dot_general x10, matrix products, inner_cols(): lax.dot_general(former, latter, (((1,), (1,)), ((), ())), preferred_eleme...  41 us
    dot_general x9, matrix products, product(): return jnp.dot(former, latter, preferred_element_type=jnp.float32)  26.7 us
    pallas_call x1, Pallas kernels, attn_fwd(): return f(*((count,) if masked else ()), mixed, mixed, mixed)  25 us

profile of v6, /device:TPU:0, one launch (start us, length us, event | category | flops | bytes accessed | tf_op | source)
XLA Modules:
  0.0 716.1 jit_solution(16824803248464330876)
XLA Ops:
  11.6 3.2 fusion.70
  18.7 261.3 %gather_and_attend.1 = (bf16[4,2,2,2,32,3072]{5,4,3,2,1,0:T(8,128)(2,1)}, bf16[4,2,2,2,32,1024]{5,4,3,2,1,0:T(8,128)(2,1)}, bf16[4,2,2,2,32,4096]{5,4,3,2,1,0:T(...) custom-call(bf16[2,2,32,3072]{3,2,1,0:T(8,128)(2,1)} %bitcast.127, ...), custom_call_target="tpu_custom_call" | custom-call | tf_op jit(solution)/shard_map/gather_and_attend/pallas_call | solution.py:376
  281.5 3.8 convert_reduce_fusion
  286.3 4.3 fusion.58
  290.7 4.8 fusion.35
  297.1 4.2 gather_fusion
  301.3 3.4 fusion.67
  305.2 3.3 convolution_convert_fusion.2.refs_0_.refs_1_.refs_2_
  308.5 25.0 %attn_fwd.1 = (bf16[1176,384]{1,0:T(8,128)(2,1)}, f32[3,4,1176]{2,1,0:T(4,128)}) custom-call(bf16[1176,1152]{1,0:T(8,128)(2,1)} %convolution_convert_fusion.2.refs_0_.refs_1_.refs_2_, bf16[1176,1152]{1,0:T(8,128)(2,1)} %convolution_convert_fusion.2.refs_0_.refs_1_.refs_2_, bf16[1176,1152]{1,0:T(8,128)(2,1)} %convolution_convert_fusion.2.refs_0_.refs_1_.refs_2_), custom_call_target="tpu_custom_call" | custom-call | flops 2124251136 | bytes 3612672 | tf_op jit(solution)/shard_map/attn_fwd/pallas_call | solution.py:119
  338.3 2.9 fusion.72
  351.7 4.0 convolution_convert_fusion.4
  355.7 6.5 fusion.13
  371.1 47.2 %attn_bwd.2 = bf16[1176,1152]{1,0:T(8,128)(2,1)} custom-call(bf16[1176,1152]{1,0:T(8,128)(2,1)} %convolution_convert_fusion.2.refs_0_.refs_1_.refs_2_, bf16[1176,1152]{1,0:T(8,128)(2,1)} %convolution_convert_fusion.2.refs_0_.refs_1_.refs_2_, bf16[1176,1152]{1,0:T(8,128)(2,1)} %convolution_convert_fusion.2.refs_0_.refs_1_.refs_2_, ...), custom_call_target="tpu_custom_call" | custom-call | flops 5310627840 | bytes 7225344 | tf_op jit(solution)/shard_map/attn_bwd/pallas_call | solution.py:161
  418.4 4.6 convolution_convert_fusion.6
  433.1 12.1 %fusion.6 = bf16[464,4096]{1,0:T(8,128)(2,1)S(1)} fusion(f32[464,4096]{1,0:T(8,128)} %copy-done.44, bf16[464,1024]{1,0:T(8,128)(2,1)S(1)} %convolution_convert_fusion.10, bf16[4096,1024]{1,0:T(8,128)(2,1)} %bitcast.155), kind=kOutput, calls=%fused_computation.13 | convolution fusion | flops 3930324992 | bytes 20742144 | tf_op jit(solution)/shard_map/dot_general | solution.py:61
  445.2 4.3 fusion.34
  454.2 16.4 %attn_bwd.3 = bf16[464,3072]{1,0:T(8,128)(2,1)} custom-call(s32[1]{0:T(128)} %dynamic_slice.9.refs_0_, bf16[464,3072]{1,0:T(8,128)(2,1)} %get-tuple-element.53.refs_1_.refs_2_.refs_3_, bf16[464,3072]{1,0:T(8,128)(2,1)} %get-tuple-element.53.refs_1_.refs_2_.refs_3_, bf16[464,3072]{1,0:T(8,128)(2,1)} %get-tuple-element.53.refs_1_.refs_2_.refs_3_, ...), custom_call_target="tpu_custom_call" | custom-call | flops 2204631040 | bytes 7602176 | tf_op jit(solution)/shard_map/attn_bwd/pallas_call | solution.py:161
  470.7 6.7 multiply_reduce_fusion
  477.4 11.9 %convolution_convert_fusion = bf16[4096,1024]{1,0:T(8,128)(2,1)} fusion(bf16[464,1024]{1,0:T(8,128)(2,1)S(1)} %convolution_convert_fusion.10, f32[464,4096]{1,0:T(8,128)} %copy-done.44), kind=kOutput, calls=%fused_computation.15 | convolution fusion | flops 3913613312 | bytes 16941056 | tf_op jit(solution)/shard_map/dot_general | solution.py:55
  499.0 5.5 convolution_convert_fusion.3
  504.5 5.0 gather_fusion.2
  509.5 4.7 select_select_fusion
  514.2 7.3 %convolution_convert_fusion.1 = bf16[1024,4096]{1,0:T(8,128)(2,1)} fusion(bf16[464,4096]{1,0:T(8,128)(2,1)S(1)} %copy-done.46, bf16[464,1024]{1,0:T(8,128)(2,1)S(1)} %copy-done.4, f32[1024]{0:T(1024)S(1)} %bitcast.139, f32[464]{0:T(512)S(1)} %fusion.55, f32[464]{0:T(512)S(1)} %broadcast_multiply_fusion.4), kind=kOutput, calls=%fused_computation.16 | convolution fusion | flops 3898884096 | bytes 13147776 | tf_op jit(solution)/shard_map/dot_general | solution.py:55
  521.5 170.9 %reduce_grads.1 = (bf16[2,2,32,3072]{3,2,1,0:T(8,128)(2,1)}, bf16[2,2,32,1024]{3,2,1,0:T(8,128)(2,1)}, bf16[2,2,32,4096]{3,2,1,0:T(8,128)(2,1)}, bf16[2,2,128,10...) custom-call(bf16[4,2,2,2,32,3072]{5,4,3,2,1,0:T(8,128)(2,1)} %bitcas, ...), custom_call_target="tpu_custom_call" | custom-call | tf_op jit(solution)/shard_map/reduce_grads/pallas_call | solution.py:513
  (213 shorter events, 88.6 us)
Async XLA Ops:
  0.7 335.4 %copy-start = (bf16[384,1536]{1,0:T(8,128)(2,1)S(1)}, bf16[384,1536]{1,0:T(8,128)(2,1)}, u32[]{:S(2)}) copy-start(bf16[384,1536]{1,0:T(8,128)(2,1)} %param.44) | copy-start | bytes 3538948
  9.8 291.5 %copy-start.29 = (pred[1176]{0:T(1024)(128)(4,1)}, pred[1176]{0:T(1024)(128)(4,1)S(1)}, u32[]{:S(2)}) copy-start(pred[1176]{0:T(1024)(128)(4,1)S(1)} %compare_and_fusion) | copy-start | bytes 3532
  9.8 287.3 %copy-start.25 = (s32[2048]{0:T(1024)}, s32[2048]{0:T(1024)S(1)}, u32[]{:S(2)}) copy-start(s32[2048]{0:T(1024)S(1)} %pad_clamp_fusion) | copy-start | bytes 24580
  16.3 263.7 %copy-start.33 = (f32[464]{0:T(512)}, f32[464]{0:T(512)S(1)}, u32[]{:S(2)}) copy-start(f32[464]{0:T(512)S(1)} %get-tuple-element.90) | copy-start | bytes 5572
  281.4 4.9 copy-start.37
  285.3 165.2 %copy-start.3 = (bf16[464,1024]{1,0:T(8,128)(2,1)}, bf16[464,1024]{1,0:T(8,128)(2,1)S(1)}, u32[]{:S(2)}) copy-start(bf16[464,1024]{1,0:T(8,128)(2,1)S(1)} %get-tuple-element.109) | copy-start | bytes 2850820
  285.3 5.3 slice-start.4
  285.7 4.9 copy-start.31
  290.6 4.8 copy-start.44
  290.7 5.8 copy-start.21
  308.5 25.0 %copy-start.14 = (bf16[384,384]{1,0:T(8,128)(2,1)S(1)}, bf16[384,384]{1,0:T(8,128)(2,1)}, u32[]{:S(2)}) copy-start(bf16[384,384]{1,0:T(8,128)(2,1)} %param.42) | copy-start | bytes 884740
  336.1 5.5 slice-start.6
  364.1 5.3 copy-start.9
  430.9 14.3 %slice-start.2 = ((s8[8388608]{0:T(1024)(128)(4,1)}), s8[4194304]{0:T(1024)(128)(4,1)S(1)}, s32[]{:S(2)}) async-start(s8[8388608]{0:T(1024)(128)(4,1)} %bitcast.152), calls=%async_computation.2 | async-start | bytes 8388608
  433.1 12.1 %slice-start.3 = ((s8[8388608]{0:T(1024)(128)(4,1)}), s8[4194304]{0:T(1024)(128)(4,1)S(1)}, s32[]{:S(2)}) async-start(s8[8388608]{0:T(1024)(128)(4,1)} %bitcast.152), calls=%async_computation.3 | async-start | bytes 8388608
  454.2 16.4 %copy-start.6 = (f32[464,1024]{1,0:T(8,128)S(1)}, f32[464,1024]{1,0:T(8,128)}, u32[]{:S(2)}) copy-start(f32[464,1024]{1,0:T(8,128)} %copy-done.5) | copy-start | bytes 5701636
  454.2 16.4 %copy-start.28 = (f32[464]{0:T(512)S(1)}, f32[464]{0:T(512)}, u32[]{:S(2)}) copy-start(f32[464]{0:T(512)} %copy-done.27) | copy-start | bytes 5572
  454.2 16.4 %copy-start.35 = (f32[8,1,128]{2,1,0:T(1,128)S(1)}, f32[8,1,128]{2,1,0:T(1,128)}, u32[]{:S(2)}) copy-start(f32[8,1,128]{2,1,0:T(1,128)} %get-tuple-element.94) | copy-start | bytes 12292
  454.2 16.4 %copy-start.36 = (f32[464]{0:T(512)S(1)}, f32[464]{0:T(512)}, u32[]{:S(2)}) copy-start(f32[464]{0:T(512)} %fusion.56) | copy-start | bytes 5572
  477.4 12.6 %copy-start.34 = (f32[464]{0:T(512)S(1)}, f32[464]{0:T(512)}, u32[]{:S(2)}) copy-start(f32[464]{0:T(512)} %copy-done.33) | copy-start | bytes 5572
  499.0 5.5 copy-start.26
  504.5 5.0 copy-start.30
  509.5 4.7 copy-start.46
  692.4 7.6 %copy-start.17 = (bf16[2,2,32,4096]{3,2,1,0:T(8,128)(2,1)S(1)}, bf16[2,2,32,4096]{3,2,1,0:T(8,128)(2,1)}, u32[]{:S(2)}) copy-start(bf16[2,2,32,4096]{3,2,1,0:T(8,128)(2,1)} %get-tuple-element.60) | copy-start | bytes 3145732
  (31 other events, 85.7 us)

commit v7 on v6

--- a/solution.py
+++ b/solution.py
@@ -298,6 +298,10 @@
         cols=pl.ds(pl.multiple_of(b*block_width,128),block_width)
         return (pltpu.make_async_copy(fulls[2].at[:,:,:,:,:,cols],ew.at[j],wsem.at[2+2*j]),
                 pltpu.make_async_copy(fulls[3].at[b//2,b%2],sw.at[j],wsem.at[3+2*j]))
+    @pl.when((turn>=dense)&(turn<finish))
+    def _():
+        for j in range(blocks):
+            for copy in take_block(j): copy.start()
     for t,fs in enumerate(turns):
         @pl.when(turn==t)
         def _(t=t,fs=fs):
@@ -326,31 +330,29 @@
                 total[...]=plain_norm(total[...])
                 pltpu.make_async_copy(total,tout,wsem.at[1]).start()
             if t==end: pltpu.make_async_copy(total,tout,wsem.at[1]).wait()
-    def block(part,g): return pw[:,:,:,:,:,pl.ds(pl.multiple_of((part*G+g)*128,128),128)].reshape(width,128)
+    def pair(rows,g):
+        columns=lambda part: pl.ds(pl.multiple_of((part*G+g)*128,128),256)
+        return [dot(rows,pw[:,:,:,:,:,columns(part)].reshape(width,256)).astype(BF) for part in range(3)]
     @pl.when((turn>=first)&(turn<outward))
     def _():
-        @pl.loop(0,2)
-        def _(j):
-            g=(turn-first)*2+j
-            q,key,v=[dot(tin[...],block(part,g)).astype(BF) for part in range(3)]
-            o,_=attend_group(q,key,v,e,None,1280)
-            tattn[:,pl.ds(pl.multiple_of(g*128,128),128)]=o
+        g=(turn-first)*2
+        parts=pair(tin[...],g)
+        for j in range(2):
+            o,_=attend_group(*[p[:,j*128:(j+1)*128] for p in parts],e,None,1280)
+            tattn[:,pl.ds(pl.multiple_of((g+j)*128,128),128)]=o
     @pl.when(turn>=other)
     def _():
+        g=(turn-other)*2
         live=live_ref[...]!=0
-        @pl.loop(0,2)
-        def _(j):
-            g=(turn-other)*2+j
-            parts=[dot(cin[...],block(part,g)).astype(BF) for part in range(3)]
-            for part in range(3):
-                cmixed[:,pl.ds(pl.multiple_of((part*G+g)*128,128),128)]=parts[part]
-            o,lse=attend_group(*parts,e,live,1280)
-            cattn[:,pl.ds(pl.multiple_of(g*128,128),128)]=o
-            clse[g]=lse
+        parts=pair(cin[...],g)
+        for part in range(3):
+            cmixed[:,pl.ds(pl.multiple_of((part*G+g)*128,128),256)]=parts[part]
+        for j in range(2):
+            o,lse=attend_group(*[p[:,j*128:(j+1)*128] for p in parts],e,live,1280)
+            cattn[:,pl.ds(pl.multiple_of((g+j)*128,128),128)]=o
+            clse[g+j]=lse
     @pl.when((turn>=dense)&(turn<finish))
     def _():
-        for j in range(blocks):
-            for copy in take_block(j): copy.start()
         for j in range(blocks):
             for copy in take_block(j): copy.wait()
             active=jax.nn.gelu(dot(tin[...],ew[j].reshape(width,block_width))).astype(BF)

time: 721 us -> 709 us (0.983)
  Pallas kernels: 521 us -> 508 us
    pallas_call x1, Pallas kernels: 261 us -> 248 us  [gather_and_attend(): pl.pallas_call(functools.partial(ag_kernel, plan, n, heads), grid=(turns,...]
where the time goes in v7:
time: 709 us; the launch traced here: 703 us
  Pallas kernels  508 us (72%)
  matrix products  114 us (16%)
  other arithmetic  45.2 us (6%)
  local copies, waits for them, and re-layouts  31.7 us (4%)
    pallas_call x1, Pallas kernels, gather_and_attend(): pl.pallas_call(functools.partial(ag_kernel, plan, n, heads), grid=(turns,...  248 us
    pallas_call x1, Pallas kernels, reduce_grads(): pl.pallas_call(functools.partial(rs_kernel, plan, n), out_shape=outs, in_...  172 us
    pallas_call x2, Pallas kernels, attn_bwd(): pl.pallas_call(functools.partial(bwd_kernel, e, step, masked), grid_spec=...  63.8 us
    dot_general x10, matrix products, inner_rows(): lax.dot_general(former, latter, (((0,), (0,)), ((), ())), preferred_eleme...  43.1 us
    dot_general x10, matrix products, inner_cols(): lax.dot_general(former, latter, (((1,), (1,)), ((), ())), preferred_eleme...  40.8 us
    dot_general x9, matrix products, product(): return jnp.dot(former, latter, preferred_element_type=jnp.float32)  26.7 us
    pallas_call x1, Pallas kernels, attn_fwd(): return f(*((count,) if masked else ()), mixed, mixed, mixed)  25.2 us

profile of v7, /device:TPU:0, one launch (start us, length us, event | category | flops | bytes accessed | tf_op | source)
XLA Modules:
  0.0 703.2 jit_solution(6497052367187919432)
XLA Ops:
  11.6 3.2 fusion.70
  18.7 247.6 %gather_and_attend.1 = (bf16[4,2,2,2,32,3072]{5,4,3,2,1,0:T(8,128)(2,1)}, bf16[4,2,2,2,32,1024]{5,4,3,2,1,0:T(8,128)(2,1)}, bf16[4,2,2,2,32,4096]{5,4,3,2,1,0:T(...) custom-call(bf16[2,2,32,3072]{3,2,1,0:T(8,128)(2,1)} %bitcast.127, ...), custom_call_target="tpu_custom_call" | custom-call | tf_op jit(solution)/shard_map/gather_and_attend/pallas_call | solution.py:378
  267.8 3.8 convert_reduce_fusion
  272.7 4.3 fusion.58
  277.0 4.8 fusion.35
  283.4 4.2 gather_fusion
  287.6 3.4 fusion.67
  291.5 3.3 convolution_convert_fusion.2.refs_0_.refs_1_.refs_2_
  294.8 25.2 %attn_fwd.1 = (bf16[1176,384]{1,0:T(8,128)(2,1)}, f32[3,4,1176]{2,1,0:T(4,128)}) custom-call(bf16[1176,1152]{1,0:T(8,128)(2,1)} %convolution_convert_fusion.2.refs_0_.refs_1_.refs_2_, bf16[1176,1152]{1,0:T(8,128)(2,1)} %convolution_convert_fusion.2.refs_0_.refs_1_.refs_2_, bf16[1176,1152]{1,0:T(8,128)(2,1)} %convolution_convert_fusion.2.refs_0_.refs_1_.refs_2_), custom_call_target="tpu_custom_call" | custom-call | flops 2124251136 | bytes 3612672 | tf_op jit(solution)/shard_map/attn_fwd/pallas_call | solution.py:119
  324.8 2.9 fusion.72
  337.9 4.0 convolution_convert_fusion.4
  341.9 6.5 fusion.13
  357.4 47.4 %attn_bwd.2 = bf16[1176,1152]{1,0:T(8,128)(2,1)} custom-call(bf16[1176,1152]{1,0:T(8,128)(2,1)} %convolution_convert_fusion.2.refs_0_.refs_1_.refs_2_, bf16[1176,1152]{1,0:T(8,128)(2,1)} %convolution_convert_fusion.2.refs_0_.refs_1_.refs_2_, bf16[1176,1152]{1,0:T(8,128)(2,1)} %convolution_convert_fusion.2.refs_0_.refs_1_.refs_2_, ...), custom_call_target="tpu_custom_call" | custom-call | flops 5310627840 | bytes 7225344 | tf_op jit(solution)/shard_map/attn_bwd/pallas_call | solution.py:161
  404.8 4.6 convolution_convert_fusion.6
  419.6 11.8 %fusion.6 = bf16[464,4096]{1,0:T(8,128)(2,1)S(1)} fusion(f32[464,4096]{1,0:T(8,128)} %copy-done.44, bf16[464,1024]{1,0:T(8,128)(2,1)S(1)} %convolution_convert_fusion.10, bf16[4096,1024]{1,0:T(8,128)(2,1)} %bitcast.155), kind=kOutput, calls=%fused_computation.13 | convolution fusion | flops 3930324992 | bytes 20742144 | tf_op jit(solution)/shard_map/dot_general | solution.py:61
  431.4 4.3 fusion.34
  440.5 16.4 %attn_bwd.3 = bf16[464,3072]{1,0:T(8,128)(2,1)} custom-call(s32[1]{0:T(128)} %dynamic_slice.9.refs_0_, bf16[464,3072]{1,0:T(8,128)(2,1)} %get-tuple-element.53.refs_1_.refs_2_.refs_3_, bf16[464,3072]{1,0:T(8,128)(2,1)} %get-tuple-element.53.refs_1_.refs_2_.refs_3_, bf16[464,3072]{1,0:T(8,128)(2,1)} %get-tuple-element.53.refs_1_.refs_2_.refs_3_, ...), custom_call_target="tpu_custom_call" | custom-call | flops 2204631040 | bytes 7602176 | tf_op jit(solution)/shard_map/attn_bwd/pallas_call | solution.py:161
  456.9 6.8 multiply_reduce_fusion
  463.7 11.9 %convolution_convert_fusion = bf16[4096,1024]{1,0:T(8,128)(2,1)} fusion(bf16[464,1024]{1,0:T(8,128)(2,1)S(1)} %convolution_convert_fusion.10, f32[464,4096]{1,0:T(8,128)} %copy-done.44), kind=kOutput, calls=%fused_computation.15 | convolution fusion | flops 3913613312 | bytes 16941056 | tf_op jit(solution)/shard_map/dot_general | solution.py:55
  485.3 5.5 convolution_convert_fusion.3
  490.8 5.0 gather_fusion.2
  495.8 4.7 select_select_fusion
  500.5 7.3 %convolution_convert_fusion.1 = bf16[1024,4096]{1,0:T(8,128)(2,1)} fusion(bf16[464,4096]{1,0:T(8,128)(2,1)S(1)} %copy-done.46, bf16[464,1024]{1,0:T(8,128)(2,1)S(1)} %copy-done.4, f32[1024]{0:T(1024)S(1)} %bitcast.139, f32[464]{0:T(512)S(1)} %fusion.55, f32[464]{0:T(512)S(1)} %broadcast_multiply_fusion.4), kind=kOutput, calls=%fused_computation.16 | convolution fusion | flops 3898884096 | bytes 13147776 | tf_op jit(solution)/shard_map/dot_general | solution.py:55
  507.8 171.7 %reduce_grads.1 = (bf16[2,2,32,3072]{3,2,1,0:T(8,128)(2,1)}, bf16[2,2,32,1024]{3,2,1,0:T(8,128)(2,1)}, bf16[2,2,32,4096]{3,2,1,0:T(8,128)(2,1)}, bf16[2,2,128,10...) custom-call(bf16[4,2,2,2,32,3072]{5,4,3,2,1,0:T(8,128)(2,1)} %bitcas, ...), custom_call_target="tpu_custom_call" | custom-call | tf_op jit(solution)/shard_map/reduce_grads/pallas_call | solution.py:515
  (213 shorter events, 88.3 us)
Async XLA Ops:
  0.7 322.0 %copy-start = (bf16[384,1536]{1,0:T(8,128)(2,1)S(1)}, bf16[384,1536]{1,0:T(8,128)(2,1)}, u32[]{:S(2)}) copy-start(bf16[384,1536]{1,0:T(8,128)(2,1)} %param.44) | copy-start | bytes 3538948
  9.8 277.8 %copy-start.29 = (pred[1176]{0:T(1024)(128)(4,1)}, pred[1176]{0:T(1024)(128)(4,1)S(1)}, u32[]{:S(2)}) copy-start(pred[1176]{0:T(1024)(128)(4,1)S(1)} %compare_and_fusion) | copy-start | bytes 3532
  9.8 273.6 %copy-start.25 = (s32[2048]{0:T(1024)}, s32[2048]{0:T(1024)S(1)}, u32[]{:S(2)}) copy-start(s32[2048]{0:T(1024)S(1)} %pad_clamp_fusion) | copy-start | bytes 24580
  16.3 250.0 %copy-start.33 = (f32[464]{0:T(512)}, f32[464]{0:T(512)S(1)}, u32[]{:S(2)}) copy-start(f32[464]{0:T(512)S(1)} %get-tuple-element.90) | copy-start | bytes 5572
  267.8 4.9 copy-start.37
  271.6 165.1 %copy-start.3 = (bf16[464,1024]{1,0:T(8,128)(2,1)}, bf16[464,1024]{1,0:T(8,128)(2,1)S(1)}, u32[]{:S(2)}) copy-start(bf16[464,1024]{1,0:T(8,128)(2,1)S(1)} %get-tuple-element.109) | copy-start | bytes 2850820
  271.6 5.3 slice-start.4
  272.0 4.9 copy-start.31
  277.0 4.8 copy-start.44
  277.0 5.8 copy-start.21
  294.8 25.2 %copy-start.14 = (bf16[384,384]{1,0:T(8,128)(2,1)S(1)}, bf16[384,384]{1,0:T(8,128)(2,1)}, u32[]{:S(2)}) copy-start(bf16[384,384]{1,0:T(8,128)(2,1)} %param.42) | copy-start | bytes 884740
  322.6 5.5 slice-start.6
  350.3 5.3 copy-start.9
  417.3 14.0 %slice-start.2 = ((s8[8388608]{0:T(1024)(128)(4,1)}), s8[4194304]{0:T(1024)(128)(4,1)S(1)}, s32[]{:S(2)}) async-start(s8[8388608]{0:T(1024)(128)(4,1)} %bitcast.152), calls=%async_computation.2 | async-start | bytes 8388608
  419.6 11.8 %slice-start.3 = ((s8[8388608]{0:T(1024)(128)(4,1)}), s8[4194304]{0:T(1024)(128)(4,1)S(1)}, s32[]{:S(2)}) async-start(s8[8388608]{0:T(1024)(128)(4,1)} %bitcast.152), calls=%async_computation.3 | async-start | bytes 8388608
  440.5 16.4 %copy-start.6 = (f32[464,1024]{1,0:T(8,128)S(1)}, f32[464,1024]{1,0:T(8,128)}, u32[]{:S(2)}) copy-start(f32[464,1024]{1,0:T(8,128)} %copy-done.5) | copy-start | bytes 5701636
  440.5 16.4 %copy-start.28 = (f32[464]{0:T(512)S(1)}, f32[464]{0:T(512)}, u32[]{:S(2)}) copy-start(f32[464]{0:T(512)} %copy-done.27) | copy-start | bytes 5572
  440.5 16.4 %copy-start.35 = (f32[8,1,128]{2,1,0:T(1,128)S(1)}, f32[8,1,128]{2,1,0:T(1,128)}, u32[]{:S(2)}) copy-start(f32[8,1,128]{2,1,0:T(1,128)} %get-tuple-element.94) | copy-start | bytes 12292
  440.5 16.4 %copy-start.36 = (f32[464]{0:T(512)S(1)}, f32[464]{0:T(512)}, u32[]{:S(2)}) copy-start(f32[464]{0:T(512)} %fusion.56) | copy-start | bytes 5572
  463.7 12.6 %copy-start.34 = (f32[464]{0:T(512)S(1)}, f32[464]{0:T(512)}, u32[]{:S(2)}) copy-start(f32[464]{0:T(512)} %copy-done.33) | copy-start | bytes 5572
  485.3 5.5 copy-start.26
  490.8 5.0 copy-start.30
  495.8 4.7 copy-start.46
  679.5 7.6 %copy-start.17 = (bf16[2,2,32,4096]{3,2,1,0:T(8,128)(2,1)S(1)}, bf16[2,2,32,4096]{3,2,1,0:T(8,128)(2,1)}, u32[]{:S(2)}) copy-start(bf16[2,2,32,4096]{3,2,1,0:T(8,128)(2,1)} %get-tuple-element.60) | copy-start | bytes 3145732
  (31 other events, 85.7 us)
